TPU v7x, 32 devices: a whole 2x2x4 slice. The times are simulated.
32 devices in a mesh: dp: 2 (over x), sp2: 4 (over z), sp: 4 (over y, core).
Axes of the slice: x: 2, y: 2, z: 4, core: 2. Of those that a mesh axis runs over, the one named last changes fastest.
Arguments:
- x: bfloat16 [32, 64, 512, 64], P('dp', 'sp', 'sp2'), parts along dimension 0
- w_a: bfloat16 [4, 3, 3, 64, 64], replicated
- bn_a: float32 [4, 2, 64], replicated
- w_down: bfloat16 [3, 3, 64, 128], replicated
- bn_down: float32 [2, 128], replicated
- w_b: bfloat16 [1, 3, 3, 128, 128], replicated
- bn_b: float32 [1, 2, 128], replicated
Outputs:
- output: bfloat16 [32, 32, 256, 128], P('dp', 'sp', 'sp2'), parts along dimension 0
There are 2 independent parts. A program takes and returns all parts, laid end to end along the dimension named above; an argument that names none is the same for every part.
All inputs are finite; a program needn't handle non-finite values.
Results may differ from a plain program's by a relative error of at most 0.00533103.
Values are sent between devices in bfloat16 or wider.
A program may use at most 1 GiB of HBM per device.

v0:
```python
import jax
import jax.numpy as jnp
from jax import lax
from jax.sharding import PartitionSpec as P

CONV_DIMS = ("NHWC", "HWIO", "NHWC")


def edge_extend(act_tile, axis_name, axis_len, line_dim, two_sided):
    tile_len = act_tile.shape[line_dim]
    first_line = lax.slice_in_dim(act_tile, 0, 1, axis=line_dim)
    from_next = lax.ppermute(first_line, axis_name, perm=[(device + 1, device) for device in range(axis_len - 1)])
    if two_sided:
        last_line = lax.slice_in_dim(act_tile, tile_len - 1, tile_len, axis=line_dim)
        from_prev = lax.ppermute(last_line, axis_name, perm=[(device, device + 1) for device in range(axis_len - 1)])
        return jnp.concatenate([from_prev, act_tile, from_next], axis=line_dim)
    return jnp.concatenate([act_tile, from_next], axis=line_dim)


def conv_bn(act_tile, weight, norm_pair, stride, grid_shape):
    rows_n, cols_n = grid_shape
    two_sided = stride == 1
    extended = edge_extend(act_tile, "sp", rows_n, 1, two_sided)
    extended = edge_extend(extended, "sp2", cols_n, 2, two_sided)
    pre_norm = lax.conv_general_dilated(extended, weight, (stride, stride), "VALID", dimension_numbers=CONV_DIMS, preferred_element_type=jnp.float32)
    moments = jnp.stack([jnp.sum(pre_norm, axis=(0, 1, 2)), jnp.sum(pre_norm * pre_norm, axis=(0, 1, 2))])
    moments = lax.psum(moments, ("sp2", "sp"))
    num_pos = pre_norm.shape[0] * pre_norm.shape[1] * pre_norm.shape[2] * rows_n * cols_n
    mean_val = moments[0] / num_pos
    var_val = moments[1] / num_pos - mean_val * mean_val
    normed = norm_pair[0] * (pre_norm - mean_val) * lax.rsqrt(var_val + 1e-5) + norm_pair[1]
    return jnp.maximum(normed, 0.0).astype(jnp.bfloat16)


def solution(mesh):
    grid_shape = (mesh.shape["sp"], mesh.shape["sp2"])

    def per_device(x, w_a, bn_a, w_down, bn_down, w_b, bn_b):
        act_tile = x
        for layer_idx in range(w_a.shape[0]):
            act_tile = conv_bn(act_tile, w_a[layer_idx], bn_a[layer_idx], 1, grid_shape)
        act_tile = conv_bn(act_tile, w_down, bn_down, 2, grid_shape)
        for layer_idx in range(w_b.shape[0]):
            act_tile = conv_bn(act_tile, w_b[layer_idx], bn_b[layer_idx], 1, grid_shape)
        return act_tile

    tile_spec = P("dp", "sp", "sp2", None)
    return jax.shard_map(per_device, mesh=mesh, in_specs=(tile_spec, P(), P(), P(), P(), P(), P()), out_specs=tile_spec, check_vma=False)
```

profile of v0, /device:TPU:0, one launch (start us, length us, event | category | flops | bytes accessed | tf_op | source)
XLA Modules:
  0.0 409.1 jit_solution(7686896079203663723)
XLA Ops:
  0.0 10.1 %copy.8 = bf16[16,16,128,64]{3,0,2,1:T(8,128)(2,1)} copy(bf16[16,16,128,64]{2,3,1,0:T(8,128)(2,1)} %param.7) | data formatting | bytes 8388608 | tf_op args[0]
  10.1 1.5 fusion.92
  11.6 2.7 collective-permute-start
  14.4 1.3 collective-permute-start.1
  15.9 4.4 %collective-permute-done.1 = bf16[16,1,128,64]{3,0,2,1:T(8,128)(2,1)S(1)} collective-permute-done((bf16[16,1,128,64]{3,0,2,1:T(8,128)(2,1)S(1)}, bf16[16,1,128,64]{3,0,2,1:T(8,128)(2,1)S(1)}, u32[]{:S(2)}, u32[]{:S(2)}) %collective-permute-start.1) | collective-permute-done | bytes 262176 | tf_op jit(solution)/shard_map/ppermute | solution.py:12
  21.2 3.5 collective-permute-start.2
  24.7 1.3 collective-permute-start.3
  26.6 4.3 %collective-permute-done.3 = bf16[16,18,1,64]{3,0,2,1:T(8,128)(2,1)S(1)} collective-permute-done((bf16[16,18,1,64]{3,0,2,1:T(8,128)(2,1)S(1)}, bf16[16,18,1,64]{3,0,2,1:T(8,128)(2,1)S(1)}, u32[]{:S(2)}, u32[]{:S(2)}) %collective-permute-start.3) | collective-permute-done | bytes 36896 | tf_op jit(solution)/shard_map/ppermute | solution.py:12
  30.9 16.5 %fusion.86 = (f32[64]{0:T(128)S(1)}, f32[64]{0:T(128)S(1)}, f32[16,16,128,64]{3,0,2,1:T(8,128)}) fusion(bf16[4,3,3,64,64]{4,3,2,1,0:T(8,128)(2,1)S(1)} %copy-done.9, bf16[16,18,1,64]{3,0,2,1:T(8,128)(2,1)S(1)} %collective-permute-done.3, bf16[16,1,128,64]{3,0,2,1:T(8,128)(2,1)S(1)} %collective-permute-done.1, bf16[16,16,128,64]{3,0,2,1:T(8,128)(2,1)S(1)} %copy-done.1, ...), kind=kOutput, calls=%fused_computation.144 | convolution fusion | flops 2431795200 | bytes 18121216 | tf_op jit(solution)/shard_map/conv_general_dilated | solution.py:25
  47.5 35.3 %psum.42 = f32[2,64]{1,0:T(2,128)S(1)} all-reduce(f32[2,64]{1,0:T(2,128)S(1)} %pad_maximum_fusion.16), channel_id=1, replica_groups=mesh['dp'=2,'sp2'=4,'sp'=4] {'sp2','sp'}, use_global_device_ids=true, to_apply=%region_2.0 | all-reduce | flops 128 | bytes 1024 | tf_op jit(solution)/shard_map/psum | solution.py:27
  82.8 7.7 %maximum_convert_fusion.3 = bf16[16,16,128,64]{3,0,2,1:T(8,128)(2,1)S(1)} fusion(f32[16,16,128,64]{3,0,2,1:T(8,128)} %get-tuple-element.49, f32[64]{0:T(128)S(1)} %get-tuple-element.39, f32[64]{0:T(128)S(1)} %fusion.76, f32[64]{0:T(128)S(1)} %multiply_bitcast_fusion.5, f32[64]{0:T(128)S(1)} %get-tuple-element.40), kind=kLoop, calls=%fused_computation.6 | loop fusion | flops 12582912 | bytes 12583936 | tf_op jit(solution)/shard_map/convert_element_type | solution.py:32
  90.7 1.3 collective-permute-start.4
  92.0 1.3 collective-permute-start.5
  93.5 2.3 collective-permute-done.5
  95.8 1.3 collective-permute-start.6
  97.1 1.3 collective-permute-start.7
  99.1 4.3 %collective-permute-done.7 = bf16[16,18,1,64]{3,0,2,1:T(8,128)(2,1)S(1)} collective-permute-done((bf16[16,18,1,64]{3,0,2,1:T(8,128)(2,1)S(1)}, bf16[16,18,1,64]{3,0,2,1:T(8,128)(2,1)S(1)}, u32[]{:S(2)}, u32[]{:S(2)}) %collective-permute-start.7) | collective-permute-done | bytes 36896 | tf_op jit(solution)/shard_map/ppermute | solution.py:12
  103.4 16.5 %fusion.85 = (f32[64]{0:T(128)S(1)}, f32[64]{0:T(128)S(1)}, f32[16,16,128,64]{3,0,2,1:T(8,128)}) fusion(bf16[4,3,3,64,64]{4,3,2,1,0:T(8,128)(2,1)S(1)} %copy-done.9, bf16[16,18,1,64]{3,0,2,1:T(8,128)(2,1)S(1)} %collective-permute-done.7, bf16[16,1,128,64]{3,0,2,1:T(8,128)(2,1)S(1)} %collective-permute-done.5, ...), kind=kOutput, calls=%fused_computation.143 | convolution fusion | flops 2431795200 | bytes 18121216 | tf_op jit(solution)/shard_map/conv_general_dilated | solution.py:25
  119.9 33.5 %psum.43 = f32[2,64]{1,0:T(2,128)S(1)} all-reduce(f32[2,64]{1,0:T(2,128)S(1)} %pad_maximum_fusion.17), channel_id=1, replica_groups=mesh['dp'=2,'sp2'=4,'sp'=4] {'sp2','sp'}, use_global_device_ids=true, to_apply=%region_5.0 | all-reduce | flops 128 | bytes 1024 | tf_op jit(solution)/shard_map/psum | solution.py:27
  153.4 7.7 %maximum_convert_fusion.2 = bf16[16,16,128,64]{3,0,2,1:T(8,128)(2,1)S(1)} fusion(f32[16,16,128,64]{3,0,2,1:T(8,128)} %get-tuple-element.50, f32[64]{0:T(128)S(1)} %get-tuple-element.38, f32[64]{0:T(128)S(1)} %fusion.74, f32[64]{0:T(128)S(1)} %multiply_bitcast_fusion.4, f32[64]{0:T(128)S(1)} %get-tuple-element.41), kind=kLoop, calls=%fused_computation.4 | loop fusion | flops 12582912 | bytes 12583936 | tf_op jit(solution)/shard_map/convert_element_type | solution.py:32
  161.3 1.3 collective-permute-start.8
  164.1 2.3 collective-permute-done.9
  166.5 1.3 collective-permute-start.10
  169.7 4.3 %collective-permute-done.11 = bf16[16,18,1,64]{3,0,2,1:T(8,128)(2,1)S(1)} collective-permute-done((bf16[16,18,1,64]{3,0,2,1:T(8,128)(2,1)S(1)}, bf16[16,18,1,64]{3,0,2,1:T(8,128)(2,1)S(1)}, u32[]{:S(2)}, u32[]{:S(2)}) %collective-permute-start.11) | collective-permute-done | bytes 36896 | tf_op jit(solution)/shard_map/ppermute | solution.py:12
  174.0 16.5 %fusion.84 = (f32[64]{0:T(128)S(1)}, f32[64]{0:T(128)S(1)}, f32[16,16,128,64]{3,0,2,1:T(8,128)}) fusion(bf16[4,3,3,64,64]{4,3,2,1,0:T(8,128)(2,1)S(1)} %copy-done.9, bf16[16,18,1,64]{3,0,2,1:T(8,128)(2,1)S(1)} %collective-permute-done.11, bf16[16,1,128,64]{3,0,2,1:T(8,128)(2,1)S(1)} %collective-permute-done.9, ...), kind=kOutput, calls=%fused_computation.142 | convolution fusion | flops 2431795200 | bytes 18121216 | tf_op jit(solution)/shard_map/conv_general_dilated | solution.py:25
  190.6 32.8 %psum.44 = f32[2,64]{1,0:T(2,128)S(1)} all-reduce(f32[2,64]{1,0:T(2,128)S(1)} %pad_maximum_fusion.18), channel_id=1, replica_groups=mesh['dp'=2,'sp2'=4,'sp'=4] {'sp2','sp'}, use_global_device_ids=true, to_apply=%region_8.0 | all-reduce | flops 128 | bytes 1024 | tf_op jit(solution)/shard_map/psum | solution.py:27
  223.4 7.7 %maximum_convert_fusion.1 = bf16[16,16,128,64]{3,0,2,1:T(8,128)(2,1)S(1)} fusion(f32[16,16,128,64]{3,0,2,1:T(8,128)} %get-tuple-element.51, f32[64]{0:T(128)S(1)} %copy-done.6, f32[64]{0:T(128)S(1)} %fusion.72, f32[64]{0:T(128)S(1)} %multiply_bitcast_fusion.3, f32[64]{0:T(128)S(1)} %copy-done.5), kind=kLoop, calls=%fused_computation.2 | loop fusion | flops 12582912 | bytes 12583936 | tf_op jit(solution)/shard_map/convert_element_type | solution.py:32
  231.3 1.3 collective-permute-start.12
  234.1 2.3 collective-permute-done.13
  236.4 1.3 collective-permute-start.14
  237.8 1.3 collective-permute-start.15
  239.7 4.3 %collective-permute-done.15 = bf16[16,18,1,64]{3,0,2,1:T(8,128)(2,1)S(1)} collective-permute-done((bf16[16,18,1,64]{3,0,2,1:T(8,128)(2,1)S(1)}, bf16[16,18,1,64]{3,0,2,1:T(8,128)(2,1)S(1)}, u32[]{:S(2)}, u32[]{:S(2)}) %collective-permute-start.15) | collective-permute-done | bytes 36896 | tf_op jit(solution)/shard_map/ppermute | solution.py:12
  244.0 16.5 %fusion.83 = (f32[64]{0:T(128)S(1)}, f32[64]{0:T(128)S(1)}, f32[16,16,128,64]{3,0,2,1:T(8,128)}) fusion(bf16[4,3,3,64,64]{4,3,2,1,0:T(8,128)(2,1)S(1)} %copy-done.9, bf16[16,18,1,64]{3,0,2,1:T(8,128)(2,1)S(1)} %collective-permute-done.15, bf16[16,1,128,64]{3,0,2,1:T(8,128)(2,1)S(1)} %collective-permute-done.13, ...), kind=kOutput, calls=%fused_computation.141 | convolution fusion | flops 2431795200 | bytes 18121216 | tf_op jit(solution)/shard_map/conv_general_dilated | solution.py:25
  260.5 33.3 %psum.45 = f32[2,64]{1,0:T(2,128)S(1)} all-reduce(f32[2,64]{1,0:T(2,128)S(1)} %pad_maximum_fusion.19), channel_id=1, replica_groups=mesh['dp'=2,'sp2'=4,'sp'=4] {'sp2','sp'}, use_global_device_ids=true, to_apply=%region_11.0 | all-reduce | flops 128 | bytes 1024 | tf_op jit(solution)/shard_map/psum | solution.py:27
  293.9 7.7 %maximum_convert_fusion = bf16[16,16,128,64]{3,0,2,1:T(8,128)(2,1)S(1)} fusion(f32[16,16,128,64]{3,0,2,1:T(8,128)} %get-tuple-element.52, f32[64]{0:T(128)S(1)} %copy-done.4, f32[64]{0:T(128)S(1)} %fusion.70, f32[64]{0:T(128)S(1)} %multiply_bitcast_fusion.2, f32[64]{0:T(128)S(1)} %copy-done.3), kind=kLoop, calls=%fused_computation | loop fusion | flops 12582912 | bytes 12583936 | tf_op jit(solution)/shard_map/convert_element_type | solution.py:32
  301.6 1.6 collective-permute-start.16
  303.3 2.3 collective-permute-done.16
  306.9 4.9 %collective-permute-done.17 = bf16[16,17,1,64]{3,0,2,1:T(8,128)(2,1)S(1)} collective-permute-done((bf16[16,17,1,64]{3,0,2,1:T(8,128)(2,1)S(1)}, bf16[16,17,1,64]{3,0,2,1:T(8,128)(2,1)S(1)}, u32[]{:S(2)}, u32[]{:S(2)}) %collective-permute-start.17) | collective-permute-done | bytes 34848 | tf_op jit(solution)/shard_map/ppermute | solution.py:12
  311.8 8.0 %fusion.88 = (f32[128]{0:T(128)S(1)}, f32[128]{0:T(128)S(1)}, f32[16,8,64,128]{3,0,2,1:T(8,128)}) fusion(bf16[3,3,64,128]{3,2,1,0:T(8,128)(2,1)S(1)} %copy-done.10, bf16[16,17,1,64]{3,0,2,1:T(8,128)(2,1)S(1)} %collective-permute-done.17, bf16[16,1,128,64]{3,0,2,1:T(8,128)(2,1)S(1)} %collective-permute-done.16, ...), kind=kOutput, calls=%fused_computation.146 | convolution fusion | flops 1215596288 | bytes 8834048 | tf_op jit(solution)/shard_map/conv_general_dilated | solution.py:25
  319.8 32.2 %psum.46 = f32[2,128]{1,0:T(2,128)S(1)} all-reduce(f32[2,128]{1,0:T(2,128)S(1)} %pad_maximum_fusion.20), channel_id=1, replica_groups=mesh['dp'=2,'sp2'=4,'sp'=4] {'sp2','sp'}, use_global_device_ids=true, to_apply=%region_14.0 | all-reduce | flops 256 | bytes 2048 | tf_op jit(solution)/shard_map/psum | solution.py:27
  352.0 3.1 maximum_convert_fusion.5
  355.2 1.3 collective-permute-start.18
  357.8 2.1 collective-permute-done.19
  362.9 4.2 %collective-permute-done.21 = bf16[16,10,1,128]{3,0,2,1:T(8,128)(2,1)S(1)} collective-permute-done((bf16[16,10,1,128]{3,0,2,1:T(8,128)(2,1)S(1)}, bf16[16,10,1,128]{3,0,2,1:T(8,128)(2,1)S(1)}, u32[]{:S(2)}, u32[]{:S(2)}) %collective-permute-start.21) | collective-permute-done | bytes 40992 | tf_op jit(solution)/shard_map/ppermute | solution.py:12
  367.1 6.6 %fusion.87 = (f32[128]{0:T(128)S(1)}, f32[128]{0:T(128)S(1)}, f32[16,8,64,128]{3,0,2,1:T(8,128)}) fusion(bf16[1,3,3,128,128]{4,3,2,1,0:T(8,128)(2,1)S(1)} %copy-done, bf16[16,10,1,128]{3,0,2,1:T(8,128)(2,1)S(1)} %collective-permute-done.21, bf16[16,1,64,128]{3,0,2,1:T(8,128)(2,1)S(1)} %collective-permute-done.19, ...), kind=kOutput, calls=%fused_computation.145 | convolution fusion | flops 2424471552 | bytes 7193600 | tf_op jit(solution)/shard_map/conv_general_dilated | solution.py:25
  373.8 30.4 %psum.47 = f32[2,128]{1,0:T(2,128)S(1)} all-reduce(f32[2,128]{1,0:T(2,128)S(1)} %pad_maximum_fusion.21), channel_id=1, replica_groups=mesh['dp'=2,'sp2'=4,'sp'=4] {'sp2','sp'}, use_global_device_ids=true, to_apply=%region_17.0 | all-reduce | flops 256 | bytes 2048 | tf_op jit(solution)/shard_map/psum | solution.py:27
  404.2 3.1 maximum_convert_fusion.4
  407.3 1.9 copy.11
  (71 shorter events, 14.6 us)
Async XLA Ops:
  0.0 367.1 %copy-start = (bf16[1,3,3,128,128]{4,3,2,1,0:T(8,128)(2,1)S(1)}, bf16[1,3,3,128,128]{4,3,2,1,0:T(8,128)(2,1)}, u32[]{:S(2)}) copy-start(bf16[1,3,3,128,128]{4,3,2,1,0:T(8,128)(2,1)} %param.12) | copy-start | bytes 884740
  0.0 26.0 %copy-start.2 = (f32[4,2,64]{2,1,0:T(2,128)S(1)}, f32[4,2,64]{2,1,0:T(2,128)}, u32[]{:S(2)}) copy-start(f32[4,2,64]{2,1,0:T(2,128)} %param.9) | copy-start | bytes 6148
  0.0 30.9 %copy-start.9 = (bf16[4,3,3,64,64]{4,3,2,1,0:T(8,128)(2,1)S(1)}, bf16[4,3,3,64,64]{4,3,2,1,0:T(8,128)(2,1)}, u32[]{:S(2)}) copy-start(bf16[4,3,3,64,64]{4,3,2,1,0:T(8,128)(2,1)} %param.8) | copy-start | bytes 884740
  10.1 20.8 %copy-start.1 = (bf16[16,16,128,64]{3,0,2,1:T(8,128)(2,1)S(1)}, bf16[16,16,128,64]{3,0,2,1:T(8,128)(2,1)}, u32[]{:S(2)}) copy-start(bf16[16,16,128,64]{3,0,2,1:T(8,128)(2,1)} %copy.8) | copy-start | bytes 12582916
  11.6 4.2 %collective-permute-start = (bf16[16,1,128,64]{3,0,2,1:T(8,128)(2,1)S(1)}, bf16[16,1,128,64]{3,0,2,1:T(8,128)(2,1)S(1)}, u32[]{:S(2)}, u32[]{:S(2)}) collective-permute-start(bf16[16,1,128,64]{3,0,2,1:T(8,128)(2,1)S(1)} %get-tuple-element.31), channel_id=1, source_target_pairs={{0,1},{1,2},{2,3},{4,5},{5,6},{6,7},{8,9},{9,10},{10,11},{12,13},{... | collective-permute-start | bytes 786440 | tf_op jit(solution)/shard_map/ppermute | solution.py:15
  14.4 5.9 %collective-permute-start.1 = (bf16[16,1,128,64]{3,0,2,1:T(8,128)(2,1)S(1)}, bf16[16,1,128,64]{3,0,2,1:T(8,128)(2,1)S(1)}, u32[]{:S(2)}, u32[]{:S(2)}) collective-permute-start(bf16[16,1,128,64]{3,0,2,1:T(8,128)(2,1)S(1)} %get-tuple-element.32), channel_id=1, source_target_pairs={{1,0},{2,1},{3,2},{5,4},{6,5},{7,6},{9,8},{10,9},{11,10},{13,12},{... | collective-permute-start | bytes 786440 | tf_op jit(solution)/shard_map/ppermute | solution.py:12
  21.2 5.5 %collective-permute-start.2 = (bf16[16,18,1,64]{3,0,2,1:T(8,128)(2,1)S(1)}, bf16[16,18,1,64]{3,0,2,1:T(8,128)(2,1)S(1)}, u32[]{:S(2)}, u32[]{:S(2)}) collective-permute-start(bf16[16,18,1,64]{3,0,2,1:T(8,128)(2,1)S(1)} %get-tuple-element.23), channel_id=1, source_target_pairs={{0,4},{4,8},{8,12},{1,5},{5,9},{9,13},{2,6},{6,10},{10,14},{3,7},{... | collective-permute-start | bytes 110600 | tf_op jit(solution)/shard_map/ppermute | solution.py:15
  24.7 6.2 %collective-permute-start.3 = (bf16[16,18,1,64]{3,0,2,1:T(8,128)(2,1)S(1)}, bf16[16,18,1,64]{3,0,2,1:T(8,128)(2,1)S(1)}, u32[]{:S(2)}, u32[]{:S(2)}) collective-permute-start(bf16[16,18,1,64]{3,0,2,1:T(8,128)(2,1)S(1)} %get-tuple-element.24), channel_id=1, source_target_pairs={{4,0},{8,4},{12,8},{5,1},{9,5},{13,9},{6,2},{10,6},{14,10},{7,3},{... | collective-permute-start | bytes 110600 | tf_op jit(solution)/shard_map/ppermute | solution.py:12
  90.7 2.8 collective-permute-start.4
  92.0 3.8 collective-permute-start.5
  95.8 3.3 collective-permute-start.6
  97.1 6.2 %collective-permute-start.7 = (bf16[16,18,1,64]{3,0,2,1:T(8,128)(2,1)S(1)}, bf16[16,18,1,64]{3,0,2,1:T(8,128)(2,1)S(1)}, u32[]{:S(2)}, u32[]{:S(2)}) collective-permute-start(bf16[16,18,1,64]{3,0,2,1:T(8,128)(2,1)S(1)} %get-tuple-element.22), channel_id=1, source_target_pairs={{4,0},{8,4},{12,8},{5,1},{9,5},{13,9},{6,2},{10,6},{14,10},{7,3},{... | collective-permute-start | bytes 110600 | tf_op jit(solution)/shard_map/ppermute | solution.py:12
  161.3 2.8 collective-permute-start.8
  162.6 3.8 collective-permute-start.9
  166.5 3.3 collective-permute-start.10
  167.8 55.6 %copy-start.5 = (f32[64]{0:T(128)S(1)}, f32[64]{0:T(128)}, u32[]{:S(2)}) copy-start(f32[64]{0:T(128)} %get-tuple-element.42) | copy-start | bytes 772
  167.8 55.6 %copy-start.6 = (f32[64]{0:T(128)S(1)}, f32[64]{0:T(128)}, u32[]{:S(2)}) copy-start(f32[64]{0:T(128)} %get-tuple-element.44) | copy-start | bytes 772
  167.8 6.2 %collective-permute-start.11 = (bf16[16,18,1,64]{3,0,2,1:T(8,128)(2,1)S(1)}, bf16[16,18,1,64]{3,0,2,1:T(8,128)(2,1)S(1)}, u32[]{:S(2)}, u32[]{:S(2)}) collective-permute-start(bf16[16,18,1,64]{3,0,2,1:T(8,128)(2,1)S(1)} %get-tuple-element.20), channel_id=1, source_target_pairs={{4,0},{8,4},{12,8},{5,1},{9,5},{13,9},{6,2},{10,6},{14,10},{7,3},{... | collective-permute-start | bytes 110600 | tf_op jit(solution)/shard_map/ppermute | solution.py:12
  231.3 2.8 collective-permute-start.12
  232.6 3.8 collective-permute-start.13
  236.4 3.3 collective-permute-start.14
  237.7 56.1 %copy-start.3 = (f32[64]{0:T(128)S(1)}, f32[64]{0:T(128)}, u32[]{:S(2)}) copy-start(f32[64]{0:T(128)} %get-tuple-element.37) | copy-start | bytes 772
  237.8 56.1 %copy-start.4 = (f32[64]{0:T(128)S(1)}, f32[64]{0:T(128)}, u32[]{:S(2)}) copy-start(f32[64]{0:T(128)} %get-tuple-element.43) | copy-start | bytes 772
  237.8 6.2 %collective-permute-start.15 = (bf16[16,18,1,64]{3,0,2,1:T(8,128)(2,1)S(1)}, bf16[16,18,1,64]{3,0,2,1:T(8,128)(2,1)S(1)}, u32[]{:S(2)}, u32[]{:S(2)}) collective-permute-start(bf16[16,18,1,64]{3,0,2,1:T(8,128)(2,1)S(1)} %get-tuple-element.18), channel_id=1, source_target_pairs={{4,0},{8,4},{12,8},{5,1},{9,5},{13,9},{6,2},{10,6},{14,10},{7,3},{... | collective-permute-start | bytes 110600 | tf_op jit(solution)/shard_map/ppermute | solution.py:12
  301.6 5.3 %copy-start.7 = (f32[2,128]{1,0:T(2,128)S(1)}, f32[2,128]{1,0:T(2,128)}, u32[]{:S(2)}) copy-start(f32[2,128]{1,0:T(2,128)} %param.11) | copy-start | bytes 3076
  301.6 10.2 %copy-start.10 = (bf16[3,3,64,128]{3,2,1,0:T(8,128)(2,1)S(1)}, bf16[3,3,64,128]{3,2,1,0:T(8,128)(2,1)}, u32[]{:S(2)}) copy-start(bf16[3,3,64,128]{3,2,1,0:T(8,128)(2,1)} %param.10) | copy-start | bytes 442372
  301.6 3.9 collective-permute-start.16
  305.6 6.2 %collective-permute-start.17 = (bf16[16,17,1,64]{3,0,2,1:T(8,128)(2,1)S(1)}, bf16[16,17,1,64]{3,0,2,1:T(8,128)(2,1)S(1)}, u32[]{:S(2)}, u32[]{:S(2)}) collective-permute-start(bf16[16,17,1,64]{3,0,2,1:T(8,128)(2,1)S(1)} %pad_maximum_fusion.12), channel_id=1, source_target_pairs={{4,0},{8,4},{12,8},{5,1},{9,5},{13,9},{6,2},{10,6},{14,10},{7,3},{... | collective-permute-start | bytes 104456 | tf_op jit(solution)/shard_map/ppermute | solution.py:12
  319.8 42.7 %copy-start.8 = (f32[1,2,128]{2,1,0:T(2,128)S(1)}, f32[1,2,128]{2,1,0:T(2,128)}, u32[]{:S(2)}) copy-start(f32[1,2,128]{2,1,0:T(2,128)} %param.13) | copy-start | bytes 3076
  355.2 2.6 collective-permute-start.18
  356.5 3.4 collective-permute-start.19
  359.9 3.0 collective-permute-start.20
  361.2 5.9 %collective-permute-start.21 = (bf16[16,10,1,128]{3,0,2,1:T(8,128)(2,1)S(1)}, bf16[16,10,1,128]{3,0,2,1:T(8,128)(2,1)S(1)}, u32[]{:S(2)}, u32[]{:S(2)}) collective-permute-start(bf16[16,10,1,128]{3,0,2,1:T(8,128)(2,1)S(1)} %get-tuple-element.34), channel_id=1, source_target_pairs={{4,0},{8,4},{12,8},{5,1},{9,5},{13,9},{6,2},{10,6},{14,10},{7,3},{... | collective-permute-start | bytes 122888 | tf_op jit(solution)/shard_map/ppermute | solution.py:12
where the time goes:
time: 410 us; the launch traced here: 409 us
  blocking collectives  198 us (48%)
  matrix products  80.7 us (20%)
  waiting for transfers between devices  45.2 us (11%)
  other arithmetic  38 us (9%)
  starting transfers between devices  32.5 us (8%)
  local copies, waits for them, and re-layouts  14.8 us (4%)
    psum x6, blocking collectives, conv_bn(): moments = lax.psum(moments, ('sp2', 'sp'))  198 us
    conv_general_dilated x6, matrix products, conv_bn(): lax.conv_general_dilated(extended, weight, (stride, stride), 'VALID', dim...  80.7 us
    ppermute x12, waiting for transfers between devices, edge_extend(): lax.ppermute(first_line, axis_name, perm=[(device + 1, device) for device...  42.1 us
    convert_element_type x6, other arithmetic, conv_bn(): return jnp.maximum(normed, 0.0).astype(jnp.bfloat16)  36.8 us
    ppermute x10, starting transfers between devices, edge_extend(): lax.ppermute(last_line, axis_name, perm=[(device, device + 1) for device...  16.7 us
    ppermute x12, starting transfers between devices, edge_extend(): lax.ppermute(first_line, axis_name, perm=[(device + 1, device) for device...  15.9 us
    unnamed x23, local copies, waits for them, and re-layouts  10.1 us
  transfers between devices with their start and end apart: 22, of which 21 were waited for; matrix products, arithmetic and copies ran while one was open for 0% of the time, Pallas kernels for 0%

commit v1 on v0

v1 whole, which is shorter than its diff:
```python
import functools

import jax
import jax.numpy as jnp
from jax import lax
from jax.experimental import pallas as pl
from jax.experimental.pallas import tpu as pltpu
from jax.sharding import PartitionSpec as P

MESH = pl.DeviceIdType.MESH
F32 = jnp.float32
BF16 = jnp.bfloat16
BIG = 3.0e38
EPS = 1e-5
PAD = 8


def kernel(dims, x_ref, w_a, bn_a, w_down, bn_down, w_b, bn_b, out_ref,
           xv, z, as0, as1, bb0, bb1, wmat, edge_l, edge_r, halo_u, halo_d, halo_l, halo_r, corner_s, corner_r,
           stats, acc, cst, caps, x_sem, row_send, row_recv, col_send, col_recv, cor_send, cor_recv, st_send, st_recv):
    n_img, rows, pairs, ch, n_sp2, n_sp = dims
    half = rows // 2
    last = PAD + pairs
    n_dev = n_sp2 * n_sp
    sp = lax.axis_index("sp")
    sp2 = lax.axis_index("sp2")
    me = sp2 * n_sp + sp
    has_u, has_d = sp > 0, sp < n_sp - 1
    has_l, has_r = sp2 > 0, sp2 < n_sp2 - 1

    def x_copy(img):
        return pltpu.make_async_copy(x_ref.at[img], xv.at[img], x_sem.at[img])

    for img in range(n_img):
        x_copy(img).start()

    def clear(img, carry):
        for par in range(2):
            halo_u[par, img] = jnp.zeros((pairs + 2 * PAD, 128), F32)
            halo_d[par, img] = jnp.zeros((pairs + 2 * PAD, 128), F32)
            halo_l[par, img] = jnp.zeros((rows, 128), F32)
            halo_r[par, img] = jnp.zeros((rows, 128), F32)
        return carry

    lax.fori_loop(0, n_img, clear, 0)
    for par in range(2):
        for c in range(4):
            corner_r[par, c] = jnp.zeros((n_img, 128), F32)

    sub = lax.broadcasted_iota(jnp.int32, (8, 128), 0)
    lane8 = lax.broadcasted_iota(jnp.int32, (8, 128), 1)
    caps[0] = jnp.where((sub == 0) & (lane8 >= ch), jnp.where(has_l, BIG, 0.0), BIG)
    caps[1] = jnp.where((sub == 7) & (lane8 < ch), jnp.where(has_r, BIG, 0.0), BIG)
    caps[2] = jnp.full((8, 128), jnp.where(has_u, BIG, 0.0), F32)
    caps[3] = jnp.full((8, 128), jnp.where(has_d, BIG, 0.0), F32)
    caps[4] = jnp.where(sub == 0, jnp.where(has_l, BIG, 0.0), BIG)
    caps[5] = jnp.where(sub == 7, jnp.where(has_r, BIG, 0.0), BIG)

    barrier = pltpu.get_barrier_semaphore()
    for d in range(1, n_dev):
        peer = lax.rem(me + d, n_dev)
        pl.semaphore_signal(barrier, inc=1, device_id={"sp2": peer // n_sp, "sp": lax.rem(peer, n_sp)}, device_id_type=MESH)
    pl.semaphore_wait(barrier, n_dev - 1)

    def rcopy(src, dst, ssem, rsem, to_sp2, to_sp):
        return pltpu.make_async_remote_copy(src_ref=src, dst_ref=dst, send_sem=ssem, recv_sem=rsem,
                                            device_id={"sp2": to_sp2, "sp": to_sp}, device_id_type=MESH)

    row_data = pl.ds(PAD, pairs)

    def start_edges(img, par, n_rows):
        @pl.when(has_u)
        def _():
            rcopy(z.at[img, 0, row_data], halo_d.at[par, img, row_data], row_send.at[0], row_recv.at[par, 1], sp2, sp - 1).start()

        @pl.when(has_d)
        def _():
            rcopy(z.at[img, n_rows - 1, row_data], halo_u.at[par, img, row_data], row_send.at[1], row_recv.at[par, 0], sp2, sp + 1).start()

        r_all = pl.ds(0, n_rows)

        @pl.when(has_l)
        def _():
            rcopy(edge_l.at[img, r_all], halo_r.at[par, img, r_all], col_send.at[0], col_recv.at[par, 1], sp2 - 1, sp).start()

        @pl.when(has_r)
        def _():
            rcopy(edge_r.at[img, r_all], halo_l.at[par, img, r_all], col_send.at[1], col_recv.at[par, 0], sp2 + 1, sp).start()

    corner_to = ((has_u & has_l, -1, -1, 3), (has_u & has_r, 1, -1, 2), (has_d & has_l, -1, 1, 1), (has_d & has_r, 1, 1, 0))

    def start_corners(par):
        for c, (there, d_sp2, d_sp, slot) in enumerate(corner_to):
            @pl.when(there)
            def _():
                rcopy(corner_s.at[c], corner_r.at[par, slot], cor_send.at[c], cor_recv.at[par, slot], sp2 + d_sp2, sp + d_sp).start()

    def wait_edges(par, n_rows):
        r_all = pl.ds(0, n_rows)
        every = pl.ds(0, n_img)

        @pl.when(has_u)
        def _():
            rcopy(z.at[every, 0, row_data], halo_u.at[par, every, row_data], row_send.at[0], row_recv.at[par, 0], sp2, sp).wait()

        @pl.when(has_d)
        def _():
            rcopy(z.at[every, n_rows - 1, row_data], halo_d.at[par, every, row_data], row_send.at[1], row_recv.at[par, 1], sp2, sp).wait()

        @pl.when(has_l)
        def _():
            rcopy(edge_l.at[every, r_all], halo_l.at[par, every, r_all], col_send.at[0], col_recv.at[par, 0], sp2, sp).wait()

        @pl.when(has_r)
        def _():
            rcopy(edge_r.at[every, r_all], halo_r.at[par, every, r_all], col_send.at[1], col_recv.at[par, 1], sp2, sp).wait()

        for c, (there, d_sp2, d_sp, slot) in enumerate(corner_to):
            @pl.when(there)
            def _():
                rcopy(corner_s.at[c], corner_r.at[par, c], cor_send.at[c], cor_recv.at[par, c], sp2, sp).wait()

    def stat_copy(d, par):
        peer = lax.rem(me + d, n_dev)
        return rcopy(stats.at[par, me], stats.at[par, me], st_send.at[d - 1], st_recv.at[par, me], peer // n_sp, lax.rem(peer, n_sp))

    def start_stats(par):
        total = acc[0] + acc[1]
        both = jnp.concatenate([jnp.sum(total[:, :128], axis=0, keepdims=True), jnp.sum(total[:, 128:], axis=0, keepdims=True)], axis=0)
        stats[par, me] = both
        for d in range(1, n_dev):
            stat_copy(d, par).start()

    def wait_stats(par):
        for d in range(1, n_dev):
            stat_copy(d, par).wait_send()
            src = lax.rem(me + d, n_dev)
            rcopy(stats.at[par, src], stats.at[par, src], st_send.at[d - 1], st_recv.at[par, src], sp2, sp).wait_recv()

    def set_constants(par, gain, shift, count, paired):
        total = stats[par, 0]
        for src in range(1, n_dev):
            total = total + stats[par, src]
        if paired:
            total = total + pltpu.roll(total, ch, 1)
        mean = total[0:1] * (1.0 / count)
        var = total[1:2] * (1.0 / count) - mean * mean
        cst[0:1, :] = mean
        cst[1:2, :] = gain * lax.rsqrt(var + EPS)
        cst[2:3, :] = shift

    lane = lax.broadcasted_iota(jnp.int32, (pairs, 128), 1)

    def save_edges(img, n_rows):
        for r in range(n_rows):
            edge_l[img, r:r + 1, :] = z[img, r, PAD:PAD + 1, :]
            edge_r[img, r:r + 1, :] = z[img, r, last - 1:last, :]
        here = pl.ds(img, 1)
        corner_s[0, here, :] = z[img, 0, PAD:PAD + 1, :]
        corner_s[1, here, :] = z[img, 0, last - 1:last, :]
        corner_s[2, here, :] = z[img, n_rows - 1, PAD:PAD + 1, :]
        corner_s[3, here, :] = z[img, n_rows - 1, last - 1:last, :]

    def place_halos(img, par, n_rows):
        for r in range(n_rows):
            z[img, r, PAD - 1:PAD, :] = halo_l[par, img, r:r + 1, :]
            z[img, r, last:last + 1, :] = halo_r[par, img, r:r + 1, :]
        here = pl.ds(img, 1)
        halo_u[par, img, PAD - 1:PAD, :] = corner_r[par, 0, here, :]
        halo_u[par, img, last:last + 1, :] = corner_r[par, 1, here, :]
        halo_d[par, img, PAD - 1:PAD, :] = corner_r[par, 2, here, :]
        halo_d[par, img, last:last + 1, :] = corner_r[par, 3, here, :]

    def line_views(img, par, n_rows):
        def view(p):
            if p == 0:
                return lambda off: halo_u[par, img, off:off + pairs, :]
            if p == n_rows + 1:
                return lambda off: halo_d[par, img, off:off + pairs, :]
            return lambda off: z[img, p - 1, off:off + pairs, :]
        return view

    def normalise(v, lower):
        return jnp.maximum((v - cst[0:1, :]) * cst[1:2, :] + cst[2:3, :], lower)

    def cap_cols(v, first, final):
        return jnp.concatenate([jnp.minimum(v[0:8], caps[first]), v[8:pairs - 8], jnp.minimum(v[pairs - 8:], caps[final])], axis=0)

    def build_pairs(img, par, dst, lower, skip_top=False):
        place_halos(img, par, rows)
        view = line_views(img, par, rows)
        for p in range(1 if skip_top else 0, rows + 2):
            load = view(p)
            own = load(PAD)
            if lower is None:
                side = jnp.where(lane < ch, load(PAD + 1), load(PAD - 1))
            else:
                own = normalise(own, lower)
                side = normalise(jnp.where(lane < ch, load(PAD + 1), load(PAD - 1)), lower)
            side = cap_cols(side, 0, 1) if lower is not None else mask_cols(side)
            if p in (0, rows + 1):
                edge = 2 if p == 0 else 3
                if lower is not None:
                    own = jnp.minimum(own, caps[edge, 0:1, :])
                    side = jnp.minimum(side, caps[edge, 0:1, :])
            base = (p % 2) * 256
            dst[p // 2, :, base:base + 128] = own.astype(BF16)
            dst[p // 2, :, base + 128:base + 256] = side.astype(BF16)

    def mask_cols(v):
        return v

    def build_wide(img, par, dst):
        place_halos(img, par, half)
        view = line_views(img, par, half)
        for p in range(half + 2):
            load = view(p)
            base = (p % 2) * 384
            for k in range(3):
                v = normalise(load(PAD - 1 + k), 0.0)
                if k == 0:
                    v = jnp.concatenate([jnp.minimum(v[0:8], caps[4]), v[8:]], axis=0)
                if k == 2:
                    v = jnp.concatenate([v[:pairs - 8], jnp.minimum(v[pairs - 8:], caps[5])], axis=0)
                if p in (0, half + 1):
                    v = jnp.minimum(v, caps[2 if p == 0 else 3, 0:1, :])
                dst[p // 2, :, base + 128 * k:base + 128 * (k + 1)] = v.astype(BF16)

    def add_stats(o):
        folded = o.reshape(o.shape[0] // 8, 8, o.shape[1])
        s = jnp.sum(folded, axis=0)
        q = jnp.sum(folded * folded, axis=0)
        acc[0] += jnp.concatenate([s[:, :128], q[:, :128]], axis=1)
        acc[1] += jnp.concatenate([s[:, 128:], q[:, 128:]], axis=1)

    def put_rows(img, o):
        for i in range(o.shape[0] // pairs):
            part = o[i * pairs:(i + 1) * pairs]
            z[img, 2 * i, row_data, :] = part[:, :128]
            z[img, 2 * i + 1, row_data, :] = part[:, 128:]

    def dot(a, b):
        return jnp.dot(a, b, preferred_element_type=F32)

    def conv_pairs(img, src):
        o = dot(src[0:half].reshape(half * pairs, 512), wmat[0:512]) + dot(src[1:half + 1].reshape(half * pairs, 512), wmat[512:1024])
        put_rows(img, o)
        add_stats(o)
        save_edges(img, rows)

    def conv_down(img, src):
        quarter = half // 2

        def pick(offset, lo):
            return jnp.concatenate([src[2 * i + offset, :, lo:512] for i in range(quarter)], axis=0)

        o = dot(pick(0, 256), wmat[0:256]) + dot(pick(1, 0), wmat[256:768]) + dot(pick(2, 0), wmat[768:1280])
        put_rows(img, o)
        add_stats(o)
        save_edges(img, half)

    def conv_wide(img, src):
        quarter = half // 2
        o = dot(src[0:quarter].reshape(quarter * pairs, 768), wmat[0:768]) + dot(src[1:quarter + 1].reshape(quarter * pairs, 768), wmat[768:1536])
        put_rows(img, o)
        add_stats(o)

    def run_layer(build, conv, buf0, buf1, par_out, rows_out, send):
        acc[...] = jnp.zeros_like(acc)
        build(0, buf0)

        def body(t, carry):
            i0 = 2 * t
            build(i0 + 1, buf1)
            conv(i0, buf0)
            if send:
                start_edges(i0, par_out, rows_out)
            build(jnp.minimum(i0 + 2, n_img - 1), buf0)
            conv(i0 + 1, buf1)
            if send:
                start_edges(i0 + 1, par_out, rows_out)
            return carry

        lax.fori_loop(0, n_img // 2, body, 0)

    def put_block(k, n_rows_k, n_taps, blocks):
        for o, blk in enumerate(blocks):
            val = jnp.zeros((n_rows_k, 128), BF16) if blk is None else blk
            wmat[k * n_rows_k:(k + 1) * n_rows_k, o * 128:(o + 1) * 128] = val

    def weights_pairs(layer):
        zero = jnp.zeros((ch, ch), BF16)
        q = []
        for kh in range(3):
            w0, w1, w2 = w_a[layer, kh, 0], w_a[layer, kh, 1], w_a[layer, kh, 2]
            q.append(jnp.concatenate([
                jnp.concatenate([w1, w0], axis=1),
                jnp.concatenate([w2, w1], axis=1),
                jnp.concatenate([zero, w2], axis=1),
                jnp.concatenate([w0, zero], axis=1)], axis=0))
        for k in range(4):
            put_block(k, 256, 4, [q[k] if k < 3 else None, q[k - 1] if k > 0 else None])

    def weights_down():
        d = [jnp.concatenate([w_down[kh, 0], w_down[kh, 1], w_down[kh, 2], jnp.zeros((ch, 128), BF16)], axis=0) for kh in range(3)]
        for k in range(5):
            put_block(k, 256, 4, [d[k] if k < 3 else None, d[k - 2] if k >= 2 else None])

    def weights_wide():
        e = [jnp.concatenate([w_b[0, kh, 0], w_b[0, kh, 1], w_b[0, kh, 2]], axis=0) for kh in range(3)]
        for k in range(4):
            put_block(k, 384, 3, [e[k] if k < 3 else None, e[k - 1] if k > 0 else None])

    wrow = lax.broadcasted_iota(jnp.int32, (128, 128), 0)
    wcol = lax.broadcasted_iota(jnp.int32, (128, 128), 1)
    source = jnp.where(wrow < pairs, 2 * wrow, 2 * (wrow - pairs) + 1)
    wmat[0:128, 0:128] = jnp.where(source == wcol, 1.0, 0.0).astype(BF16)

    def load_image(img, carry):
        x_copy(img).wait()
        for g in range(rows // 4):
            block = xv[img, 4 * g:4 * g + 4].reshape(4 * ch, 128)
            t = lax.dot_general(wmat[0:128, 0:128], block, (((1,), (1,)), ((), ())), preferred_element_type=F32)
            for b in range(2):
                even = t[0:pairs, 128 * b:128 * b + 128]
                odd = t[pairs:2 * pairs, 128 * b:128 * b + 128]
                r = 4 * g + 2 * b
                z[img, r, row_data, :] = jnp.where(lane < ch, even, pltpu.roll(odd, ch, 1))
                z[img, r + 1, row_data, :] = jnp.where(lane < ch, pltpu.roll(even, ch, 1), odd)
        save_edges(img, rows)
        start_edges(img, 0, rows)
        return carry

    lax.fori_loop(0, n_img, load_image, 0)
    start_corners(0)

    count_a = float(n_dev * n_img * rows * pairs * 2)
    count_b = float(n_dev * n_img * half * pairs)

    weights_pairs(0)
    wait_edges(0, rows)
    run_layer(lambda i, buf: build_pairs(i, 0, buf, None), conv_pairs, as0, as1, 1, rows, True)
    start_corners(1)
    start_stats(1)

    def gains(layer):
        g, s = bn_a[layer, 0:1, :], bn_a[layer, 1:2, :]
        return jnp.concatenate([g, g], axis=1), jnp.concatenate([s, s], axis=1)

    n_layers = w_a.shape[0]

    def a_layer(layer, carry):
        par = lax.rem(layer, 2)
        weights_pairs(layer)
        wait_edges(par, rows)
        wait_stats(par)
        g, s = gains(layer - 1)
        set_constants(par, g, s, count_a, True)
        run_layer(lambda i, buf: build_pairs(i, par, buf, 0.0), conv_pairs, as0, as1, 1 - par, rows, True)
        start_corners(1 - par)
        start_stats(1 - par)
        return carry

    lax.fori_loop(1, n_layers, a_layer, 0)

    par = n_layers % 2
    weights_down()
    wait_edges(par, rows)
    wait_stats(par)
    g, s = gains(n_layers - 1)
    set_constants(par, g, s, count_a, True)
    run_layer(lambda i, buf: build_pairs(i, par, buf, 0.0, True), conv_down, as0, as1, 1 - par, half, True)
    start_corners(1 - par)
    start_stats(1 - par)

    weights_wide()
    wait_edges(1 - par, half)
    wait_stats(1 - par)
    set_constants(1 - par, bn_down[0:1, :], bn_down[1:2, :], count_b, False)
    run_layer(lambda i, buf: build_wide(i, 1 - par, buf), conv_wide, bb0, bb1, par, half, False)
    start_stats(par)
    wait_stats(par)
    set_constants(par, bn_b[0, 0:1, :], bn_b[0, 1:2, :], count_b, False)

    def finish(img, carry):
        for r in range(half):
            out_ref[img, r] = normalise(z[img, r, row_data, :], 0.0).astype(BF16)
        return carry

    lax.fori_loop(0, n_img, finish, 0)


def solution(mesh):
    n_sp, n_sp2 = mesh.shape["sp"], mesh.shape["sp2"]

    def per_device(x, w_a, bn_a, w_down, bn_down, w_b, bn_b):
        n_img, rows, cols, ch = x.shape
        pairs, half = cols // 2, rows // 2
        n_dev = n_sp * n_sp2
        dims = (n_img, rows, pairs, ch, n_sp2, n_sp)
        wide = pairs + 2 * PAD
        vmem = pltpu.VMEM
        dma = pltpu.SemaphoreType.DMA
        scratch = [
            vmem((n_img, rows, ch, cols), BF16),
            vmem((n_img, rows, wide, 128), F32),
            vmem((half + 1, pairs, 512), BF16),
            vmem((half + 1, pairs, 512), BF16),
            vmem((half // 2 + 1, pairs, 768), BF16),
            vmem((half // 2 + 1, pairs, 768), BF16),
            vmem((1536, 256), BF16),
            vmem((n_img, rows, 128), F32),
            vmem((n_img, rows, 128), F32),
            vmem((2, n_img, wide, 128), F32),
            vmem((2, n_img, wide, 128), F32),
            vmem((2, n_img, rows, 128), F32),
            vmem((2, n_img, rows, 128), F32),
            vmem((4, n_img, 128), F32),
            vmem((2, 4, n_img, 128), F32),
            vmem((2, n_dev, 2, 128), F32),
            vmem((2, 8, 256), F32),
            vmem((8, 128), F32),
            vmem((6, 8, 128), F32),
            dma((n_img,)),
            dma((2,)), dma((2, 2)),
            dma((2,)), dma((2, 2)),
            dma((4,)), dma((2, 4)),
            dma((n_dev - 1,)), dma((2, n_dev)),
        ]
        in_vmem = pl.BlockSpec(memory_space=pltpu.VMEM)
        return pl.pallas_call(
            functools.partial(kernel, dims),
            out_shape=jax.ShapeDtypeStruct((n_img, half, pairs, 128), BF16),
            in_specs=[pl.BlockSpec(memory_space=pl.ANY)] + [in_vmem] * 6,
            out_specs=in_vmem,
            scratch_shapes=scratch,
            compiler_params=pltpu.CompilerParams(collective_id=0, has_side_effects=True, vmem_limit_bytes=56 * 1024 * 1024),
        )(jnp.transpose(x, (0, 1, 3, 2)), w_a, bn_a, w_down, bn_down, w_b, bn_b)

    tile_spec = P("dp", "sp", "sp2", None)
    return jax.shard_map(per_device, mesh=mesh, in_specs=(tile_spec, P(), P(), P(), P(), P(), P()), out_specs=tile_spec, check_vma=False)
```

time: 410 us -> 117 us (0.29)
  blocking collectives: 198 us -> 0 us
  Pallas kernels: 0 us -> 114 us
  matrix products: 80.7 us -> 0 us
  waiting for transfers between devices: 45.2 us -> 0 us
  other arithmetic: 38 us -> 0 us
  starting transfers between devices: 32.5 us -> 0 us
  local copies, waits for them, and re-layouts: 14.8 us -> 3.14 us
    psum x6 -> x0, blocking collectives: 198 us -> none  [conv_bn(): moments = lax.psum(moments, ('sp2', 'sp'))]
    pallas_call x0 -> x1, Pallas kernels: none -> 114 us  [per_device(): pl.pallas_call(functools.partial(kernel, dims), out_shape=jax.ShapeDtypeS...]
    conv_general_dilated x6 -> x0, matrix products: 80.7 us -> none  [conv_bn(): lax.conv_general_dilated(extended, weight, (stride, stride), 'VALID', dim...]
    ppermute x22 -> x0, waiting for transfers between devices: 45.2 us -> none  [the longest x12 42.1 us: edge_extend(): lax.ppermute(first_line, axis_name, perm=[(device + 1, device) for device...]
    convert_element_type x6 -> x0, other arithmetic: 36.8 us -> none  [conv_bn(): return jnp.maximum(normed, 0.0).astype(jnp.bfloat16)]
    ppermute x22 -> x0, starting transfers between devices: 32.5 us -> none  [the longest x10 16.7 us: edge_extend(): lax.ppermute(last_line, axis_name, perm=[(device, device + 1) for device...]
    unnamed x23 -> x1, local copies, waits for them, and re-layouts: 10.1 us -> 3.14 us
  transfers between devices with their start and end apart: 22 -> 0, of which waited for: 21 -> 0; matrix products, arithmetic and copies ran while one was open for 0% -> 0% of each run, Pallas kernels for 0% -> 0%
where the time goes in v1:
time: 117 us
  Pallas kernels  114 us (97%)
  local copies, waits for them, and re-layouts  3.14 us (3%)
    pallas_call x1, Pallas kernels, per_device(): pl.pallas_call(functools.partial(kernel, dims), out_shape=jax.ShapeDtypeS...  114 us
    unnamed x1, local copies, waits for them, and re-layouts  3.14 us

profile of v1, /device:TPU:0, one launch (start us, length us, event | category | flops | bytes accessed | tf_op | source)
XLA Modules:
  0.0 117.0 jit_solution(13203388996224455495)
XLA Ops:
  0.0 113.8 %shard_map.73 = bf16[16,8,64,128]{3,2,1,0:T(8,128)(2,1)} custom-call(bf16[16,16,64,128]{3,2,1,0:T(8,128)(2,1)} %bitcast.1, bf16[4,3,3,64,64]{4,3,2,1,0:T(8,128)(2,1)} %w_a.1, f32[4,2,64]{2,1,0:T(2,128)} %bn_a.1, bf16[3,3,64,128]{3,2,1,0:T(8,128)(2,1)} %w_down.1, f32[2,128]{1,0:T(2,128)} %bn_down.1, bf16[1,3,3,128,128]{4,3,2,1,0:T(8,128)(2,1)} %w_b.1, ...), custom_call_target="tpu_custom_call" | custom-call | tf_op jit(solution)/shard_map/pallas_call | solution.py:431
  113.8 3.1 %copy.9 = bf16[16,8,64,128]{3,2,1,0:T(8,128)(2,1)} copy(bf16[16,8,64,128]{3,2,1,0:T(8,128)(2,1)} %shard_map.73) | data formatting | bytes 4194304

commit v2 on v1

v2 whole, which is shorter than its diff:
```python
import functools

import jax
import jax.numpy as jnp
from jax import lax
from jax.experimental import pallas as pl
from jax.experimental.pallas import tpu as pltpu
from jax.sharding import PartitionSpec as P

MESH = pl.DeviceIdType.MESH
F32 = jnp.float32
BF16 = jnp.bfloat16
EPS = 1e-5
GROUP = 2
EDGE = 8


def normalise(v, cst):
    return jnp.maximum((v - cst[0:1, :]) * cst[1:2, :] + cst[2:3, :], 0.0)


def stack_kernel(dims, x_ref, w_a, bn_a, w_down, bn_down, w_b, bn_b, z_out, cst_out,
                 xv, z, as0, as1, bb0, bb1, lines, wmat, perm, edge_l, edge_r, halo_u, halo_d, halo_l, halo_r,
                 corner_s, corner_r, corner_n, stats, acc, cst,
                 x_sem, z_sem, row_send, row_recv, col_send, col_recv, cor_send, cor_recv, st_send, st_recv):
    n_img, rows, pairs, ch, n_sp2, n_sp = dims
    half, quarter = rows // 2, rows // 4
    wide = pairs + 2 * EDGE
    n_dev = n_sp2 * n_sp
    sp = lax.axis_index("sp")
    sp2 = lax.axis_index("sp2")
    me = sp2 * n_sp + sp
    has_u, has_d = sp > 0, sp < n_sp - 1
    has_l, has_r = sp2 > 0, sp2 < n_sp2 - 1

    def x_copy(img):
        return pltpu.make_async_copy(x_ref.at[img], xv.at[img], x_sem.at[img])

    for img in range(n_img):
        x_copy(img).start()

    barrier = pltpu.get_barrier_semaphore()
    for d in range(1, n_dev):
        peer = lax.rem(me + d, n_dev)
        pl.semaphore_signal(barrier, inc=1, device_id={"sp2": peer // n_sp, "sp": lax.rem(peer, n_sp)}, device_id_type=MESH)

    def rcopy(src, dst, ssem, rsem, to_sp2, to_sp):
        return pltpu.make_async_remote_copy(src_ref=src, dst_ref=dst, send_sem=ssem, recv_sem=rsem,
                                            device_id={"sp2": to_sp2, "sp": to_sp}, device_id_type=MESH)

    def start_edges(img, par, n_rows):
        r_all = pl.ds(0, n_rows)

        @pl.when(has_u)
        def _():
            rcopy(z.at[img, 0], halo_d.at[par, img], row_send.at[0], row_recv.at[par, 1], sp2, sp - 1).start()

        @pl.when(has_d)
        def _():
            rcopy(z.at[img, n_rows - 1], halo_u.at[par, img], row_send.at[1], row_recv.at[par, 0], sp2, sp + 1).start()

        @pl.when(has_l)
        def _():
            rcopy(edge_l.at[img, r_all], halo_r.at[par, img, r_all], col_send.at[0], col_recv.at[par, 1], sp2 - 1, sp).start()

        @pl.when(has_r)
        def _():
            rcopy(edge_r.at[img, r_all], halo_l.at[par, img, r_all], col_send.at[1], col_recv.at[par, 0], sp2 + 1, sp).start()

    corner_to = ((has_u & has_l, -1, -1, 3), (has_u & has_r, 1, -1, 2), (has_d & has_l, -1, 1, 1), (has_d & has_r, 1, 1, 0))

    def start_corners(par):
        for c, (there, d_sp2, d_sp, slot) in enumerate(corner_to):
            @pl.when(there)
            def _():
                rcopy(corner_s.at[c], corner_r.at[par, slot], cor_send.at[c], cor_recv.at[par, slot], sp2 + d_sp2, sp + d_sp).start()

    def wait_edges(par, n_rows):
        r_all = pl.ds(0, n_rows)
        every = pl.ds(0, n_img)

        @pl.when(has_u)
        def _():
            rcopy(z.at[every, 0], halo_u.at[par], row_send.at[0], row_recv.at[par, 0], sp2, sp).wait()

        @pl.when(has_d)
        def _():
            rcopy(z.at[every, n_rows - 1], halo_d.at[par], row_send.at[1], row_recv.at[par, 1], sp2, sp).wait()

        @pl.when(has_l)
        def _():
            rcopy(edge_l.at[every, r_all], halo_l.at[par, every, r_all], col_send.at[0], col_recv.at[par, 0], sp2, sp).wait()

        @pl.when(has_r)
        def _():
            rcopy(edge_r.at[every, r_all], halo_r.at[par, every, r_all], col_send.at[1], col_recv.at[par, 1], sp2, sp).wait()

        for c, (there, d_sp2, d_sp, slot) in enumerate(corner_to):
            @pl.when(there)
            def _():
                rcopy(corner_s.at[c], corner_r.at[par, c], cor_send.at[c], cor_recv.at[par, c], sp2, sp).wait()

    def stat_copy(d, par):
        peer = lax.rem(me + d, n_dev)
        return rcopy(stats.at[par, me], stats.at[par, me], st_send.at[d - 1], st_recv.at[par, me], peer // n_sp, lax.rem(peer, n_sp))

    def start_stats(par):
        total = acc[0] + acc[1]
        stats[par, me] = jnp.concatenate([jnp.sum(total[:, :128], axis=0, keepdims=True), jnp.sum(total[:, 128:], axis=0, keepdims=True)], axis=0)
        for d in range(1, n_dev):
            stat_copy(d, par).start()

    def wait_stats(par):
        for d in range(1, n_dev):
            stat_copy(d, par).wait_send()
            src = lax.rem(me + d, n_dev)
            rcopy(stats.at[par, src], stats.at[par, src], st_send.at[d - 1], st_recv.at[par, src], sp2, sp).wait_recv()

    def set_constants(par, gain, shift, count, paired):
        total = stats[par, 0]
        for src in range(1, n_dev):
            total = total + stats[par, src]
        if paired:
            total = total + pltpu.roll(total, ch, 1)
        mean = total[0:1] * (1.0 / count)
        var = total[1:2] * (1.0 / count) - mean * mean
        cst[0:1, :] = mean
        cst[1:2, :] = gain * lax.rsqrt(var + EPS)
        cst[2:3, :] = shift

    lane = lax.broadcasted_iota(jnp.int32, (pairs, 128), 1)

    def save_edges(img, n_rows):
        flat = z.at[img].reshape(rows * pairs, 128)
        first = flat[pl.ds(0, n_rows, stride=pairs), :]
        final = flat[pl.ds(pairs - 1, n_rows, stride=pairs), :]
        edge_l[img, 0:n_rows, :] = first
        edge_r[img, 0:n_rows, :] = final
        here = pl.ds(img, 1)
        corner_s[0, here, :] = first[0:1]
        corner_s[1, here, :] = final[0:1]
        corner_s[2, here, :] = first[n_rows - 1:n_rows]
        corner_s[3, here, :] = final[n_rows - 1:n_rows]

    def act(v, raw):
        return v if raw else normalise(v, cst)

    def prepare_corners(par, raw):
        for c, (there, d_sp2, d_sp, slot) in enumerate(corner_to):
            corner_n[c] = jnp.where(there, act(corner_r[par, c], raw), 0.0)

    def fill_lines(img, par, a, n_rows, raw, first_p):
        left = jnp.where(has_l, act(halo_l[par, img, 0:n_rows, :], raw), 0.0)
        right = jnp.where(has_r, act(halo_r[par, img, 0:n_rows, :], raw), 0.0)
        lines[a, pl.ds(wide + EDGE - 1, n_rows, stride=wide), :] = left
        lines[a, pl.ds(wide + EDGE + pairs, n_rows, stride=wide), :] = right
        here = pl.ds(img, 1)
        bottom = (n_rows + 1) * wide
        lines[a, EDGE - 1:EDGE, :] = corner_n[0, here, :]
        lines[a, EDGE + pairs:EDGE + pairs + 1, :] = corner_n[1, here, :]
        lines[a, bottom + EDGE - 1:bottom + EDGE, :] = corner_n[2, here, :]
        lines[a, bottom + EDGE + pairs:bottom + EDGE + pairs + 1, :] = corner_n[3, here, :]
        out = []
        for p in range(first_p, n_rows + 2):
            if p == 0:
                v = jnp.where(has_u, act(halo_u[par, img], raw), 0.0)
            elif p == n_rows + 1:
                v = jnp.where(has_d, act(halo_d[par, img], raw), 0.0)
            else:
                v = act(z[img, p - 1], raw)
            base = p * wide + EDGE
            lines[a, base:base + pairs, :] = v
            out.append((p, base, v))
        return out

    def build_pairs(g, par, dst, raw, first_p=0):
        for a in range(GROUP):
            for p, base, own in fill_lines(g * GROUP + a, par, a, rows, raw, first_p):
                side = jnp.where(lane < ch, lines[a, base + 1:base + 1 + pairs, :], lines[a, base - 1:base - 1 + pairs, :])
                dst[2 * (p % 2), a, p // 2] = own.astype(BF16)
                dst[2 * (p % 2) + 1, a, p // 2] = side.astype(BF16)

    def build_wide(g, par, dst):
        for a in range(GROUP):
            for p, base, own in fill_lines(g * GROUP + a, par, a, half, False, 0):
                c = 3 * (p % 2)
                dst[c, a, p // 2] = lines[a, base - 1:base - 1 + pairs, :].astype(BF16)
                dst[c + 1, a, p // 2] = own.astype(BF16)
                dst[c + 2, a, p // 2] = lines[a, base + 1:base + 1 + pairs, :].astype(BF16)

    def finish_conv(g, o, n_pairs):
        folded = o.reshape(o.shape[0] // 8, 8, 256)
        s = jnp.sum(folded, axis=0)
        q = jnp.sum(folded * folded, axis=0)
        acc[0] += jnp.concatenate([s[:, :128], q[:, :128]], axis=1)
        acc[1] += jnp.concatenate([s[:, 128:], q[:, 128:]], axis=1)
        for a in range(GROUP):
            for i in range(n_pairs):
                at = (a * n_pairs + i) * pairs
                z[g * GROUP + a, 2 * i] = o[at:at + pairs, :128]
                z[g * GROUP + a, 2 * i + 1] = o[at:at + pairs, 128:]

    def dot(parts, lo):
        lhs = jnp.concatenate(parts, axis=1)
        hi = lo + lhs.shape[1]
        rhs = jnp.concatenate([wmat[0, lo:hi], wmat[1, lo:hi]], axis=1)
        return jnp.dot(lhs, rhs, preferred_element_type=F32)

    def conv_pairs(g, src):
        def part(c, lo):
            return src[c, :, lo:lo + half].reshape(GROUP * half * pairs, 128)

        o = dot([part(c, 0) for c in range(4)], 0) + dot([part(c, 1) for c in range(4)], 512)
        finish_conv(g, o, half)
        for a in range(GROUP):
            save_edges(g * GROUP + a, rows)

    def conv_down(g, src):
        def part(c, offset):
            return jnp.concatenate([src[c, a, 2 * i + offset] for a in range(GROUP) for i in range(quarter)], axis=0)

        o = (dot([part(c, 0) for c in (2, 3)], 0) + dot([part(c, 1) for c in range(4)], 256) + dot([part(c, 2) for c in range(4)], 768))
        finish_conv(g, o, quarter)
        for a in range(GROUP):
            save_edges(g * GROUP + a, half)

    def conv_wide(g, src):
        def part(c, lo):
            return src[c, :, lo:lo + quarter].reshape(GROUP * quarter * pairs, 128)

        o = dot([part(c, 0) for c in range(6)], 0) + dot([part(c, 1) for c in range(6)], 768)
        finish_conv(g, o, quarter)

    n_groups = n_img // GROUP

    def run_layer(build, conv, buf0, buf1, done):
        acc[...] = jnp.zeros_like(acc)
        build(0, buf0)

        def body(t, carry):
            g = 2 * t
            build(g + 1, buf1)
            conv(g, buf0)
            done(g)
            build(jnp.minimum(g + 2, n_groups - 1), buf0)
            conv(g + 1, buf1)
            done(g + 1)
            return carry

        lax.fori_loop(0, n_groups // 2, body, 0)

    def send_edges(par, n_rows):
        def done(g):
            for a in range(GROUP):
                start_edges(g * GROUP + a, par, n_rows)
        return done

    def z_copy(g):
        some = pl.ds(g * GROUP, GROUP)
        return pltpu.make_async_copy(z.at[some, pl.ds(0, half)], z_out.at[some], z_sem.at[g])

    def put_block(k, n_k, blocks):
        for o, blk in enumerate(blocks):
            wmat[o, k * n_k:(k + 1) * n_k, :] = jnp.zeros((n_k, 128), BF16) if blk is None else blk

    def weights_pairs(layer):
        zero = jnp.zeros((ch, ch), BF16)
        q = []
        for kh in range(3):
            w0, w1, w2 = w_a[layer, kh, 0], w_a[layer, kh, 1], w_a[layer, kh, 2]
            q.append(jnp.concatenate([
                jnp.concatenate([w1, w0], axis=1),
                jnp.concatenate([w2, w1], axis=1),
                jnp.concatenate([zero, w2], axis=1),
                jnp.concatenate([w0, zero], axis=1)], axis=0))
        for k in range(4):
            put_block(k, 256, [q[k] if k < 3 else None, q[k - 1] if k > 0 else None])

    def weights_down():
        d = [jnp.concatenate([w_down[kh, 0], w_down[kh, 1], w_down[kh, 2], jnp.zeros((ch, 128), BF16)], axis=0) for kh in range(3)]
        for k in range(5):
            put_block(k, 256, [d[k] if k < 3 else None, d[k - 2] if k >= 2 else None])

    def weights_wide():
        e = [jnp.concatenate([w_b[0, kh, 0], w_b[0, kh, 1], w_b[0, kh, 2]], axis=0) for kh in range(3)]
        for k in range(4):
            put_block(k, 384, [e[k] if k < 3 else None, e[k - 1] if k > 0 else None])

    wrow = lax.broadcasted_iota(jnp.int32, (128, 128), 0)
    wcol = lax.broadcasted_iota(jnp.int32, (128, 128), 1)
    source = jnp.where(wrow < pairs, 2 * wrow, 2 * (wrow - pairs) + 1)
    perm[...] = jnp.where(source == wcol, 1.0, 0.0).astype(BF16)
    pl.semaphore_wait(barrier, n_dev - 1)

    def load_image(img, carry):
        x_copy(img).wait()
        for g in range(rows // 4):
            block = xv[img, 4 * g:4 * g + 4].reshape(4 * ch, 128)
            t = lax.dot_general(perm[...], block, (((1,), (1,)), ((), ())), preferred_element_type=F32)
            for b in range(2):
                even = t[0:pairs, 128 * b:128 * b + 128]
                odd = t[pairs:2 * pairs, 128 * b:128 * b + 128]
                r = 4 * g + 2 * b
                z[img, r] = jnp.where(lane < ch, even, pltpu.roll(odd, ch, 1))
                z[img, r + 1] = jnp.where(lane < ch, pltpu.roll(even, ch, 1), odd)
        save_edges(img, rows)
        start_edges(img, 0, rows)
        return carry

    lax.fori_loop(0, n_img, load_image, 0)
    start_corners(0)

    count_a = float(n_dev * n_img * rows * pairs * 2)
    count_b = float(n_dev * n_img * half * pairs)

    weights_pairs(0)
    wait_edges(0, rows)
    prepare_corners(0, True)
    run_layer(lambda g, buf: build_pairs(g, 0, buf, True), conv_pairs, as0, as1, send_edges(1, rows))
    start_stats(1)
    start_corners(1)

    def gains(layer):
        g, s = bn_a[layer, 0:1, :], bn_a[layer, 1:2, :]
        return jnp.concatenate([g, g], axis=1), jnp.concatenate([s, s], axis=1)

    n_layers = w_a.shape[0]

    def a_layer(layer, carry):
        par = lax.rem(layer, 2)
        weights_pairs(layer)
        wait_edges(par, rows)
        wait_stats(par)
        g, s = gains(layer - 1)
        set_constants(par, g, s, count_a, True)
        prepare_corners(par, False)
        run_layer(lambda g, buf: build_pairs(g, par, buf, False), conv_pairs, as0, as1, send_edges(1 - par, rows))
        start_stats(1 - par)
        start_corners(1 - par)
        return carry

    lax.fori_loop(1, n_layers, a_layer, 0)

    par = n_layers % 2
    weights_down()
    wait_edges(par, rows)
    wait_stats(par)
    g, s = gains(n_layers - 1)
    set_constants(par, g, s, count_a, True)
    prepare_corners(par, False)
    run_layer(lambda g, buf: build_pairs(g, par, buf, False, 1), conv_down, as0, as1, send_edges(1 - par, half))
    start_stats(1 - par)
    start_corners(1 - par)

    weights_wide()
    wait_edges(1 - par, half)
    wait_stats(1 - par)
    set_constants(1 - par, bn_down[0:1, :], bn_down[1:2, :], count_b, False)
    prepare_corners(1 - par, False)
    run_layer(lambda g, buf: build_wide(g, 1 - par, buf), conv_wide, bb0, bb1, lambda g: z_copy(g).start())
    start_stats(par)
    wait_stats(par)
    set_constants(par, bn_b[0, 0:1, :], bn_b[0, 1:2, :], count_b, False)
    cst_out[...] = cst[...]
    for g in range(n_groups):
        z_copy(g).wait()


def finish_kernel(z_ref, cst_ref, out_ref):
    for img in range(z_ref.shape[0]):
        for r in range(z_ref.shape[1]):
            out_ref[img, r] = normalise(z_ref[img, r], cst_ref).astype(BF16)


def solution(mesh):
    n_sp, n_sp2 = mesh.shape["sp"], mesh.shape["sp2"]

    def per_device(x, w_a, bn_a, w_down, bn_down, w_b, bn_b):
        n_img, rows, cols, ch = x.shape
        pairs, half = cols // 2, rows // 2
        n_dev = n_sp * n_sp2
        dims = (n_img, rows, pairs, ch, n_sp2, n_sp)
        vmem = pltpu.VMEM
        dma = pltpu.SemaphoreType.DMA
        scratch = [
            vmem((n_img, rows, ch, cols), BF16),
            vmem((n_img, rows, pairs, 128), F32),
            vmem((4, GROUP, half + 1, pairs, 128), BF16),
            vmem((4, GROUP, half + 1, pairs, 128), BF16),
            vmem((6, GROUP, half // 2 + 1, pairs, 128), BF16),
            vmem((6, GROUP, half // 2 + 1, pairs, 128), BF16),
            vmem((GROUP, (rows + 2) * (pairs + 2 * EDGE), 128), F32),
            vmem((2, 1536, 128), BF16),
            vmem((128, 128), BF16),
            vmem((n_img, rows, 128), F32),
            vmem((n_img, rows, 128), F32),
            vmem((2, n_img, pairs, 128), F32),
            vmem((2, n_img, pairs, 128), F32),
            vmem((2, n_img, rows, 128), F32),
            vmem((2, n_img, rows, 128), F32),
            vmem((4, n_img, 128), F32),
            vmem((2, 4, n_img, 128), F32),
            vmem((4, n_img, 128), F32),
            vmem((2, n_dev, 2, 128), F32),
            vmem((2, 8, 256), F32),
            vmem((8, 128), F32),
            dma((n_img,)),
            dma((n_img // GROUP,)),
            dma((2,)), dma((2, 2)),
            dma((2,)), dma((2, 2)),
            dma((4,)), dma((2, 4)),
            dma((n_dev - 1,)), dma((2, n_dev)),
        ]
        in_vmem = pl.BlockSpec(memory_space=pltpu.VMEM)
        in_any = pl.BlockSpec(memory_space=pl.ANY)
        z, cst = pl.pallas_call(
            functools.partial(stack_kernel, dims),
            out_shape=(jax.ShapeDtypeStruct((n_img, half, pairs, 128), F32), jax.ShapeDtypeStruct((8, 128), F32)),
            in_specs=[in_any] + [in_vmem] * 6,
            out_specs=(in_any, in_vmem),
            scratch_shapes=scratch,
            compiler_params=pltpu.CompilerParams(collective_id=0, has_side_effects=True, vmem_limit_bytes=48 * 1024 * 1024),
        )(jnp.transpose(x, (0, 1, 3, 2)), w_a, bn_a, w_down, bn_down, w_b, bn_b)
        block = pl.BlockSpec((GROUP, half, pairs, 128), lambda i: (i, 0, 0, 0))
        return pl.pallas_call(
            finish_kernel,
            grid=(n_img // GROUP,),
            out_shape=jax.ShapeDtypeStruct((n_img, half, pairs, 128), BF16),
            in_specs=[block, pl.BlockSpec((8, 128), lambda i: (0, 0))],
            out_specs=block,
        )(z, cst)

    tile_spec = P("dp", "sp", "sp2", None)
    return jax.shard_map(per_device, mesh=mesh, in_specs=(tile_spec, P(), P(), P(), P(), P(), P()), out_specs=tile_spec, check_vma=False)
```

time: 117 us -> 123 us (1.051)
  local copies, waits for them, and re-layouts: 3.14 us -> 7.49 us
    unnamed x1 -> x16, local copies, waits for them, and re-layouts: 3.14 us -> 7.49 us
    pallas_call x1 -> x2, Pallas kernels: 114 us -> 115 us  [the longest x1 109 us: per_device(): pl.pallas_call(functools.partial(stack_kernel, dims), out_shape=(jax.Shap...]
where the time goes in v2:
time: 123 us
  Pallas kernels  115 us (93%)
  local copies, waits for them, and re-layouts  7.49 us (6%)
    pallas_call x1, Pallas kernels, per_device(): pl.pallas_call(functools.partial(stack_kernel, dims), out_shape=(jax.Shap...  109 us
    unnamed x16, local copies, waits for them, and re-layouts  7.49 us
    pallas_call x1, Pallas kernels, per_device(): pl.pallas_call(finish_kernel, grid=(n_img // GROUP,), out_shape=jax.Shape...  6.29 us

profile of v2, /device:TPU:0, one launch (start us, length us, event | category | flops | bytes accessed | tf_op | source)
XLA Modules:
  0.0 122.6 jit_solution(15878685543577048186)
XLA Ops:
  0.0 0.0 copy-start.1
  0.0 1.1 copy-done.1
  1.1 0.0 copy-start.2
  1.1 1.0 copy-done.2
  2.0 0.0 copy-start.3
  2.0 0.9 copy-done.3
  2.9 0.0 copy-start.4
  2.9 0.7 copy-done.4
  3.6 0.0 copy-start.6
  3.6 0.7 copy-done.6
  4.3 0.0 copy-start.7
  4.3 0.7 copy-done.7
  5.0 108.8 %shard_map.73 = (f32[16,8,64,128]{3,2,1,0:T(8,128)S(1)}, f32[8,128]{1,0:T(8,128)S(1)}) custom-call(bf16[16,16,64,128]{3,2,1,0:T(8,128)(2,1)} %bitcast.1, bf16[4,3,3,64,64]{4,3,2,1,0:T(8,128)(2,1)S(1)} %copy-done.1, f32[4,2,64]{2,1,0:T(2,128)S(1)} %copy-done.4, bf16[3,3,64,128]{3,2,1,0:T(8,128)(2,1)S(1)} %copy-done.3, f32[2,128]{1,0:T(2,128)S(1)} %copy-done.6, ...), custom_call_target="tpu_custom_call" | custom-call | tf_op jit(solution)/shard_map/pallas_call | solution.py:416
  113.8 0.0 copy-start
  113.8 1.9 %copy-done = f32[16,8,64,128]{3,2,1,0:T(8,128)} copy-done((f32[16,8,64,128]{3,2,1,0:T(8,128)}, f32[16,8,64,128]{3,2,1,0:T(8,128)S(1)}, u32[]{:S(2)}) %copy-start) | copy-done | bytes 4194328
  115.7 0.0 copy-start.5
  115.7 0.6 copy-done.5
  116.3 6.3 %shard_map.74 = bf16[16,8,64,128]{3,2,1,0:T(8,128)(2,1)} custom-call(f32[16,8,64,128]{3,2,1,0:T(8,128)} %copy-done, f32[8,128]{1,0:T(8,128)} %copy-done.5), custom_call_target="tpu_custom_call" | custom-call | tf_op jit(solution)/shard_map/pallas_call | solution.py:425
Async XLA Ops:
  0.0 1.1 copy-start.1
  1.1 1.0 copy-start.2
  2.0 0.9 copy-start.3
  2.9 0.7 copy-start.4
  3.6 0.7 copy-start.6
  4.3 0.7 copy-start.7
  113.8 1.9 %copy-start = (f32[16,8,64,128]{3,2,1,0:T(8,128)}, f32[16,8,64,128]{3,2,1,0:T(8,128)S(1)}, u32[]{:S(2)}) copy-start(f32[16,8,64,128]{3,2,1,0:T(8,128)S(1)} %get-tuple-element.7.z_ref) | copy-start | bytes 12582916
  115.7 0.6 copy-start.5

commit v3 on v2

v3 whole, which is shorter than its diff:
```python
import functools

import jax
import jax.numpy as jnp
from jax import lax
from jax.experimental import pallas as pl
from jax.experimental.pallas import tpu as pltpu
from jax.sharding import PartitionSpec as P

MESH = pl.DeviceIdType.MESH
F32 = jnp.float32
BF16 = jnp.bfloat16
EPS = 1e-5
UNROLL = 4
SPLIT = 1
VMEM_LIMIT = 56 * 1024 * 1024
EDGE = 8


def normalise(v, cst):
    return jnp.maximum((v - cst[0:1, :]) * cst[1:2, :] + cst[2:3, :], 0.0)


def stack_kernel(dims, x_ref, w_a_ref, bn_a, w_down_ref, bn_down, w_b_ref, bn_b, z_out, cst_out,
                 xv, w_a, w_down, w_b, z, bufs, lines, wmat, perm, edge_u, edge_d, first_u, first_d, edge_l, edge_r, halo_u, halo_d, halo_l, halo_r,
                 corner_s, corner_r, corner_n, stats, acc, cst,
                 x_sem, w_sem, z_sem, row_send, row_recv, col_send, col_recv, cor_send, cor_recv, st_send, st_recv):
    n_img, rows, pairs, ch, n_sp2, n_sp = dims
    half, quarter = rows // 2, rows // 4
    wide = pairs + 2 * EDGE
    n_dev = n_sp2 * n_sp
    sp = lax.axis_index("sp")
    sp2 = lax.axis_index("sp2")
    me = sp2 * n_sp + sp
    has_u, has_d = sp > 0, sp < n_sp - 1
    has_l, has_r = sp2 > 0, sp2 < n_sp2 - 1

    def x_copy(img):
        return pltpu.make_async_copy(x_ref.at[img], xv.at[img], x_sem.at[img])

    for img in range(n_img):
        x_copy(img).start()

    w_copies = [pltpu.make_async_copy(src, dst, w_sem.at[i]) for i, (src, dst) in enumerate(((w_a_ref, w_a), (w_down_ref, w_down), (w_b_ref, w_b)))]
    for copy in w_copies:
        copy.start()

    barrier = pltpu.get_barrier_semaphore()
    for d in range(1, n_dev):
        peer = lax.rem(me + d, n_dev)
        pl.semaphore_signal(barrier, inc=1, device_id={"sp2": peer // n_sp, "sp": lax.rem(peer, n_sp)}, device_id_type=MESH)

    def rcopy(src, dst, ssem, rsem, to_sp2, to_sp):
        return pltpu.make_async_remote_copy(src_ref=src, dst_ref=dst, send_sem=ssem, recv_sem=rsem,
                                            device_id={"sp2": to_sp2, "sp": to_sp}, device_id_type=MESH)

    def start_edges(img, par, n_rows, first=False):
        r_all = pl.ds(0, n_rows)

        @pl.when(has_u)
        def _():
            src, dst = (edge_u.at[img], first_d.at[img]) if first else (z.at[img, 0], halo_d.at[par, img])
            rcopy(src, dst, row_send.at[0], row_recv.at[par, 1], sp2, sp - 1).start()

        @pl.when(has_d)
        def _():
            src, dst = (edge_d.at[img], first_u.at[img]) if first else (z.at[img, n_rows - 1], halo_u.at[par, img])
            rcopy(src, dst, row_send.at[1], row_recv.at[par, 0], sp2, sp + 1).start()

        @pl.when(has_l)
        def _():
            rcopy(edge_l.at[img, r_all], halo_r.at[par, img, r_all], col_send.at[0], col_recv.at[par, 1], sp2 - 1, sp).start()

        @pl.when(has_r)
        def _():
            rcopy(edge_r.at[img, r_all], halo_l.at[par, img, r_all], col_send.at[1], col_recv.at[par, 0], sp2 + 1, sp).start()

    corner_to = ((has_u & has_l, -1, -1, 3), (has_u & has_r, 1, -1, 2), (has_d & has_l, -1, 1, 1), (has_d & has_r, 1, 1, 0))

    def start_corners(par):
        for c, (there, d_sp2, d_sp, slot) in enumerate(corner_to):
            @pl.when(there)
            def _():
                rcopy(corner_s.at[c], corner_r.at[par, slot], cor_send.at[c], cor_recv.at[par, slot], sp2 + d_sp2, sp + d_sp).start()

    def wait_edges(par, n_rows, first=False):
        r_all = pl.ds(0, n_rows)
        every = pl.ds(0, n_img)

        @pl.when(has_u)
        def _():
            src, dst = (edge_u, first_u) if first else (z.at[every, 0], halo_u.at[par])
            rcopy(src, dst, row_send.at[0], row_recv.at[par, 0], sp2, sp).wait()

        @pl.when(has_d)
        def _():
            src, dst = (edge_d, first_d) if first else (z.at[every, n_rows - 1], halo_d.at[par])
            rcopy(src, dst, row_send.at[1], row_recv.at[par, 1], sp2, sp).wait()

        @pl.when(has_l)
        def _():
            rcopy(edge_l.at[every, r_all], halo_l.at[par, every, r_all], col_send.at[0], col_recv.at[par, 0], sp2, sp).wait()

        @pl.when(has_r)
        def _():
            rcopy(edge_r.at[every, r_all], halo_r.at[par, every, r_all], col_send.at[1], col_recv.at[par, 1], sp2, sp).wait()

        for c, (there, d_sp2, d_sp, slot) in enumerate(corner_to):
            @pl.when(there)
            def _():
                rcopy(corner_s.at[c], corner_r.at[par, c], cor_send.at[c], cor_recv.at[par, c], sp2, sp).wait()

    def stat_copy(d, par):
        peer = lax.rem(me + d, n_dev)
        return rcopy(stats.at[par, me], stats.at[par, me], st_send.at[d - 1], st_recv.at[par, me], peer // n_sp, lax.rem(peer, n_sp))

    def start_stats(par):
        total = acc[0] + acc[1]
        stats[par, me] = jnp.concatenate([jnp.sum(total[:, :128], axis=0, keepdims=True), jnp.sum(total[:, 128:], axis=0, keepdims=True)], axis=0)
        for d in range(1, n_dev):
            stat_copy(d, par).start()

    def wait_stats(par):
        for d in range(1, n_dev):
            stat_copy(d, par).wait_send()
            src = lax.rem(me + d, n_dev)
            rcopy(stats.at[par, src], stats.at[par, src], st_send.at[d - 1], st_recv.at[par, src], sp2, sp).wait_recv()

    def set_constants(par, gain, shift, count, paired):
        total = stats[par, 0]
        for src in range(1, n_dev):
            total = total + stats[par, src]
        if paired:
            total = total + pltpu.roll(total, ch, 1)
        mean = total[0:1] * (1.0 / count)
        var = total[1:2] * (1.0 / count) - mean * mean
        cst[0:1, :] = mean
        cst[1:2, :] = gain * lax.rsqrt(var + EPS)
        cst[2:3, :] = shift

    lane = lax.broadcasted_iota(jnp.int32, (pairs, 128), 1)

    def save_edges(img, n_rows):
        flat = z.at[img].reshape(rows * pairs, 128)
        first = flat[pl.ds(0, n_rows, stride=pairs), :]
        final = flat[pl.ds(pairs - 1, n_rows, stride=pairs), :]
        edge_l[img, 0:n_rows, :] = first
        edge_r[img, 0:n_rows, :] = final
        here = pl.ds(img, 1)
        corner_s[0, here, :] = first[0:1]
        corner_s[1, here, :] = final[0:1]
        corner_s[2, here, :] = first[n_rows - 1:n_rows]
        corner_s[3, here, :] = final[n_rows - 1:n_rows]

    def act(v, raw):
        return v if raw else normalise(v, cst)

    def prepare_corners(par, raw):
        for c, (there, d_sp2, d_sp, slot) in enumerate(corner_to):
            corner_n[c] = jnp.where(there, act(corner_r[par, c], raw), 0.0)

    def fill_lines(img, par, u, n_rows, raw, first_p):
        buf = lines[u]
        left = jnp.where(has_l, act(halo_l[par, img, 0:n_rows, :], raw), 0.0)
        right = jnp.where(has_r, act(halo_r[par, img, 0:n_rows, :], raw), 0.0)
        buf[pl.ds(wide + EDGE - 1, n_rows, stride=wide), :] = left
        buf[pl.ds(wide + EDGE + pairs, n_rows, stride=wide), :] = right
        here = pl.ds(img, 1)
        bottom = (n_rows + 1) * wide
        buf[EDGE - 1:EDGE, :] = corner_n[0, here, :]
        buf[EDGE + pairs:EDGE + pairs + 1, :] = corner_n[1, here, :]
        buf[bottom + EDGE - 1:bottom + EDGE, :] = corner_n[2, here, :]
        buf[bottom + EDGE + pairs:bottom + EDGE + pairs + 1, :] = corner_n[3, here, :]
        out = []
        for p in range(first_p, n_rows + 2):
            if p == 0:
                v = jnp.where(has_u, first_u[img].astype(F32) if raw else act(halo_u[par, img], raw), 0.0)
            elif p == n_rows + 1:
                v = jnp.where(has_d, first_d[img].astype(F32) if raw else act(halo_d[par, img], raw), 0.0)
            else:
                v = act(z[img, p - 1], raw)
            base = p * wide + EDGE
            buf[base:base + pairs, :] = v
            out.append((p, base, v))
        return out

    def build_pairs(img, par, u, raw, first_p=0):
        n_q = half + 1
        for p, base, own in fill_lines(img, par, u, rows, raw, first_p):
            side = jnp.where(lane < ch, lines[u][base + 1:base + 1 + pairs, :], lines[u][base - 1:base - 1 + pairs, :])
            bufs[u][2 * (p % 2) * n_q + p // 2] = own.astype(BF16)
            bufs[u][(2 * (p % 2) + 1) * n_q + p // 2] = side.astype(BF16)

    def build_wide(img, par, u):
        n_q = quarter + 1
        for p, base, own in fill_lines(img, par, u, half, False, 0):
            at = 3 * (p % 2) * n_q + p // 2
            bufs[u][at] = lines[u][base - 1:base - 1 + pairs, :].astype(BF16)
            bufs[u][at + n_q] = own.astype(BF16)
            bufs[u][at + 2 * n_q] = lines[u][base + 1:base + 1 + pairs, :].astype(BF16)

    def finish_conv(img, i0, o):
        folded = o.reshape(o.shape[0] // 8, 8, 256)
        s = jnp.sum(folded, axis=0)
        q = jnp.sum(folded * folded, axis=0)
        acc[0] += jnp.concatenate([s[:, :128], q[:, :128]], axis=1)
        acc[1] += jnp.concatenate([s[:, 128:], q[:, 128:]], axis=1)
        for i in range(o.shape[0] // pairs):
            z[img, 2 * (i0 + i)] = o[i * pairs:(i + 1) * pairs, :128]
            z[img, 2 * (i0 + i) + 1] = o[i * pairs:(i + 1) * pairs, 128:]

    def dot(parts):
        lhs = jnp.concatenate(parts, axis=1)
        rhs = jnp.concatenate([wmat[0, 0:lhs.shape[1]], wmat[1, 0:lhs.shape[1]]], axis=1)
        return jnp.dot(lhs, rhs, preferred_element_type=F32)

    def conv_pairs(img, u):
        n_q, n_i = half + 1, half // SPLIT
        for i0 in range(0, half, n_i):
            at = [c * n_q + i0 + lo for lo in (0, 1) for c in range(4)]
            finish_conv(img, i0, dot([bufs[u][k:k + n_i].reshape(n_i * pairs, 128) for k in at]))
        save_edges(img, rows)

    def conv_down(img, u):
        n_q = half + 1
        at = [c * n_q + k for k, c in ((0, 2), (0, 3), (1, 0), (1, 1), (1, 2), (1, 3), (2, 0), (2, 1), (2, 2), (2, 3))]
        finish_conv(img, 0, dot([jnp.concatenate([bufs[u][k + 2 * i] for i in range(quarter)], axis=0) for k in at]))
        save_edges(img, half)

    def conv_wide(img, u):
        n_q = quarter + 1
        at = [c * n_q + lo for lo in (0, 1) for c in range(6)]
        finish_conv(img, 0, dot([bufs[u][k:k + quarter].reshape(quarter * pairs, 128) for k in at]))

    def run_layer(build, conv, done):
        acc[...] = jnp.zeros_like(acc)

        def body(t, carry):
            for u in range(UNROLL):
                build(t * UNROLL + u, u)
                conv(t * UNROLL + u, u)
            for u in range(UNROLL):
                done(t * UNROLL + u)
            return carry

        lax.fori_loop(0, n_img // UNROLL, body, 0)

    def z_copy(img):
        return pltpu.make_async_copy(z.at[img, pl.ds(0, half)], z_out.at[img], z_sem.at[img])

    def put_block(k, n_k, blocks):
        for o, blk in enumerate(blocks):
            wmat[o, k * n_k:(k + 1) * n_k, :] = jnp.zeros((n_k, 128), BF16) if blk is None else blk

    def weights_pairs(layer):
        zero = jnp.zeros((ch, ch), BF16)
        q = []
        for kh in range(3):
            w0, w1, w2 = w_a[layer, kh, 0], w_a[layer, kh, 1], w_a[layer, kh, 2]
            q.append(jnp.concatenate([
                jnp.concatenate([w1, w0], axis=1),
                jnp.concatenate([w2, w1], axis=1),
                jnp.concatenate([zero, w2], axis=1),
                jnp.concatenate([w0, zero], axis=1)], axis=0))
        for k in range(4):
            put_block(k, 256, [q[k] if k < 3 else None, q[k - 1] if k > 0 else None])

    def weights_down():
        d = [jnp.concatenate([w_down[kh, 0], w_down[kh, 1], w_down[kh, 2], jnp.zeros((ch, 128), BF16)], axis=0) for kh in range(3)]
        for k in range(5):
            put_block(k, 256, [d[k] if k < 3 else None, d[k - 2] if k >= 2 else None])

    def weights_wide():
        e = [jnp.concatenate([w_b[0, kh, 0], w_b[0, kh, 1], w_b[0, kh, 2]], axis=0) for kh in range(3)]
        for k in range(4):
            put_block(k, 384, [e[k] if k < 3 else None, e[k - 1] if k > 0 else None])

    wrow = lax.broadcasted_iota(jnp.int32, (128, 128), 0)
    wcol = lax.broadcasted_iota(jnp.int32, (128, 128), 1)
    source = jnp.where(wrow < pairs, 2 * wrow, 2 * (wrow - pairs) + 1)
    perm[...] = jnp.where(source == wcol, 1.0, 0.0).astype(BF16)
    pl.semaphore_wait(barrier, n_dev - 1)

    def load_images(t, carry):
        for img in [t * UNROLL + u for u in range(UNROLL)]:
            x_copy(img).wait()
        for img in [t * UNROLL + u for u in range(UNROLL)]:
            for g in range(rows // 4):
                block = xv[img, 4 * g:4 * g + 4].reshape(4 * ch, 128)
                m = lax.dot_general(perm[...], block, (((1,), (1,)), ((), ())), preferred_element_type=F32)
                for b in range(2):
                    even = m[0:pairs, 128 * b:128 * b + 128]
                    odd = m[pairs:2 * pairs, 128 * b:128 * b + 128]
                    r = 4 * g + 2 * b
                    upper = jnp.where(lane < ch, even, pltpu.roll(odd, ch, 1))
                    lower = jnp.where(lane < ch, pltpu.roll(even, ch, 1), odd)
                    z[img, r] = upper
                    z[img, r + 1] = lower
                    if r == 0:
                        edge_u[img] = upper.astype(BF16)
                    if r + 2 == rows:
                        edge_d[img] = lower.astype(BF16)
            save_edges(img, rows)
        for img in [t * UNROLL + u for u in range(UNROLL)]:
            start_edges(img, 0, rows, True)
        return carry

    lax.fori_loop(0, n_img // UNROLL, load_images, 0)
    start_corners(0)

    count_a = float(n_dev * n_img * rows * pairs * 2)
    count_b = float(n_dev * n_img * half * pairs)

    for copy in w_copies:
        copy.wait()
    weights_pairs(0)
    wait_edges(0, rows, True)
    prepare_corners(0, True)
    run_layer(lambda i, u: build_pairs(i, 0, u, True), conv_pairs, lambda i: start_edges(i, 1, rows))
    start_stats(1)
    start_corners(1)

    def gains(layer):
        g, s = bn_a[layer, 0:1, :], bn_a[layer, 1:2, :]
        return jnp.concatenate([g, g], axis=1), jnp.concatenate([s, s], axis=1)

    n_layers = w_a.shape[0]

    def a_layer(layer, carry):
        par = lax.rem(layer, 2)
        weights_pairs(layer)
        wait_edges(par, rows)
        wait_stats(par)
        g, s = gains(layer - 1)
        set_constants(par, g, s, count_a, True)
        prepare_corners(par, False)
        run_layer(lambda i, u: build_pairs(i, par, u, False), conv_pairs, lambda i: start_edges(i, 1 - par, rows))
        start_stats(1 - par)
        start_corners(1 - par)
        return carry

    lax.fori_loop(1, n_layers, a_layer, 0)

    par = n_layers % 2
    weights_down()
    wait_edges(par, rows)
    wait_stats(par)
    g, s = gains(n_layers - 1)
    set_constants(par, g, s, count_a, True)
    prepare_corners(par, False)
    run_layer(lambda i, u: build_pairs(i, par, u, False, 1), conv_down, lambda i: start_edges(i, 1 - par, half))
    start_stats(1 - par)
    start_corners(1 - par)

    weights_wide()
    wait_edges(1 - par, half)
    wait_stats(1 - par)
    set_constants(1 - par, bn_down[0:1, :], bn_down[1:2, :], count_b, False)
    prepare_corners(1 - par, False)
    run_layer(lambda i, u: build_wide(i, 1 - par, u), conv_wide, lambda i: z_copy(i).start())
    start_stats(par)
    wait_stats(par)
    set_constants(par, bn_b[0, 0:1, :], bn_b[0, 1:2, :], count_b, False)
    cst_out[...] = cst[...]
    for img in range(n_img):
        z_copy(img).wait()


def finish_kernel(z_ref, cst_ref, out_ref, z, y, in_sem, out_sem):
    n_img, n_rows = z.shape[:2]

    def fetch(img):
        return pltpu.make_async_copy(z_ref.at[img], z.at[img], in_sem.at[img])

    def copy(img):
        return pltpu.make_async_copy(y.at[img], out_ref.at[img], out_sem.at[img])

    for img in range(n_img):
        fetch(img).start()

    def step(img, carry):
        fetch(img).wait()
        for r in range(n_rows):
            y[img, r] = normalise(z[img, r], cst_ref).astype(BF16)
        copy(img).start()
        return carry

    lax.fori_loop(0, n_img, step, 0)
    for img in range(n_img):
        copy(img).wait()


def solution(mesh):
    n_sp, n_sp2 = mesh.shape["sp"], mesh.shape["sp2"]

    def per_device(x, w_a, bn_a, w_down, bn_down, w_b, bn_b):
        n_img, rows, cols, ch = x.shape
        pairs, half = cols // 2, rows // 2
        n_dev = n_sp * n_sp2
        dims = (n_img, rows, pairs, ch, n_sp2, n_sp)
        vmem = pltpu.VMEM
        dma = pltpu.SemaphoreType.DMA
        scratch = [
            vmem((n_img, rows, ch, cols), BF16),
            vmem(w_a.shape, BF16), vmem(w_down.shape, BF16), vmem(w_b.shape, BF16),
            vmem((n_img, rows, pairs, 128), F32),
            [vmem((4 * (half + 1), pairs, 128), BF16) for _ in range(UNROLL)],
            [vmem(((rows + 2) * (pairs + 2 * EDGE), 128), F32) for _ in range(UNROLL)],
            vmem((2, 1536, 128), BF16),
            vmem((128, 128), BF16),
            vmem((n_img, pairs, 128), BF16), vmem((n_img, pairs, 128), BF16),
            vmem((n_img, pairs, 128), BF16), vmem((n_img, pairs, 128), BF16),
            vmem((n_img, rows, 128), F32),
            vmem((n_img, rows, 128), F32),
            vmem((2, n_img, pairs, 128), F32),
            vmem((2, n_img, pairs, 128), F32),
            vmem((2, n_img, rows, 128), F32),
            vmem((2, n_img, rows, 128), F32),
            vmem((4, n_img, 128), F32),
            vmem((2, 4, n_img, 128), F32),
            vmem((4, n_img, 128), F32),
            vmem((2, n_dev, 2, 128), F32),
            vmem((2, 8, 256), F32),
            vmem((8, 128), F32),
            dma((n_img,)),
            dma((3,)),
            dma((n_img,)),
            dma((2,)), dma((2, 2)),
            dma((2,)), dma((2, 2)),
            dma((4,)), dma((2, 4)),
            dma((n_dev - 1,)), dma((2, n_dev)),
        ]
        in_vmem = pl.BlockSpec(memory_space=pltpu.VMEM)
        in_hbm = pl.BlockSpec(memory_space=pltpu.HBM)
        in_any = pl.BlockSpec(memory_space=pl.ANY)
        z, cst = pl.pallas_call(
            functools.partial(stack_kernel, dims),
            out_shape=(jax.ShapeDtypeStruct((n_img, half, pairs, 128), F32), jax.ShapeDtypeStruct((8, 128), F32)),
            in_specs=[in_hbm, in_hbm, in_vmem, in_hbm, in_vmem, in_hbm, in_vmem],
            out_specs=(in_any, in_vmem),
            scratch_shapes=scratch,
            compiler_params=pltpu.CompilerParams(collective_id=0, has_side_effects=True, vmem_limit_bytes=VMEM_LIMIT),
        )(jnp.transpose(x, (0, 1, 3, 2)), w_a, bn_a, w_down, bn_down, w_b, bn_b)
        return pl.pallas_call(
            finish_kernel,
            out_shape=jax.ShapeDtypeStruct((n_img, half, pairs, 128), BF16),
            in_specs=[in_any, in_vmem],
            out_specs=in_any,
            scratch_shapes=[vmem((n_img, half, pairs, 128), F32), vmem((n_img, half, pairs, 128), BF16), dma((n_img,)), dma((n_img,))],
            compiler_params=pltpu.CompilerParams(vmem_limit_bytes=VMEM_LIMIT),
        )(z, cst)

    tile_spec = P("dp", "sp", "sp2", None)
    return jax.shard_map(per_device, mesh=mesh, in_specs=(tile_spec, P(), P(), P(), P(), P(), P()), out_specs=tile_spec, check_vma=False)
```

time: 123 us -> 82.7 us (0.67)
  Pallas kernels: 115 us -> 82.5 us
  local copies, waits for them, and re-layouts: 7.49 us -> 0 us
    pallas_call x1, Pallas kernels: 109 us -> 78.3 us  [per_device(): pl.pallas_call(functools.partial(stack_kernel, dims), out_shape=(jax.Shap...]
    unnamed x16 -> x0, local copies, waits for them, and re-layouts: 7.49 us -> none
    pallas_call x1, Pallas kernels: 6.29 us -> 4.16 us  [per_device(): pl.pallas_call(finish_kernel, out_shape=jax.ShapeDtypeStruct((n_img, half...]
where the time goes in v3:
time: 82.7 us; the launch traced here: 82.5 us
  Pallas kernels  82.5 us (100%)
    pallas_call x1, Pallas kernels, per_device(): pl.pallas_call(functools.partial(stack_kernel, dims), out_shape=(jax.Shap...  78.3 us
    pallas_call x1, Pallas kernels, per_device(): pl.pallas_call(finish_kernel, out_shape=jax.ShapeDtypeStruct((n_img, half...  4.16 us

profile of v3, /device:TPU:0, one launch (start us, length us, event | category | flops | bytes accessed | tf_op | source)
XLA Modules:
  0.0 82.5 jit_solution(10195783738524669188)
XLA Ops:
  0.0 78.3 %shard_map.73 = (f32[16,8,64,128]{3,2,1,0:T(8,128)}, f32[8,128]{1,0:T(8,128)}) custom-call(bf16[16,16,64,128]{3,2,1,0:T(8,128)(2,1)} %bitcast.1, bf16[4,3,3,64,64]{4,3,2,1,0:T(8,128)(2,1)} %w_a_ref.1, f32[4,2,64]{2,1,0:T(2,128)} %bn_a.1, bf16[3,3,64,128]{3,2,1,0:T(8,128)(2,1)} %w_down_ref.1, f32[2,128]{1,0:T(2,128)} %bn_down.1, ...), custom_call_target="tpu_custom_call" | custom-call | tf_op jit(solution)/shard_map/pallas_call | solution.py:436
  78.3 4.2 %shard_map.74 = bf16[16,8,64,128]{3,2,1,0:T(8,128)(2,1)} custom-call(f32[16,8,64,128]{3,2,1,0:T(8,128)} %get-tuple-element.7.z_ref, f32[8,128]{1,0:T(8,128)} %get-tuple-element.8.cst_ref), custom_call_target="tpu_custom_call" | custom-call | tf_op jit(solution)/shard_map/pallas_call | solution.py:444

commit v4 on v3

v4 whole, which is shorter than its diff:
```python
import functools

import jax
import jax.numpy as jnp
from jax import lax
from jax.experimental import pallas as pl
from jax.experimental.pallas import tpu as pltpu
from jax.sharding import PartitionSpec as P

MESH = pl.DeviceIdType.MESH
F32 = jnp.float32
BF16 = jnp.bfloat16
EPS = 1e-5
UNROLL = 4
VMEM_LIMIT = 56 * 1024 * 1024
EDGE = 8


def normalise(v, cst):
    return jnp.maximum((v - cst[0:1, :]) * cst[1:2, :] + cst[2:3, :], 0.0)


def stack_kernel(dims, x_ref, w_a_ref, bn_a, w_down_ref, bn_down, w_b_ref, bn_b, z_out, cst_out,
                 xv, w_a, w_down, w_b, z, bufs, lines, wmat, perm, edge_u, edge_d, halo_u, halo_d,
                 mid_s, mid_r, end_s, end_r, corner_s, corner_r, corner_n, stats, acc, cst,
                 x_sem, w_sem, z_sem, row_send, row_recv, mid_send, mid_recv, end_send, end_recv, cor_send, cor_recv, st_send, st_recv):
    n_img, rows, pairs, ch, n_sp2, n_sp = dims
    half, quarter = rows // 2, rows // 4
    wide = pairs + 2 * EDGE
    n_dev = n_sp2 * n_sp
    n_steps = n_img // UNROLL
    sp = lax.axis_index("sp")
    sp2 = lax.axis_index("sp2")
    me = sp2 * n_sp + sp
    has_u, has_d = sp > 0, sp < n_sp - 1
    has_l, has_r = sp2 > 0, sp2 < n_sp2 - 1

    def x_copy(img):
        return pltpu.make_async_copy(x_ref.at[img], xv.at[img], x_sem.at[img])

    for img in range(n_img):
        x_copy(img).start()
    w_copies = [pltpu.make_async_copy(src, dst, w_sem.at[i]) for i, (src, dst) in enumerate(((w_a_ref, w_a), (w_down_ref, w_down), (w_b_ref, w_b)))]
    for copy in w_copies:
        copy.start()

    barrier = pltpu.get_barrier_semaphore()
    for d in range(1, n_dev):
        peer = lax.rem(me + d, n_dev)
        pl.semaphore_signal(barrier, inc=1, device_id={"sp2": peer // n_sp, "sp": lax.rem(peer, n_sp)}, device_id_type=MESH)

    def rcopy(src, dst, ssem, rsem, to_sp2, to_sp):
        return pltpu.make_async_remote_copy(src_ref=src, dst_ref=dst, send_sem=ssem, recv_sem=rsem,
                                            device_id={"sp2": to_sp2, "sp": to_sp}, device_id_type=MESH)

    def batch(t):
        return pl.ds(t * UNROLL, UNROLL)

    def start_rows(t):
        some = batch(t)

        @pl.when(has_u)
        def _():
            rcopy(edge_u.at[some], halo_d.at[some], row_send.at[0], row_recv.at[1], sp2, sp - 1).start()

        @pl.when(has_d)
        def _():
            rcopy(edge_d.at[some], halo_u.at[some], row_send.at[1], row_recv.at[0], sp2, sp + 1).start()

    def wait_rows():
        @pl.when(has_u)
        def _():
            rcopy(edge_u, halo_u, row_send.at[0], row_recv.at[0], sp2, sp).wait()

        @pl.when(has_d)
        def _():
            rcopy(edge_d, halo_d, row_send.at[1], row_recv.at[1], sp2, sp).wait()

    def start_columns(src, dst, ssem, rsem, t, par):
        some = batch(t)

        @pl.when(has_l)
        def _():
            rcopy(src.at[par, 0, some], dst.at[par, 1, some], ssem.at[par, 0], rsem.at[par, 1, t], sp2 - 1, sp).start()

        @pl.when(has_r)
        def _():
            rcopy(src.at[par, 1, some], dst.at[par, 0, some], ssem.at[par, 1], rsem.at[par, 0, t], sp2 + 1, sp).start()

    def wait_columns(t, par):
        some = batch(t)
        for side, there in ((0, has_l), (1, has_r)):
            @pl.when(there)
            def _():
                rcopy(mid_s.at[par, side, some], mid_r.at[par, side, some], mid_send.at[par, side], mid_recv.at[par, side, t], sp2, sp).wait_recv()
                rcopy(end_s.at[par, side, some], end_r.at[par, side, some], end_send.at[par, side], end_recv.at[par, side, t], sp2, sp).wait_recv()

    def wait_columns_sent(par):
        for side, there in ((0, has_l), (1, has_r)):
            @pl.when(there)
            def _():
                rcopy(mid_s.at[par, side], mid_r.at[par, side], mid_send.at[par, side], mid_recv.at[par, side, 0], sp2, sp).wait_send()
                rcopy(end_s.at[par, side], end_r.at[par, side], end_send.at[par, side], end_recv.at[par, side, 0], sp2, sp).wait_send()

    corner_to = ((has_u & has_l, -1, -1, 3), (has_u & has_r, 1, -1, 2), (has_d & has_l, -1, 1, 1), (has_d & has_r, 1, 1, 0))

    def start_corners(par):
        for c, (there, d_sp2, d_sp, slot) in enumerate(corner_to):
            @pl.when(there)
            def _():
                rcopy(corner_s.at[c], corner_r.at[par, slot], cor_send.at[c], cor_recv.at[par, slot], sp2 + d_sp2, sp + d_sp).start()

    def wait_corners(par):
        for c, (there, d_sp2, d_sp, slot) in enumerate(corner_to):
            @pl.when(there)
            def _():
                rcopy(corner_s.at[c], corner_r.at[par, c], cor_send.at[c], cor_recv.at[par, c], sp2, sp).wait()

    def stat_copy(d, par):
        peer = lax.rem(me + d, n_dev)
        return rcopy(stats.at[par, me], stats.at[par, me], st_send.at[d - 1], st_recv.at[par, me], peer // n_sp, lax.rem(peer, n_sp))

    def start_stats(par):
        total = acc[0] + acc[1]
        stats[par, me] = jnp.concatenate([jnp.sum(total[:, :128], axis=0, keepdims=True), jnp.sum(total[:, 128:], axis=0, keepdims=True)], axis=0)
        for d in range(1, n_dev):
            stat_copy(d, par).start()

    def wait_stats(par):
        for d in range(1, n_dev):
            stat_copy(d, par).wait_send()
            src = lax.rem(me + d, n_dev)
            rcopy(stats.at[par, src], stats.at[par, src], st_send.at[d - 1], st_recv.at[par, src], sp2, sp).wait_recv()

    def set_constants(par, gain, shift, count, paired):
        total = stats[par, 0]
        for src in range(1, n_dev):
            total = total + stats[par, src]
        if paired:
            total = total + pltpu.roll(total, ch, 1)
        mean = total[0:1] * (1.0 / count)
        var = total[1:2] * (1.0 / count) - mean * mean
        cst[0:1, :] = mean
        cst[1:2, :] = gain * lax.rsqrt(var + EPS)
        cst[2:3, :] = shift

    lane = lax.broadcasted_iota(jnp.int32, (pairs, 128), 1)

    def act(v, raw):
        return v if raw else normalise(v, cst)

    def column(img, side, first, count):
        flat = z.at[img].reshape(rows * pairs, 128)
        return flat[pl.ds(first * pairs + side * (pairs - 1), count, stride=pairs), :]

    def save_mid(img, n_rows, par):
        for side in range(2):
            mid_s[par, side, img, 0:n_rows - 4, :] = column(img, side, 2, n_rows - 4)

    def save_end(img, n_rows, par):
        here = pl.ds(img, 1)
        for side in range(2):
            top, bottom = column(img, side, 0, 2), column(img, side, n_rows - 2, 2)
            end_s[par, side, img, 0:2, :] = top
            end_s[par, side, img, 2:4, :] = bottom
            corner_s[side, here, :] = top[0:1]
            corner_s[2 + side, here, :] = bottom[1:2]

    def prepare_corners(par, raw):
        for c, (there, d_sp2, d_sp, slot) in enumerate(corner_to):
            corner_n[c] = jnp.where(there, act(corner_r[par, c], raw), 0.0)

    def line_place(p):
        return p * wide + EDGE

    def inner_lines(img, par, u, n_rows, raw):
        buf = lines[u]
        for side, there, off in ((0, has_l, -1), (1, has_r, pairs)):
            for src, at, count, r in ((end_r, 0, 2, 0), (mid_r, 0, n_rows - 4, 2), (end_r, 2, 2, n_rows - 2)):
                v = jnp.where(there, act(src[par, side, img, at:at + count, :], raw), 0.0)
                buf[pl.ds(line_place(r + 1) + off, count, stride=wide), :] = v
        for p in range(1, n_rows + 1):
            v = act(z[img, p - 1], raw)
            buf[line_place(p):line_place(p) + pairs, :] = v
            yield p, v

    def outer_lines(img, u, n_rows, which):
        buf = lines[u]
        here = pl.ds(img, 1)
        for side in which:
            p = side * (n_rows + 1)
            v = jnp.where((has_u, has_d)[side], (halo_u, halo_d)[side][img].astype(F32), 0.0)
            at = line_place(p)
            buf[at - 1:at, :] = corner_n[2 * side, here, :]
            buf[at + pairs:at + pairs + 1, :] = corner_n[2 * side + 1, here, :]
            buf[at:at + pairs, :] = v
            yield p, v

    def put_pairs(t, u, p, own):
        n_q, at = half + 1, line_place(p)
        side = jnp.where(lane < ch, lines[u][at + 1:at + 1 + pairs, :], lines[u][at - 1:at - 1 + pairs, :])
        bufs[u][t, 2 * (p % 2) * n_q + p // 2] = own.astype(BF16)
        bufs[u][t, (2 * (p % 2) + 1) * n_q + p // 2] = side.astype(BF16)

    def put_wide(t, u, p, own):
        n_q, at = quarter + 1, line_place(p)
        slot = 3 * (p % 2) * n_q + p // 2
        bufs[u][t, slot] = lines[u][at - 1:at - 1 + pairs, :].astype(BF16)
        bufs[u][t, slot + n_q] = own.astype(BF16)
        bufs[u][t, slot + 2 * n_q] = lines[u][at + 1:at + 1 + pairs, :].astype(BF16)

    def slots_pairs(i):
        return [c * (half + 1) + i + lo for lo in (0, 1) for c in range(4)]

    def slots_down(i):
        return [c * (half + 1) + 2 * i + k for k, c in ((0, 2), (0, 3), (1, 0), (1, 1), (1, 2), (1, 3), (2, 0), (2, 1), (2, 2), (2, 3))]

    def slots_wide(i):
        return [c * (quarter + 1) + i + lo for lo in (0, 1) for c in range(6)]

    def conv(t, blocks, slots):
        lhs = jnp.concatenate([jnp.concatenate([bufs[u][t, slots(i)[k]] for u, i in blocks], axis=0) for k in range(len(slots(0)))], axis=1)
        rhs = jnp.concatenate([wmat[0, 0:lhs.shape[1]], wmat[1, 0:lhs.shape[1]]], axis=1)
        o = jnp.dot(lhs, rhs, preferred_element_type=F32)
        folded = o.reshape(o.shape[0] // 8, 8, 256)
        s = jnp.sum(folded, axis=0)
        q = jnp.sum(folded * folded, axis=0)
        acc[0] += jnp.concatenate([s[:, :128], q[:, :128]], axis=1)
        acc[1] += jnp.concatenate([s[:, 128:], q[:, 128:]], axis=1)
        for n, (u, i) in enumerate(blocks):
            z[t * UNROLL + u, 2 * i] = o[n * pairs:(n + 1) * pairs, :128]
            z[t * UNROLL + u, 2 * i + 1] = o[n * pairs:(n + 1) * pairs, 128:]

    def run_layer(par, raw, n_rows, put, slots, inner, outer, sides, join, n_out, par_out):
        acc[...] = jnp.zeros_like(acc)
        if not raw:
            def send_rows(t, carry):
                for u in range(UNROLL):
                    img = t * UNROLL + u
                    edge_u[img] = act(z[img, 0], raw).astype(BF16)
                    edge_d[img] = act(z[img, n_rows - 1], raw).astype(BF16)
                start_rows(t)
                return carry

            lax.fori_loop(0, n_steps, send_rows, 0)

        def groups(size):
            return [range(u, u + size) for u in range(0, UNROLL, size)]

        def first_pass(t, carry):
            wait_columns(t, par)
            for us in groups(join[0]):
                for u in us:
                    for p, own in inner_lines(t * UNROLL + u, par, u, n_rows, raw):
                        put(t, u, p, own)
                conv(t, [(u, i) for u in us for i in inner], slots)
            if n_out:
                for u in range(UNROLL):
                    save_mid(t * UNROLL + u, n_out, par_out)
                start_columns(mid_s, mid_r, mid_send, mid_recv, t, par_out)
            return carry

        lax.fori_loop(0, n_steps, first_pass, 0)
        wait_corners(par)
        prepare_corners(par, raw)
        wait_rows()

        def second_pass(t, carry):
            for us in groups(join[1]):
                for u in us:
                    for p, own in outer_lines(t * UNROLL + u, u, n_rows, sides):
                        put(t, u, p, own)
                conv(t, [(u, i) for u in us for i in outer], slots)
            if n_out:
                for u in range(UNROLL):
                    save_end(t * UNROLL + u, n_out, par_out)
                start_columns(end_s, end_r, end_send, end_recv, t, par_out)
            else:
                for u in range(UNROLL):
                    z_copy(t * UNROLL + u).start()
            return carry

        lax.fori_loop(0, n_steps, second_pass, 0)
        start_stats(par_out)
        if n_out:
            start_corners(par_out)

    def z_copy(img):
        return pltpu.make_async_copy(z.at[img, pl.ds(0, half)], z_out.at[img], z_sem.at[img])

    def put_block(k, n_k, blocks):
        for o, blk in enumerate(blocks):
            wmat[o, k * n_k:(k + 1) * n_k, :] = jnp.zeros((n_k, 128), BF16) if blk is None else blk

    def weights_pairs(layer):
        zero = jnp.zeros((ch, ch), BF16)
        q = []
        for kh in range(3):
            w0, w1, w2 = w_a[layer, kh, 0], w_a[layer, kh, 1], w_a[layer, kh, 2]
            q.append(jnp.concatenate([
                jnp.concatenate([w1, w0], axis=1),
                jnp.concatenate([w2, w1], axis=1),
                jnp.concatenate([zero, w2], axis=1),
                jnp.concatenate([w0, zero], axis=1)], axis=0))
        for k in range(4):
            put_block(k, 256, [q[k] if k < 3 else None, q[k - 1] if k > 0 else None])

    def weights_down():
        d = [jnp.concatenate([w_down[kh, 0], w_down[kh, 1], w_down[kh, 2], jnp.zeros((ch, 128), BF16)], axis=0) for kh in range(3)]
        for k in range(5):
            put_block(k, 256, [d[k] if k < 3 else None, d[k - 2] if k >= 2 else None])

    def weights_wide():
        e = [jnp.concatenate([w_b[0, kh, 0], w_b[0, kh, 1], w_b[0, kh, 2]], axis=0) for kh in range(3)]
        for k in range(4):
            put_block(k, 384, [e[k] if k < 3 else None, e[k - 1] if k > 0 else None])

    wrow = lax.broadcasted_iota(jnp.int32, (128, 128), 0)
    wcol = lax.broadcasted_iota(jnp.int32, (128, 128), 1)
    source = jnp.where(wrow < pairs, 2 * wrow, 2 * (wrow - pairs) + 1)
    perm[...] = jnp.where(source == wcol, 1.0, 0.0).astype(BF16)

    def load_images(t, carry):
        images = [t * UNROLL + u for u in range(UNROLL)]
        for img in images:
            x_copy(img).wait()
        for img in images:
            for g in range(rows // 4):
                block = xv[img, 4 * g:4 * g + 4].reshape(4 * ch, 128)
                m = lax.dot_general(perm[...], block, (((1,), (1,)), ((), ())), preferred_element_type=F32)
                for b in range(2):
                    even = m[0:pairs, 128 * b:128 * b + 128]
                    odd = m[pairs:2 * pairs, 128 * b:128 * b + 128]
                    r = 4 * g + 2 * b
                    upper = jnp.where(lane < ch, even, pltpu.roll(odd, ch, 1))
                    lower = jnp.where(lane < ch, pltpu.roll(even, ch, 1), odd)
                    z[img, r] = upper
                    z[img, r + 1] = lower
                    if r == 0:
                        edge_u[img] = upper.astype(BF16)
                    if r + 2 == rows:
                        edge_d[img] = lower.astype(BF16)
            save_mid(img, rows, 0)
            save_end(img, rows, 0)

        @pl.when(t == 0)
        def _():
            pl.semaphore_wait(barrier, n_dev - 1)

        start_columns(mid_s, mid_r, mid_send, mid_recv, t, 0)
        start_columns(end_s, end_r, end_send, end_recv, t, 0)
        start_rows(t)
        return carry

    lax.fori_loop(0, n_steps, load_images, 0)
    start_corners(0)

    count_a = float(n_dev * n_img * rows * pairs * 2)
    count_b = float(n_dev * n_img * half * pairs)
    a_inner, a_outer = range(1, half - 1), (0, half - 1)

    for copy in w_copies:
        copy.wait()
    weights_pairs(0)
    run_layer(0, True, rows, put_pairs, slots_pairs, a_inner, a_outer, (0, 1), (1, 2), rows, 1)

    def gains(layer):
        g, s = bn_a[layer, 0:1, :], bn_a[layer, 1:2, :]
        return jnp.concatenate([g, g], axis=1), jnp.concatenate([s, s], axis=1)

    n_layers = w_a.shape[0]

    def a_layer(layer, carry):
        par = lax.rem(layer, 2)
        weights_pairs(layer)
        wait_columns_sent(1 - par)
        wait_stats(par)
        g, s = gains(layer - 1)
        set_constants(par, g, s, count_a, True)
        run_layer(par, False, rows, put_pairs, slots_pairs, a_inner, a_outer, (0, 1), (1, 2), rows, 1 - par)
        return carry

    lax.fori_loop(1, n_layers, a_layer, 0)

    par = n_layers % 2
    weights_down()
    wait_columns_sent(1 - par)
    wait_stats(par)
    g, s = gains(n_layers - 1)
    set_constants(par, g, s, count_a, True)
    run_layer(par, False, rows, put_pairs, slots_down, range(quarter - 1), (quarter - 1,), (1,), (1, 2), half, 1 - par)

    weights_wide()
    wait_columns_sent(par)
    wait_columns_sent(1 - par)
    wait_stats(1 - par)
    set_constants(1 - par, bn_down[0:1, :], bn_down[1:2, :], count_b, False)
    run_layer(1 - par, False, half, put_wide, slots_wide, range(1, quarter - 1), (0, quarter - 1), (0, 1), (2, 2), 0, par)
    wait_stats(par)
    set_constants(par, bn_b[0, 0:1, :], bn_b[0, 1:2, :], count_b, False)
    cst_out[...] = cst[...]
    for img in range(n_img):
        z_copy(img).wait()


def finish_kernel(z_ref, cst_ref, out_ref, z, y, in_sem, out_sem):
    n_img, n_rows = z.shape[:2]

    def fetch(img):
        return pltpu.make_async_copy(z_ref.at[img], z.at[img], in_sem.at[img])

    def copy(img):
        return pltpu.make_async_copy(y.at[img], out_ref.at[img], out_sem.at[img])

    for img in range(n_img):
        fetch(img).start()

    def step(img, carry):
        fetch(img).wait()
        for r in range(n_rows):
            y[img, r] = normalise(z[img, r], cst_ref).astype(BF16)
        copy(img).start()
        return carry

    lax.fori_loop(0, n_img, step, 0)
    for img in range(n_img):
        copy(img).wait()


def solution(mesh):
    n_sp, n_sp2 = mesh.shape["sp"], mesh.shape["sp2"]

    def per_device(x, w_a, bn_a, w_down, bn_down, w_b, bn_b):
        n_img, rows, cols, ch = x.shape
        pairs, half = cols // 2, rows // 2
        n_dev = n_sp * n_sp2
        dims = (n_img, rows, pairs, ch, n_sp2, n_sp)
        vmem = pltpu.VMEM
        dma = pltpu.SemaphoreType.DMA
        scratch = [
            vmem((n_img, rows, ch, cols), BF16),
            vmem(w_a.shape, BF16), vmem(w_down.shape, BF16), vmem(w_b.shape, BF16),
            vmem((n_img, rows, pairs, 128), F32),
            [vmem((n_img // UNROLL, 4 * (half + 1), pairs, 128), BF16) for _ in range(UNROLL)],
            [vmem(((rows + 2) * (pairs + 2 * EDGE), 128), F32) for _ in range(UNROLL)],
            vmem((2, 1536, 128), BF16),
            vmem((128, 128), BF16),
            vmem((n_img, pairs, 128), BF16), vmem((n_img, pairs, 128), BF16),
            vmem((n_img, pairs, 128), BF16), vmem((n_img, pairs, 128), BF16),
            vmem((2, 2, n_img, rows - 4, 128), F32), vmem((2, 2, n_img, rows - 4, 128), F32),
            vmem((2, 2, n_img, 4, 128), F32), vmem((2, 2, n_img, 4, 128), F32),
            vmem((4, n_img, 128), F32),
            vmem((2, 4, n_img, 128), F32),
            vmem((4, n_img, 128), F32),
            vmem((2, n_dev, 2, 128), F32),
            vmem((2, 8, 256), F32),
            vmem((8, 128), F32),
            dma((n_img,)),
            dma((3,)),
            dma((n_img,)),
            dma((2,)), dma((2,)),
            dma((2, 2)), dma((2, 2, n_img // UNROLL)),
            dma((2, 2)), dma((2, 2, n_img // UNROLL)),
            dma((4,)), dma((2, 4)),
            dma((n_dev - 1,)), dma((2, n_dev)),
        ]
        in_vmem = pl.BlockSpec(memory_space=pltpu.VMEM)
        in_hbm = pl.BlockSpec(memory_space=pltpu.HBM)
        in_any = pl.BlockSpec(memory_space=pl.ANY)
        z, cst = pl.pallas_call(
            functools.partial(stack_kernel, dims),
            out_shape=(jax.ShapeDtypeStruct((n_img, half, pairs, 128), F32), jax.ShapeDtypeStruct((8, 128), F32)),
            in_specs=[in_hbm, in_hbm, in_vmem, in_hbm, in_vmem, in_hbm, in_vmem],
            out_specs=(in_any, in_vmem),
            scratch_shapes=scratch,
            compiler_params=pltpu.CompilerParams(collective_id=0, has_side_effects=True, vmem_limit_bytes=VMEM_LIMIT),
        )(jnp.transpose(x, (0, 1, 3, 2)), w_a, bn_a, w_down, bn_down, w_b, bn_b)
        return pl.pallas_call(
            finish_kernel,
            out_shape=jax.ShapeDtypeStruct((n_img, half, pairs, 128), BF16),
            in_specs=[in_any, in_vmem],
            out_specs=in_any,
            scratch_shapes=[vmem((n_img, half, pairs, 128), F32), vmem((n_img, half, pairs, 128), BF16), dma((n_img,)), dma((n_img,))],
            compiler_params=pltpu.CompilerParams(vmem_limit_bytes=VMEM_LIMIT),
        )(z, cst)

    tile_spec = P("dp", "sp", "sp2", None)
    return jax.shard_map(per_device, mesh=mesh, in_specs=(tile_spec, P(), P(), P(), P(), P(), P()), out_specs=tile_spec, check_vma=False)
```

time: 82.7 us -> 83.9 us (1.015)
  Pallas kernels: 82.5 us -> 83.7 us
    pallas_call x1, Pallas kernels: 78.3 us -> 79.6 us  [per_device(): pl.pallas_call(functools.partial(stack_kernel, dims), out_shape=(jax.Shap...]
where the time goes in v4:
time: 83.9 us; the launch traced here: 83.7 us
  Pallas kernels  83.7 us (100%)
    pallas_call x1, Pallas kernels, per_device(): pl.pallas_call(functools.partial(stack_kernel, dims), out_shape=(jax.Shap...  79.6 us
    pallas_call x1, Pallas kernels, per_device(): pl.pallas_call(finish_kernel, out_shape=jax.ShapeDtypeStruct((n_img, half...  4.16 us

profile of v4, /device:TPU:0, one launch (start us, length us, event | category | flops | bytes accessed | tf_op | source)
XLA Modules:
  0.0 83.7 jit_solution(10893743617770453481)
XLA Ops:
  0.0 79.6 %shard_map.73 = (f32[16,8,64,128]{3,2,1,0:T(8,128)}, f32[8,128]{1,0:T(8,128)}) custom-call(bf16[16,16,64,128]{3,2,1,0:T(8,128)(2,1)} %bitcast.1, bf16[4,3,3,64,64]{4,3,2,1,0:T(8,128)(2,1)} %w_a_ref.1, f32[4,2,64]{2,1,0:T(2,128)} %bn_a.1, bf16[3,3,64,128]{3,2,1,0:T(8,128)(2,1)} %w_down_ref.1, f32[2,128]{1,0:T(2,128)} %bn_down.1, ...), custom_call_target="tpu_custom_call" | custom-call | tf_op jit(solution)/shard_map/pallas_call | solution.py:470
  79.6 4.2 %shard_map.74 = bf16[16,8,64,128]{3,2,1,0:T(8,128)(2,1)} custom-call(f32[16,8,64,128]{3,2,1,0:T(8,128)} %get-tuple-element.7.z_ref, f32[8,128]{1,0:T(8,128)} %get-tuple-element.8.cst_ref), custom_call_target="tpu_custom_call" | custom-call | tf_op jit(solution)/shard_map/pallas_call | solution.py:478

commit v5 on v3

--- a/solution.py
+++ b/solution.py
@@ -13,7 +13,7 @@
 EPS = 1e-5
 UNROLL = 4
 SPLIT = 1
-VMEM_LIMIT = 56 * 1024 * 1024
+VMEM_LIMIT = 51 * 1024 * 1024
 EDGE = 8
 
 
@@ -24,7 +24,7 @@
 def stack_kernel(dims, x_ref, w_a_ref, bn_a, w_down_ref, bn_down, w_b_ref, bn_b, z_out, cst_out,
                  xv, w_a, w_down, w_b, z, bufs, lines, wmat, perm, edge_u, edge_d, first_u, first_d, edge_l, edge_r, halo_u, halo_d, halo_l, halo_r,
                  corner_s, corner_r, corner_n, stats, acc, cst,
-                 x_sem, w_sem, z_sem, row_send, row_recv, col_send, col_recv, cor_send, cor_recv, st_send, st_recv):
+                 x_sem, w_sem, row_send, row_recv, col_send, col_recv, cor_send, cor_recv, st_send, st_recv):
     n_img, rows, pairs, ch, n_sp2, n_sp = dims
     half, quarter = rows // 2, rows // 4
     wide = pairs + 2 * EDGE
@@ -35,11 +35,12 @@
     has_u, has_d = sp > 0, sp < n_sp - 1
     has_l, has_r = sp2 > 0, sp2 < n_sp2 - 1
 
-    def x_copy(img):
-        return pltpu.make_async_copy(x_ref.at[img], xv.at[img], x_sem.at[img])
-
-    for img in range(n_img):
-        x_copy(img).start()
+    def x_copy(t):
+        some = pl.ds(t * UNROLL, UNROLL)
+        return pltpu.make_async_copy(x_ref.at[some], xv.at[some], x_sem.at[t])
+
+    for t in range(n_img // UNROLL):
+        x_copy(t).start()
 
     w_copies = [pltpu.make_async_copy(src, dst, w_sem.at[i]) for i, (src, dst) in enumerate(((w_a_ref, w_a), (w_down_ref, w_down), (w_b_ref, w_b)))]
     for copy in w_copies:
@@ -54,26 +55,26 @@
         return pltpu.make_async_remote_copy(src_ref=src, dst_ref=dst, send_sem=ssem, recv_sem=rsem,
                                             device_id={"sp2": to_sp2, "sp": to_sp}, device_id_type=MESH)
 
-    def start_edges(img, par, n_rows, first=False):
-        r_all = pl.ds(0, n_rows)
+    def start_edges(t, par, n_rows, first=False):
+        some, r_all = pl.ds(t * UNROLL, UNROLL), pl.ds(0, n_rows)
 
         @pl.when(has_u)
         def _():
-            src, dst = (edge_u.at[img], first_d.at[img]) if first else (z.at[img, 0], halo_d.at[par, img])
+            src, dst = (edge_u.at[some], first_d.at[some]) if first else (z.at[some, 0], halo_d.at[par, some])
             rcopy(src, dst, row_send.at[0], row_recv.at[par, 1], sp2, sp - 1).start()
 
         @pl.when(has_d)
         def _():
-            src, dst = (edge_d.at[img], first_u.at[img]) if first else (z.at[img, n_rows - 1], halo_u.at[par, img])
+            src, dst = (edge_d.at[some], first_u.at[some]) if first else (z.at[some, n_rows - 1], halo_u.at[par, some])
             rcopy(src, dst, row_send.at[1], row_recv.at[par, 0], sp2, sp + 1).start()
 
         @pl.when(has_l)
         def _():
-            rcopy(edge_l.at[img, r_all], halo_r.at[par, img, r_all], col_send.at[0], col_recv.at[par, 1], sp2 - 1, sp).start()
+            rcopy(edge_l.at[some, r_all], halo_r.at[par, some, r_all], col_send.at[0], col_recv.at[par, 1], sp2 - 1, sp).start()
 
         @pl.when(has_r)
         def _():
-            rcopy(edge_r.at[img, r_all], halo_l.at[par, img, r_all], col_send.at[1], col_recv.at[par, 0], sp2 + 1, sp).start()
+            rcopy(edge_r.at[some, r_all], halo_l.at[par, some, r_all], col_send.at[1], col_recv.at[par, 0], sp2 + 1, sp).start()
 
     corner_to = ((has_u & has_l, -1, -1, 3), (has_u & has_r, 1, -1, 2), (has_d & has_l, -1, 1, 1), (has_d & has_r, 1, 1, 0))
 
@@ -199,15 +200,15 @@
             bufs[u][at + n_q] = own.astype(BF16)
             bufs[u][at + 2 * n_q] = lines[u][base + 1:base + 1 + pairs, :].astype(BF16)
 
-    def finish_conv(img, i0, o):
+    def finish_conv(img, i0, o, dst=z):
         folded = o.reshape(o.shape[0] // 8, 8, 256)
         s = jnp.sum(folded, axis=0)
         q = jnp.sum(folded * folded, axis=0)
         acc[0] += jnp.concatenate([s[:, :128], q[:, :128]], axis=1)
         acc[1] += jnp.concatenate([s[:, 128:], q[:, 128:]], axis=1)
         for i in range(o.shape[0] // pairs):
-            z[img, 2 * (i0 + i)] = o[i * pairs:(i + 1) * pairs, :128]
-            z[img, 2 * (i0 + i) + 1] = o[i * pairs:(i + 1) * pairs, 128:]
+            dst[img, 2 * (i0 + i)] = o[i * pairs:(i + 1) * pairs, :128]
+            dst[img, 2 * (i0 + i) + 1] = o[i * pairs:(i + 1) * pairs, 128:]
 
     def dot(parts):
         lhs = jnp.concatenate(parts, axis=1)
@@ -230,7 +231,7 @@
     def conv_wide(img, u):
         n_q = quarter + 1
         at = [c * n_q + lo for lo in (0, 1) for c in range(6)]
-        finish_conv(img, 0, dot([bufs[u][k:k + quarter].reshape(quarter * pairs, 128) for k in at]))
+        finish_conv(img, 0, dot([bufs[u][k:k + quarter].reshape(quarter * pairs, 128) for k in at]), z_out)
 
     def run_layer(build, conv, done):
         acc[...] = jnp.zeros_like(acc)
@@ -239,14 +240,10 @@
             for u in range(UNROLL):
                 build(t * UNROLL + u, u)
                 conv(t * UNROLL + u, u)
-            for u in range(UNROLL):
-                done(t * UNROLL + u)
+            done(t)
             return carry
 
         lax.fori_loop(0, n_img // UNROLL, body, 0)
-
-    def z_copy(img):
-        return pltpu.make_async_copy(z.at[img, pl.ds(0, half)], z_out.at[img], z_sem.at[img])
 
     def put_block(k, n_k, blocks):
         for o, blk in enumerate(blocks):
@@ -279,11 +276,9 @@
     wcol = lax.broadcasted_iota(jnp.int32, (128, 128), 1)
     source = jnp.where(wrow < pairs, 2 * wrow, 2 * (wrow - pairs) + 1)
     perm[...] = jnp.where(source == wcol, 1.0, 0.0).astype(BF16)
-    pl.semaphore_wait(barrier, n_dev - 1)
 
     def load_images(t, carry):
-        for img in [t * UNROLL + u for u in range(UNROLL)]:
-            x_copy(img).wait()
+        x_copy(t).wait()
         for img in [t * UNROLL + u for u in range(UNROLL)]:
             for g in range(rows // 4):
                 block = xv[img, 4 * g:4 * g + 4].reshape(4 * ch, 128)
@@ -301,8 +296,12 @@
                     if r + 2 == rows:
                         edge_d[img] = lower.astype(BF16)
             save_edges(img, rows)
-        for img in [t * UNROLL + u for u in range(UNROLL)]:
-            start_edges(img, 0, rows, True)
+
+        @pl.when(t == 0)
+        def _():
+            pl.semaphore_wait(barrier, n_dev - 1)
+
+        start_edges(t, 0, rows, True)
         return carry
 
     lax.fori_loop(0, n_img // UNROLL, load_images, 0)
@@ -316,7 +315,7 @@
     weights_pairs(0)
     wait_edges(0, rows, True)
     prepare_corners(0, True)
-    run_layer(lambda i, u: build_pairs(i, 0, u, True), conv_pairs, lambda i: start_edges(i, 1, rows))
+    run_layer(lambda i, u: build_pairs(i, 0, u, True), conv_pairs, lambda t: start_edges(t, 1, rows))
     start_stats(1)
     start_corners(1)
 
@@ -334,7 +333,7 @@
         g, s = gains(layer - 1)
         set_constants(par, g, s, count_a, True)
         prepare_corners(par, False)
-        run_layer(lambda i, u: build_pairs(i, par, u, False), conv_pairs, lambda i: start_edges(i, 1 - par, rows))
+        run_layer(lambda i, u: build_pairs(i, par, u, False), conv_pairs, lambda t: start_edges(t, 1 - par, rows))
         start_stats(1 - par)
         start_corners(1 - par)
         return carry
@@ -348,7 +347,7 @@
     g, s = gains(n_layers - 1)
     set_constants(par, g, s, count_a, True)
     prepare_corners(par, False)
-    run_layer(lambda i, u: build_pairs(i, par, u, False, 1), conv_down, lambda i: start_edges(i, 1 - par, half))
+    run_layer(lambda i, u: build_pairs(i, par, u, False, 1), conv_down, lambda t: start_edges(t, 1 - par, half))
     start_stats(1 - par)
     start_corners(1 - par)
 
@@ -357,29 +356,20 @@
     wait_stats(1 - par)
     set_constants(1 - par, bn_down[0:1, :], bn_down[1:2, :], count_b, False)
     prepare_corners(1 - par, False)
-    run_layer(lambda i, u: build_wide(i, 1 - par, u), conv_wide, lambda i: z_copy(i).start())
+    run_layer(lambda i, u: build_wide(i, 1 - par, u), conv_wide, lambda t: None)
     start_stats(par)
     wait_stats(par)
     set_constants(par, bn_b[0, 0:1, :], bn_b[0, 1:2, :], count_b, False)
     cst_out[...] = cst[...]
-    for img in range(n_img):
-        z_copy(img).wait()
-
-
-def finish_kernel(z_ref, cst_ref, out_ref, z, y, in_sem, out_sem):
+
+
+def finish_kernel(z, cst_ref, out_ref, y, out_sem):
     n_img, n_rows = z.shape[:2]
-
-    def fetch(img):
-        return pltpu.make_async_copy(z_ref.at[img], z.at[img], in_sem.at[img])
 
     def copy(img):
         return pltpu.make_async_copy(y.at[img], out_ref.at[img], out_sem.at[img])
 
-    for img in range(n_img):
-        fetch(img).start()
-
     def step(img, carry):
-        fetch(img).wait()
         for r in range(n_rows):
             y[img, r] = normalise(z[img, r], cst_ref).astype(BF16)
         copy(img).start()
@@ -422,9 +412,8 @@
             vmem((2, n_dev, 2, 128), F32),
             vmem((2, 8, 256), F32),
             vmem((8, 128), F32),
-            dma((n_img,)),
+            dma((n_img // UNROLL,)),
             dma((3,)),
-            dma((n_img,)),
             dma((2,)), dma((2, 2)),
             dma((2,)), dma((2, 2)),
             dma((4,)), dma((2, 4)),
@@ -435,19 +424,19 @@
         in_any = pl.BlockSpec(memory_space=pl.ANY)
         z, cst = pl.pallas_call(
             functools.partial(stack_kernel, dims),
-            out_shape=(jax.ShapeDtypeStruct((n_img, half, pairs, 128), F32), jax.ShapeDtypeStruct((8, 128), F32)),
+            out_shape=(vmem((n_img, half, pairs, 128), F32), jax.ShapeDtypeStruct((8, 128), F32)),
             in_specs=[in_hbm, in_hbm, in_vmem, in_hbm, in_vmem, in_hbm, in_vmem],
-            out_specs=(in_any, in_vmem),
+            out_specs=(in_vmem, in_vmem),
             scratch_shapes=scratch,
             compiler_params=pltpu.CompilerParams(collective_id=0, has_side_effects=True, vmem_limit_bytes=VMEM_LIMIT),
         )(jnp.transpose(x, (0, 1, 3, 2)), w_a, bn_a, w_down, bn_down, w_b, bn_b)
         return pl.pallas_call(
             finish_kernel,
             out_shape=jax.ShapeDtypeStruct((n_img, half, pairs, 128), BF16),
-            in_specs=[in_any, in_vmem],
+            in_specs=[in_vmem, in_vmem],
             out_specs=in_any,
-            scratch_shapes=[vmem((n_img, half, pairs, 128), F32), vmem((n_img, half, pairs, 128), BF16), dma((n_img,)), dma((n_img,))],
-            compiler_params=pltpu.CompilerParams(vmem_limit_bytes=VMEM_LIMIT),
+            scratch_shapes=[vmem((n_img, half, pairs, 128), BF16), dma((n_img,))],
+            compiler_params=pltpu.CompilerParams(vmem_limit_bytes=16 * 1024 * 1024),
         )(z, cst)
 
     tile_spec = P("dp", "sp", "sp2", None)

time: 82.7 us -> 78.4 us (0.948)
  Pallas kernels: 82.5 us -> 77.5 us
    pallas_call x1, Pallas kernels: 4.16 us -> 1.49 us  [per_device(): pl.pallas_call(finish_kernel, out_shape=jax.ShapeDtypeStruct((n_img, half...]
    pallas_call x1, Pallas kernels: 78.3 us -> 76 us  [per_device(): pl.pallas_call(functools.partial(stack_kernel, dims), out_shape=(vmem((n_...]
where the time goes in v5:
time: 78.4 us; the launch traced here: 78.2 us
  Pallas kernels  77.5 us (99%)
    pallas_call x1, Pallas kernels, per_device(): pl.pallas_call(functools.partial(stack_kernel, dims), out_shape=(vmem((n_...  76 us

profile of v5, /device:TPU:0, one launch (start us, length us, event | category | flops | bytes accessed | tf_op | source)
XLA Modules:
  0.0 78.2 jit_solution(1382498036000337527)
XLA Ops:
  0.0 76.0 %shard_map.73 = (f32[16,8,64,128]{3,2,1,0:T(8,128)S(1)}, f32[8,128]{1,0:T(8,128)}) custom-call(bf16[16,16,64,128]{3,2,1,0:T(8,128)(2,1)} %bitcast.1, bf16[4,3,3,64,64]{4,3,2,1,0:T(8,128)(2,1)} %w_a_ref.1, f32[4,2,64]{2,1,0:T(2,128)} %bn_a.1, bf16[3,3,64,128]{3,2,1,0:T(8,128)(2,1)} %w_down_ref.1, f32[2,128]{1,0:T(2,128)} %bn_down.1, ...), custom_call_target="tpu_custom_call" | custom-call | tf_op jit(solution)/shard_map/pallas_call | solution.py:425
  76.0 0.0 copy-start
  76.1 0.7 copy-done
  76.7 1.5 %shard_map.74 = bf16[16,8,64,128]{3,2,1,0:T(8,128)(2,1)} custom-call(f32[16,8,64,128]{3,2,1,0:T(8,128)S(1)} %get-tuple-element.7.z, f32[8,128]{1,0:T(8,128)S(1)} %copy-done), custom_call_target="tpu_custom_call" | custom-call | tf_op jit(solution)/shard_map/pallas_call | solution.py:433
Async XLA Ops:
  76.0 0.7 copy-start

commit v6 on v5

--- a/solution.py
+++ b/solution.py
@@ -55,61 +55,86 @@
         return pltpu.make_async_remote_copy(src_ref=src, dst_ref=dst, send_sem=ssem, recv_sem=rsem,
                                             device_id={"sp2": to_sp2, "sp": to_sp}, device_id_type=MESH)
 
+    corner_to = ((has_u & has_l, -1, -1, 3), (has_u & has_r, 1, -1, 2), (has_d & has_l, -1, 1, 1), (has_d & has_r, 1, 1, 0))
+
     def start_edges(t, par, n_rows, first=False):
         some, r_all = pl.ds(t * UNROLL, UNROLL), pl.ds(0, n_rows)
 
-        @pl.when(has_u)
-        def _():
-            src, dst = (edge_u.at[some], first_d.at[some]) if first else (z.at[some, 0], halo_d.at[par, some])
-            rcopy(src, dst, row_send.at[0], row_recv.at[par, 1], sp2, sp - 1).start()
-
-        @pl.when(has_d)
-        def _():
-            src, dst = (edge_d.at[some], first_u.at[some]) if first else (z.at[some, n_rows - 1], halo_u.at[par, some])
-            rcopy(src, dst, row_send.at[1], row_recv.at[par, 0], sp2, sp + 1).start()
-
         @pl.when(has_l)
         def _():
-            rcopy(edge_l.at[some, r_all], halo_r.at[par, some, r_all], col_send.at[0], col_recv.at[par, 1], sp2 - 1, sp).start()
+            rcopy(edge_l.at[some, r_all], halo_r.at[par, some, r_all], col_send.at[0], col_recv.at[par, 1, t], sp2 - 1, sp).start()
 
         @pl.when(has_r)
         def _():
-            rcopy(edge_r.at[some, r_all], halo_l.at[par, some, r_all], col_send.at[1], col_recv.at[par, 0], sp2 + 1, sp).start()
-
-    corner_to = ((has_u & has_l, -1, -1, 3), (has_u & has_r, 1, -1, 2), (has_d & has_l, -1, 1, 1), (has_d & has_r, 1, 1, 0))
-
-    def start_corners(par):
+            rcopy(edge_r.at[some, r_all], halo_l.at[par, some, r_all], col_send.at[1], col_recv.at[par, 0, t], sp2 + 1, sp).start()
+
         for c, (there, d_sp2, d_sp, slot) in enumerate(corner_to):
             @pl.when(there)
             def _():
-                rcopy(corner_s.at[c], corner_r.at[par, slot], cor_send.at[c], cor_recv.at[par, slot], sp2 + d_sp2, sp + d_sp).start()
-
-    def wait_edges(par, n_rows, first=False):
-        r_all = pl.ds(0, n_rows)
-        every = pl.ds(0, n_img)
+                rcopy(corner_s.at[c, t], corner_r.at[par, slot, t], cor_send.at[c], cor_recv.at[par, slot, t], sp2 + d_sp2, sp + d_sp).start()
 
         @pl.when(has_u)
         def _():
-            src, dst = (edge_u, first_u) if first else (z.at[every, 0], halo_u.at[par])
-            rcopy(src, dst, row_send.at[0], row_recv.at[par, 0], sp2, sp).wait()
+            src, dst = (edge_u.at[some], first_d.at[some]) if first else (z.at[some, 0], halo_d.at[par, some])
+            rcopy(src, dst, row_send.at[0], row_recv.at[par, 1, t], sp2, sp - 1).start()
 
         @pl.when(has_d)
         def _():
-            src, dst = (edge_d, first_d) if first else (z.at[every, n_rows - 1], halo_d.at[par])
-            rcopy(src, dst, row_send.at[1], row_recv.at[par, 1], sp2, sp).wait()
+            src, dst = (edge_d.at[some], first_u.at[some]) if first else (z.at[some, n_rows - 1], halo_u.at[par, some])
+            rcopy(src, dst, row_send.at[1], row_recv.at[par, 0, t], sp2, sp + 1).start()
+
+    def wait_edges(t, par, n_rows, first=False):
+        some, r_all = pl.ds(t * UNROLL, UNROLL), pl.ds(0, n_rows)
+
+        @pl.when(has_u)
+        def _():
+            src, dst = (edge_u.at[some], first_u.at[some]) if first else (z.at[some, 0], halo_u.at[par, some])
+            rcopy(src, dst, row_send.at[0], row_recv.at[par, 0, t], sp2, sp).wait_recv()
+
+        @pl.when(has_d)
+        def _():
+            src, dst = (edge_d.at[some], first_d.at[some]) if first else (z.at[some, n_rows - 1], halo_d.at[par, some])
+            rcopy(src, dst, row_send.at[1], row_recv.at[par, 1, t], sp2, sp).wait_recv()
 
         @pl.when(has_l)
         def _():
-            rcopy(edge_l.at[every, r_all], halo_l.at[par, every, r_all], col_send.at[0], col_recv.at[par, 0], sp2, sp).wait()
+            rcopy(edge_l.at[some, r_all], halo_l.at[par, some, r_all], col_send.at[0], col_recv.at[par, 0, t], sp2, sp).wait_recv()
 
         @pl.when(has_r)
         def _():
-            rcopy(edge_r.at[every, r_all], halo_r.at[par, every, r_all], col_send.at[1], col_recv.at[par, 1], sp2, sp).wait()
+            rcopy(edge_r.at[some, r_all], halo_r.at[par, some, r_all], col_send.at[1], col_recv.at[par, 1, t], sp2, sp).wait_recv()
 
         for c, (there, d_sp2, d_sp, slot) in enumerate(corner_to):
             @pl.when(there)
             def _():
-                rcopy(corner_s.at[c], corner_r.at[par, c], cor_send.at[c], cor_recv.at[par, c], sp2, sp).wait()
+                rcopy(corner_s.at[c, t], corner_r.at[par, c, t], cor_send.at[c], cor_recv.at[par, c, t], sp2, sp).wait_recv()
+
+    def wait_edges_sent(n_rows, first=False):
+        r_all = pl.ds(0, n_rows)
+        every = pl.ds(0, n_img)
+
+        @pl.when(has_u)
+        def _():
+            src, dst = (edge_u, first_u) if first else (z.at[every, 0], halo_u.at[0])
+            rcopy(src, dst, row_send.at[0], row_recv.at[0, 0, 0], sp2, sp).wait_send()
+
+        @pl.when(has_d)
+        def _():
+            src, dst = (edge_d, first_d) if first else (z.at[every, n_rows - 1], halo_d.at[0])
+            rcopy(src, dst, row_send.at[1], row_recv.at[0, 1, 0], sp2, sp).wait_send()
+
+        @pl.when(has_l)
+        def _():
+            rcopy(edge_l.at[every, r_all], halo_l.at[0, every, r_all], col_send.at[0], col_recv.at[0, 0, 0], sp2, sp).wait_send()
+
+        @pl.when(has_r)
+        def _():
+            rcopy(edge_r.at[every, r_all], halo_r.at[0, every, r_all], col_send.at[1], col_recv.at[0, 1, 0], sp2, sp).wait_send()
+
+        for c, (there, d_sp2, d_sp, slot) in enumerate(corner_to):
+            @pl.when(there)
+            def _():
+                rcopy(corner_s.at[c], corner_r.at[0, c], cor_send.at[c], cor_recv.at[0, c, 0], sp2, sp).wait_send()
 
     def stat_copy(d, par):
         peer = lax.rem(me + d, n_dev)
@@ -141,37 +166,36 @@
 
     lane = lax.broadcasted_iota(jnp.int32, (pairs, 128), 1)
 
-    def save_edges(img, n_rows):
+    def save_edges(t, u, n_rows):
+        img = t * UNROLL + u
         flat = z.at[img].reshape(rows * pairs, 128)
         first = flat[pl.ds(0, n_rows, stride=pairs), :]
         final = flat[pl.ds(pairs - 1, n_rows, stride=pairs), :]
         edge_l[img, 0:n_rows, :] = first
         edge_r[img, 0:n_rows, :] = final
-        here = pl.ds(img, 1)
-        corner_s[0, here, :] = first[0:1]
-        corner_s[1, here, :] = final[0:1]
-        corner_s[2, here, :] = first[n_rows - 1:n_rows]
-        corner_s[3, here, :] = final[n_rows - 1:n_rows]
+        corner_s[0, t, u:u + 1, :] = first[0:1]
+        corner_s[1, t, u:u + 1, :] = final[0:1]
+        corner_s[2, t, u:u + 1, :] = first[n_rows - 1:n_rows]
+        corner_s[3, t, u:u + 1, :] = final[n_rows - 1:n_rows]
 
     def act(v, raw):
         return v if raw else normalise(v, cst)
 
-    def prepare_corners(par, raw):
+    def prepare_corners(t, par, raw):
         for c, (there, d_sp2, d_sp, slot) in enumerate(corner_to):
-            corner_n[c] = jnp.where(there, act(corner_r[par, c], raw), 0.0)
-
-    def fill_lines(img, par, u, n_rows, raw, first_p):
-        buf = lines[u]
+            corner_n[c] = jnp.where(there, act(corner_r[par, c, t], raw), 0.0)
+
+    def fill_lines(t, par, u, n_rows, raw, first_p):
+        buf, img = lines[u], t * UNROLL + u
         left = jnp.where(has_l, act(halo_l[par, img, 0:n_rows, :], raw), 0.0)
         right = jnp.where(has_r, act(halo_r[par, img, 0:n_rows, :], raw), 0.0)
         buf[pl.ds(wide + EDGE - 1, n_rows, stride=wide), :] = left
         buf[pl.ds(wide + EDGE + pairs, n_rows, stride=wide), :] = right
-        here = pl.ds(img, 1)
         bottom = (n_rows + 1) * wide
-        buf[EDGE - 1:EDGE, :] = corner_n[0, here, :]
-        buf[EDGE + pairs:EDGE + pairs + 1, :] = corner_n[1, here, :]
-        buf[bottom + EDGE - 1:bottom + EDGE, :] = corner_n[2, here, :]
-        buf[bottom + EDGE + pairs:bottom + EDGE + pairs + 1, :] = corner_n[3, here, :]
+        buf[EDGE - 1:EDGE, :] = corner_n[0, u:u + 1, :]
+        buf[EDGE + pairs:EDGE + pairs + 1, :] = corner_n[1, u:u + 1, :]
+        buf[bottom + EDGE - 1:bottom + EDGE, :] = corner_n[2, u:u + 1, :]
+        buf[bottom + EDGE + pairs:bottom + EDGE + pairs + 1, :] = corner_n[3, u:u + 1, :]
         out = []
         for p in range(first_p, n_rows + 2):
             if p == 0:
@@ -185,16 +209,16 @@
             out.append((p, base, v))
         return out
 
-    def build_pairs(img, par, u, raw, first_p=0):
+    def build_pairs(t, par, u, raw, first_p=0):
         n_q = half + 1
-        for p, base, own in fill_lines(img, par, u, rows, raw, first_p):
+        for p, base, own in fill_lines(t, par, u, rows, raw, first_p):
             side = jnp.where(lane < ch, lines[u][base + 1:base + 1 + pairs, :], lines[u][base - 1:base - 1 + pairs, :])
             bufs[u][2 * (p % 2) * n_q + p // 2] = own.astype(BF16)
             bufs[u][(2 * (p % 2) + 1) * n_q + p // 2] = side.astype(BF16)
 
-    def build_wide(img, par, u):
+    def build_wide(t, par, u):
         n_q = quarter + 1
-        for p, base, own in fill_lines(img, par, u, half, False, 0):
+        for p, base, own in fill_lines(t, par, u, half, False, 0):
             at = 3 * (p % 2) * n_q + p // 2
             bufs[u][at] = lines[u][base - 1:base - 1 + pairs, :].astype(BF16)
             bufs[u][at + n_q] = own.astype(BF16)
@@ -215,35 +239,45 @@
         rhs = jnp.concatenate([wmat[0, 0:lhs.shape[1]], wmat[1, 0:lhs.shape[1]]], axis=1)
         return jnp.dot(lhs, rhs, preferred_element_type=F32)
 
-    def conv_pairs(img, u):
+    def conv_pairs(t, u):
         n_q, n_i = half + 1, half // SPLIT
         for i0 in range(0, half, n_i):
             at = [c * n_q + i0 + lo for lo in (0, 1) for c in range(4)]
-            finish_conv(img, i0, dot([bufs[u][k:k + n_i].reshape(n_i * pairs, 128) for k in at]))
-        save_edges(img, rows)
-
-    def conv_down(img, u):
+            finish_conv(t * UNROLL + u, i0, dot([bufs[u][k:k + n_i].reshape(n_i * pairs, 128) for k in at]))
+        save_edges(t, u, rows)
+
+    def conv_down(t, u):
         n_q = half + 1
         at = [c * n_q + k for k, c in ((0, 2), (0, 3), (1, 0), (1, 1), (1, 2), (1, 3), (2, 0), (2, 1), (2, 2), (2, 3))]
-        finish_conv(img, 0, dot([jnp.concatenate([bufs[u][k + 2 * i] for i in range(quarter)], axis=0) for k in at]))
-        save_edges(img, half)
-
-    def conv_wide(img, u):
+        finish_conv(t * UNROLL + u, 0, dot([jnp.concatenate([bufs[u][k + 2 * i] for i in range(quarter)], axis=0) for k in at]))
+        save_edges(t, u, half)
+
+    def conv_wide(t, u):
         n_q = quarter + 1
         at = [c * n_q + lo for lo in (0, 1) for c in range(6)]
-        finish_conv(img, 0, dot([bufs[u][k:k + quarter].reshape(quarter * pairs, 128) for k in at]), z_out)
-
-    def run_layer(build, conv, done):
+        finish_conv(t * UNROLL + u, 0, dot([bufs[u][k:k + quarter].reshape(quarter * pairs, 128) for k in at]), z_out)
+
+    n_steps = n_img // UNROLL
+
+    def run_layer(par, raw, n_rows, build, conv, n_out, par_out):
         acc[...] = jnp.zeros_like(acc)
 
         def body(t, carry):
+            wait_edges(t, par, n_rows, raw)
+            prepare_corners(t, par, raw)
             for u in range(UNROLL):
-                build(t * UNROLL + u, u)
-                conv(t * UNROLL + u, u)
-            done(t)
+                build(t, u)
+                conv(t, u)
+            if n_out:
+                @pl.when(t < n_steps - 1)
+                def _():
+                    start_edges(t, par_out, n_out)
             return carry
 
-        lax.fori_loop(0, n_img // UNROLL, body, 0)
+        lax.fori_loop(0, n_steps, body, 0)
+        start_stats(par_out)
+        if n_out:
+            start_edges(n_steps - 1, par_out, n_out)
 
     def put_block(k, n_k, blocks):
         for o, blk in enumerate(blocks):
@@ -279,7 +313,8 @@
 
     def load_images(t, carry):
         x_copy(t).wait()
-        for img in [t * UNROLL + u for u in range(UNROLL)]:
+        for img_u in range(UNROLL):
+            img = t * UNROLL + img_u
             for g in range(rows // 4):
                 block = xv[img, 4 * g:4 * g + 4].reshape(4 * ch, 128)
                 m = lax.dot_general(perm[...], block, (((1,), (1,)), ((), ())), preferred_element_type=F32)
@@ -295,7 +330,7 @@
                         edge_u[img] = upper.astype(BF16)
                     if r + 2 == rows:
                         edge_d[img] = lower.astype(BF16)
-            save_edges(img, rows)
+            save_edges(t, img_u, rows)
 
         @pl.when(t == 0)
         def _():
@@ -304,8 +339,7 @@
         start_edges(t, 0, rows, True)
         return carry
 
-    lax.fori_loop(0, n_img // UNROLL, load_images, 0)
-    start_corners(0)
+    lax.fori_loop(0, n_steps, load_images, 0)
 
     count_a = float(n_dev * n_img * rows * pairs * 2)
     count_b = float(n_dev * n_img * half * pairs)
@@ -313,11 +347,8 @@
     for copy in w_copies:
         copy.wait()
     weights_pairs(0)
-    wait_edges(0, rows, True)
-    prepare_corners(0, True)
-    run_layer(lambda i, u: build_pairs(i, 0, u, True), conv_pairs, lambda t: start_edges(t, 1, rows))
-    start_stats(1)
-    start_corners(1)
+    wait_edges_sent(rows, True)
+    run_layer(0, True, rows, lambda t, u: build_pairs(t, 0, u, True), conv_pairs, rows, 1)
 
     def gains(layer):
         g, s = bn_a[layer, 0:1, :], bn_a[layer, 1:2, :]
@@ -328,36 +359,28 @@
     def a_layer(layer, carry):
         par = lax.rem(layer, 2)
         weights_pairs(layer)
-        wait_edges(par, rows)
+        wait_edges_sent(rows)
         wait_stats(par)
         g, s = gains(layer - 1)
         set_constants(par, g, s, count_a, True)
-        prepare_corners(par, False)
-        run_layer(lambda i, u: build_pairs(i, par, u, False), conv_pairs, lambda t: start_edges(t, 1 - par, rows))
-        start_stats(1 - par)
-        start_corners(1 - par)
+        run_layer(par, False, rows, lambda t, u: build_pairs(t, par, u, False), conv_pairs, rows, 1 - par)
         return carry
 
     lax.fori_loop(1, n_layers, a_layer, 0)
 
     par = n_layers % 2
     weights_down()
-    wait_edges(par, rows)
+    wait_edges_sent(rows)
     wait_stats(par)
     g, s = gains(n_layers - 1)
     set_constants(par, g, s, count_a, True)
-    prepare_corners(par, False)
-    run_layer(lambda i, u: build_pairs(i, par, u, False, 1), conv_down, lambda t: start_edges(t, 1 - par, half))
-    start_stats(1 - par)
-    start_corners(1 - par)
+    run_layer(par, False, rows, lambda t, u: build_pairs(t, par, u, False, 1), conv_down, half, 1 - par)
 
     weights_wide()
-    wait_edges(1 - par, half)
+    wait_edges_sent(half)
     wait_stats(1 - par)
     set_constants(1 - par, bn_down[0:1, :], bn_down[1:2, :], count_b, False)
-    prepare_corners(1 - par, False)
-    run_layer(lambda i, u: build_wide(i, 1 - par, u), conv_wide, lambda t: None)
-    start_stats(par)
+    run_layer(1 - par, False, half, lambda t, u: build_wide(t, 1 - par, u), conv_wide, 0, par)
     wait_stats(par)
     set_constants(par, bn_b[0, 0:1, :], bn_b[0, 1:2, :], count_b, False)
     cst_out[...] = cst[...]
@@ -406,17 +429,17 @@
             vmem((2, n_img, pairs, 128), F32),
             vmem((2, n_img, rows, 128), F32),
             vmem((2, n_img, rows, 128), F32),
-            vmem((4, n_img, 128), F32),
-            vmem((2, 4, n_img, 128), F32),
-            vmem((4, n_img, 128), F32),
+            vmem((4, n_img // UNROLL, UNROLL, 128), F32),
+            vmem((2, 4, n_img // UNROLL, UNROLL, 128), F32),
+            vmem((4, UNROLL, 128), F32),
             vmem((2, n_dev, 2, 128), F32),
             vmem((2, 8, 256), F32),
             vmem((8, 128), F32),
             dma((n_img // UNROLL,)),
             dma((3,)),
-            dma((2,)), dma((2, 2)),
-            dma((2,)), dma((2, 2)),
-            dma((4,)), dma((2, 4)),
+            dma((2,)), dma((2, 2, n_img // UNROLL)),
+            dma((2,)), dma((2, 2, n_img // UNROLL)),
+            dma((4,)), dma((2, 4, n_img // UNROLL)),
             dma((n_dev - 1,)), dma((2, n_dev)),
         ]
         in_vmem = pl.BlockSpec(memory_space=pltpu.VMEM)
@@ -424,7 +447,7 @@
         in_any = pl.BlockSpec(memory_space=pl.ANY)
         z, cst = pl.pallas_call(
             functools.partial(stack_kernel, dims),
-            out_shape=(vmem((n_img, half, pairs, 128), F32), jax.ShapeDtypeStruct((8, 128), F32)),
+            out_shape=(vmem((n_img, half, pairs, 128), F32), vmem((8, 128), F32)),
             in_specs=[in_hbm, in_hbm, in_vmem, in_hbm, in_vmem, in_hbm, in_vmem],
             out_specs=(in_vmem, in_vmem),
             scratch_shapes=scratch,

time: 78.4 us -> 75.3 us (0.960)
  Pallas kernels: 77.5 us -> 75.1 us
    pallas_call x1, Pallas kernels: 76 us -> 73.6 us  [per_device(): pl.pallas_call(functools.partial(stack_kernel, dims), out_shape=(vmem((n_...]
where the time goes in v6:
time: 75.3 us; the launch traced here: 75.1 us
  Pallas kernels  75.1 us (100%)
    pallas_call x1, Pallas kernels, per_device(): pl.pallas_call(functools.partial(stack_kernel, dims), out_shape=(vmem((n_...  73.6 us

profile of v6, /device:TPU:0, one launch (start us, length us, event | category | flops | bytes accessed | tf_op | source)
XLA Modules:
  0.0 75.1 jit_solution(18245024645945189445)
XLA Ops:
  0.0 73.6 %shard_map.73 = (f32[16,8,64,128]{3,2,1,0:T(8,128)S(1)}, f32[8,128]{1,0:T(8,128)S(1)}) custom-call(bf16[16,16,64,128]{3,2,1,0:T(8,128)(2,1)} %bitcast.1, bf16[4,3,3,64,64]{4,3,2,1,0:T(8,128)(2,1)} %w_a_ref.1, f32[4,2,64]{2,1,0:T(2,128)} %bn_a.1, bf16[3,3,64,128]{3,2,1,0:T(8,128)(2,1)} %w_down_ref.1, f32[2,128]{1,0:T(2,128)} %bn_down.1, ...), custom_call_target="tpu_custom_call" | custom-call | tf_op jit(solution)/shard_map/pallas_call | solution.py:448
  73.6 1.5 %shard_map.74 = bf16[16,8,64,128]{3,2,1,0:T(8,128)(2,1)} custom-call(f32[16,8,64,128]{3,2,1,0:T(8,128)S(1)} %get-tuple-element.7.z, f32[8,128]{1,0:T(8,128)S(1)} %get-tuple-element.8.cst_ref), custom_call_target="tpu_custom_call" | custom-call | tf_op jit(solution)/shard_map/pallas_call | solution.py:456

commit v7 on v6

--- a/solution.py
+++ b/solution.py
@@ -12,6 +12,7 @@
 BF16 = jnp.bfloat16
 EPS = 1e-5
 UNROLL = 4
+BATCHES = 2
 SPLIT = 1
 VMEM_LIMIT = 51 * 1024 * 1024
 EDGE = 8
@@ -62,26 +63,26 @@
 
         @pl.when(has_l)
         def _():
-            rcopy(edge_l.at[some, r_all], halo_r.at[par, some, r_all], col_send.at[0], col_recv.at[par, 1, t], sp2 - 1, sp).start()
+            rcopy(edge_l.at[par, some, r_all], halo_r.at[par, some, r_all], col_send.at[par, 0], col_recv.at[par, 1, t], sp2 - 1, sp).start()
 
         @pl.when(has_r)
         def _():
-            rcopy(edge_r.at[some, r_all], halo_l.at[par, some, r_all], col_send.at[1], col_recv.at[par, 0, t], sp2 + 1, sp).start()
+            rcopy(edge_r.at[par, some, r_all], halo_l.at[par, some, r_all], col_send.at[par, 1], col_recv.at[par, 0, t], sp2 + 1, sp).start()
 
         for c, (there, d_sp2, d_sp, slot) in enumerate(corner_to):
             @pl.when(there)
             def _():
-                rcopy(corner_s.at[c, t], corner_r.at[par, slot, t], cor_send.at[c], cor_recv.at[par, slot, t], sp2 + d_sp2, sp + d_sp).start()
+                rcopy(corner_s.at[par, c, t], corner_r.at[par, slot, t], cor_send.at[par, c], cor_recv.at[par, slot, t], sp2 + d_sp2, sp + d_sp).start()
 
         @pl.when(has_u)
         def _():
             src, dst = (edge_u.at[some], first_d.at[some]) if first else (z.at[some, 0], halo_d.at[par, some])
-            rcopy(src, dst, row_send.at[0], row_recv.at[par, 1, t], sp2, sp - 1).start()
+            rcopy(src, dst, row_send.at[par, 0], row_recv.at[par, 1, t], sp2, sp - 1).start()
 
         @pl.when(has_d)
         def _():
             src, dst = (edge_d.at[some], first_u.at[some]) if first else (z.at[some, n_rows - 1], halo_u.at[par, some])
-            rcopy(src, dst, row_send.at[1], row_recv.at[par, 0, t], sp2, sp + 1).start()
+            rcopy(src, dst, row_send.at[par, 1], row_recv.at[par, 0, t], sp2, sp + 1).start()
 
     def wait_edges(t, par, n_rows, first=False):
         some, r_all = pl.ds(t * UNROLL, UNROLL), pl.ds(0, n_rows)
@@ -89,52 +90,52 @@
         @pl.when(has_u)
         def _():
             src, dst = (edge_u.at[some], first_u.at[some]) if first else (z.at[some, 0], halo_u.at[par, some])
-            rcopy(src, dst, row_send.at[0], row_recv.at[par, 0, t], sp2, sp).wait_recv()
+            rcopy(src, dst, row_send.at[par, 0], row_recv.at[par, 0, t], sp2, sp).wait_recv()
 
         @pl.when(has_d)
         def _():
             src, dst = (edge_d.at[some], first_d.at[some]) if first else (z.at[some, n_rows - 1], halo_d.at[par, some])
-            rcopy(src, dst, row_send.at[1], row_recv.at[par, 1, t], sp2, sp).wait_recv()
+            rcopy(src, dst, row_send.at[par, 1], row_recv.at[par, 1, t], sp2, sp).wait_recv()
 
         @pl.when(has_l)
         def _():
-            rcopy(edge_l.at[some, r_all], halo_l.at[par, some, r_all], col_send.at[0], col_recv.at[par, 0, t], sp2, sp).wait_recv()
+            rcopy(edge_l.at[par, some, r_all], halo_l.at[par, some, r_all], col_send.at[par, 0], col_recv.at[par, 0, t], sp2, sp).wait_recv()
 
         @pl.when(has_r)
         def _():
-            rcopy(edge_r.at[some, r_all], halo_r.at[par, some, r_all], col_send.at[1], col_recv.at[par, 1, t], sp2, sp).wait_recv()
+            rcopy(edge_r.at[par, some, r_all], halo_r.at[par, some, r_all], col_send.at[par, 1], col_recv.at[par, 1, t], sp2, sp).wait_recv()
 
         for c, (there, d_sp2, d_sp, slot) in enumerate(corner_to):
             @pl.when(there)
             def _():
-                rcopy(corner_s.at[c, t], corner_r.at[par, c, t], cor_send.at[c], cor_recv.at[par, c, t], sp2, sp).wait_recv()
-
-    def wait_edges_sent(n_rows, first=False):
+                rcopy(corner_s.at[par, c, t], corner_r.at[par, c, t], cor_send.at[par, c], cor_recv.at[par, c, t], sp2, sp).wait_recv()
+
+    def wait_edges_sent(par, n_rows, first=False):
         r_all = pl.ds(0, n_rows)
         every = pl.ds(0, n_img)
 
         @pl.when(has_u)
         def _():
             src, dst = (edge_u, first_u) if first else (z.at[every, 0], halo_u.at[0])
-            rcopy(src, dst, row_send.at[0], row_recv.at[0, 0, 0], sp2, sp).wait_send()
+            rcopy(src, dst, row_send.at[par, 0], row_recv.at[0, 0, 0], sp2, sp).wait_send()
 
         @pl.when(has_d)
         def _():
             src, dst = (edge_d, first_d) if first else (z.at[every, n_rows - 1], halo_d.at[0])
-            rcopy(src, dst, row_send.at[1], row_recv.at[0, 1, 0], sp2, sp).wait_send()
+            rcopy(src, dst, row_send.at[par, 1], row_recv.at[0, 1, 0], sp2, sp).wait_send()
 
         @pl.when(has_l)
         def _():
-            rcopy(edge_l.at[every, r_all], halo_l.at[0, every, r_all], col_send.at[0], col_recv.at[0, 0, 0], sp2, sp).wait_send()
+            rcopy(edge_l.at[par, every, r_all], halo_l.at[0, every, r_all], col_send.at[par, 0], col_recv.at[0, 0, 0], sp2, sp).wait_send()
 
         @pl.when(has_r)
         def _():
-            rcopy(edge_r.at[every, r_all], halo_r.at[0, every, r_all], col_send.at[1], col_recv.at[0, 1, 0], sp2, sp).wait_send()
+            rcopy(edge_r.at[par, every, r_all], halo_r.at[0, every, r_all], col_send.at[par, 1], col_recv.at[0, 1, 0], sp2, sp).wait_send()
 
         for c, (there, d_sp2, d_sp, slot) in enumerate(corner_to):
             @pl.when(there)
             def _():
-                rcopy(corner_s.at[c], corner_r.at[0, c], cor_send.at[c], cor_recv.at[0, c, 0], sp2, sp).wait_send()
+                rcopy(corner_s.at[par, c], corner_r.at[0, c], cor_send.at[par, c], cor_recv.at[0, c, 0], sp2, sp).wait_send()
 
     def stat_copy(d, par):
         peer = lax.rem(me + d, n_dev)
@@ -166,36 +167,36 @@
 
     lane = lax.broadcasted_iota(jnp.int32, (pairs, 128), 1)
 
-    def save_edges(t, u, n_rows):
+    def save_edges(t, u, n_rows, par):
         img = t * UNROLL + u
         flat = z.at[img].reshape(rows * pairs, 128)
         first = flat[pl.ds(0, n_rows, stride=pairs), :]
         final = flat[pl.ds(pairs - 1, n_rows, stride=pairs), :]
-        edge_l[img, 0:n_rows, :] = first
-        edge_r[img, 0:n_rows, :] = final
-        corner_s[0, t, u:u + 1, :] = first[0:1]
-        corner_s[1, t, u:u + 1, :] = final[0:1]
-        corner_s[2, t, u:u + 1, :] = first[n_rows - 1:n_rows]
-        corner_s[3, t, u:u + 1, :] = final[n_rows - 1:n_rows]
+        edge_l[par, img, 0:n_rows, :] = first
+        edge_r[par, img, 0:n_rows, :] = final
+        corner_s[par, 0, t, u:u + 1, :] = first[0:1]
+        corner_s[par, 1, t, u:u + 1, :] = final[0:1]
+        corner_s[par, 2, t, u:u + 1, :] = first[n_rows - 1:n_rows]
+        corner_s[par, 3, t, u:u + 1, :] = final[n_rows - 1:n_rows]
 
     def act(v, raw):
         return v if raw else normalise(v, cst)
 
-    def prepare_corners(t, par, raw):
+    def prepare_corners(b, t, par, raw):
         for c, (there, d_sp2, d_sp, slot) in enumerate(corner_to):
-            corner_n[c] = jnp.where(there, act(corner_r[par, c, t], raw), 0.0)
-
-    def fill_lines(t, par, u, n_rows, raw, first_p):
-        buf, img = lines[u], t * UNROLL + u
+            corner_n[b, c] = jnp.where(there, act(corner_r[par, c, t], raw), 0.0)
+
+    def fill_lines(t, par, u, k, n_rows, raw, first_p):
+        buf, img, b = lines[k], t * UNROLL + u, k // UNROLL
         left = jnp.where(has_l, act(halo_l[par, img, 0:n_rows, :], raw), 0.0)
         right = jnp.where(has_r, act(halo_r[par, img, 0:n_rows, :], raw), 0.0)
         buf[pl.ds(wide + EDGE - 1, n_rows, stride=wide), :] = left
         buf[pl.ds(wide + EDGE + pairs, n_rows, stride=wide), :] = right
         bottom = (n_rows + 1) * wide
-        buf[EDGE - 1:EDGE, :] = corner_n[0, u:u + 1, :]
-        buf[EDGE + pairs:EDGE + pairs + 1, :] = corner_n[1, u:u + 1, :]
-        buf[bottom + EDGE - 1:bottom + EDGE, :] = corner_n[2, u:u + 1, :]
-        buf[bottom + EDGE + pairs:bottom + EDGE + pairs + 1, :] = corner_n[3, u:u + 1, :]
+        buf[EDGE - 1:EDGE, :] = corner_n[b, 0, u:u + 1, :]
+        buf[EDGE + pairs:EDGE + pairs + 1, :] = corner_n[b, 1, u:u + 1, :]
+        buf[bottom + EDGE - 1:bottom + EDGE, :] = corner_n[b, 2, u:u + 1, :]
+        buf[bottom + EDGE + pairs:bottom + EDGE + pairs + 1, :] = corner_n[b, 3, u:u + 1, :]
         out = []
         for p in range(first_p, n_rows + 2):
             if p == 0:
@@ -209,20 +210,20 @@
             out.append((p, base, v))
         return out
 
-    def build_pairs(t, par, u, raw, first_p=0):
+    def build_pairs(t, par, u, k, raw, first_p=0):
         n_q = half + 1
-        for p, base, own in fill_lines(t, par, u, rows, raw, first_p):
-            side = jnp.where(lane < ch, lines[u][base + 1:base + 1 + pairs, :], lines[u][base - 1:base - 1 + pairs, :])
-            bufs[u][2 * (p % 2) * n_q + p // 2] = own.astype(BF16)
-            bufs[u][(2 * (p % 2) + 1) * n_q + p // 2] = side.astype(BF16)
-
-    def build_wide(t, par, u):
+        for p, base, own in fill_lines(t, par, u, k, rows, raw, first_p):
+            side = jnp.where(lane < ch, lines[k][base + 1:base + 1 + pairs, :], lines[k][base - 1:base - 1 + pairs, :])
+            bufs[k][2 * (p % 2) * n_q + p // 2] = own.astype(BF16)
+            bufs[k][(2 * (p % 2) + 1) * n_q + p // 2] = side.astype(BF16)
+
+    def build_wide(t, par, u, k):
         n_q = quarter + 1
-        for p, base, own in fill_lines(t, par, u, half, False, 0):
+        for p, base, own in fill_lines(t, par, u, k, half, False, 0):
             at = 3 * (p % 2) * n_q + p // 2
-            bufs[u][at] = lines[u][base - 1:base - 1 + pairs, :].astype(BF16)
-            bufs[u][at + n_q] = own.astype(BF16)
-            bufs[u][at + 2 * n_q] = lines[u][base + 1:base + 1 + pairs, :].astype(BF16)
+            bufs[k][at] = lines[k][base - 1:base - 1 + pairs, :].astype(BF16)
+            bufs[k][at + n_q] = own.astype(BF16)
+            bufs[k][at + 2 * n_q] = lines[k][base + 1:base + 1 + pairs, :].astype(BF16)
 
     def finish_conv(img, i0, o, dst=z):
         folded = o.reshape(o.shape[0] // 8, 8, 256)
@@ -239,45 +240,52 @@
         rhs = jnp.concatenate([wmat[0, 0:lhs.shape[1]], wmat[1, 0:lhs.shape[1]]], axis=1)
         return jnp.dot(lhs, rhs, preferred_element_type=F32)
 
-    def conv_pairs(t, u):
+    def conv_pairs(t, u, k, par_out):
         n_q, n_i = half + 1, half // SPLIT
         for i0 in range(0, half, n_i):
             at = [c * n_q + i0 + lo for lo in (0, 1) for c in range(4)]
-            finish_conv(t * UNROLL + u, i0, dot([bufs[u][k:k + n_i].reshape(n_i * pairs, 128) for k in at]))
-        save_edges(t, u, rows)
-
-    def conv_down(t, u):
+            finish_conv(t * UNROLL + u, i0, dot([bufs[k][j:j + n_i].reshape(n_i * pairs, 128) for j in at]))
+        save_edges(t, u, rows, par_out)
+
+    def conv_down(t, u, k, par_out):
         n_q = half + 1
-        at = [c * n_q + k for k, c in ((0, 2), (0, 3), (1, 0), (1, 1), (1, 2), (1, 3), (2, 0), (2, 1), (2, 2), (2, 3))]
-        finish_conv(t * UNROLL + u, 0, dot([jnp.concatenate([bufs[u][k + 2 * i] for i in range(quarter)], axis=0) for k in at]))
-        save_edges(t, u, half)
-
-    def conv_wide(t, u):
+        at = [c * n_q + j for j, c in ((0, 2), (0, 3), (1, 0), (1, 1), (1, 2), (1, 3), (2, 0), (2, 1), (2, 2), (2, 3))]
+        finish_conv(t * UNROLL + u, 0, dot([jnp.concatenate([bufs[k][j + 2 * i] for i in range(quarter)], axis=0) for j in at]))
+        save_edges(t, u, half, par_out)
+
+    def conv_wide(t, u, k, par_out):
         n_q = quarter + 1
         at = [c * n_q + lo for lo in (0, 1) for c in range(6)]
-        finish_conv(t * UNROLL + u, 0, dot([bufs[u][k:k + quarter].reshape(quarter * pairs, 128) for k in at]), z_out)
+        finish_conv(t * UNROLL + u, 0, dot([bufs[k][j:j + quarter].reshape(quarter * pairs, 128) for j in at]), z_out)
 
     n_steps = n_img // UNROLL
 
-    def run_layer(par, raw, n_rows, build, conv, n_out, par_out):
+    n_steps = n_img // UNROLL
+
+    def run_layer(par, raw, n_rows, build, conv, n_out, par_out, batches=1):
         acc[...] = jnp.zeros_like(acc)
 
-        def body(t, carry):
-            wait_edges(t, par, n_rows, raw)
-            prepare_corners(t, par, raw)
-            for u in range(UNROLL):
-                build(t, u)
-                conv(t, u)
+        def body(step, carry):
+            steps = [step * batches + b for b in range(batches)]
+            for b, t in enumerate(steps):
+                wait_edges(t, par, n_rows, raw)
+                prepare_corners(b, t, par, raw)
+            for b, t in enumerate(steps):
+                for u in range(UNROLL):
+                    build(t, u, b * UNROLL + u)
+                    conv(t, u, b * UNROLL + u, par_out)
             if n_out:
-                @pl.when(t < n_steps - 1)
+                @pl.when(step < n_steps // batches - 1)
                 def _():
-                    start_edges(t, par_out, n_out)
+                    for t in steps:
+                        start_edges(t, par_out, n_out)
             return carry
 
-        lax.fori_loop(0, n_steps, body, 0)
+        lax.fori_loop(0, n_steps // batches, body, 0)
         start_stats(par_out)
         if n_out:
-            start_edges(n_steps - 1, par_out, n_out)
+            for b in range(batches):
+                start_edges(n_steps - batches + b, par_out, n_out)
 
     def put_block(k, n_k, blocks):
         for o, blk in enumerate(blocks):
@@ -330,7 +338,7 @@
                         edge_u[img] = upper.astype(BF16)
                     if r + 2 == rows:
                         edge_d[img] = lower.astype(BF16)
-            save_edges(t, img_u, rows)
+            save_edges(t, img_u, rows, 0)
 
         @pl.when(t == 0)
         def _():
@@ -347,8 +355,8 @@
     for copy in w_copies:
         copy.wait()
     weights_pairs(0)
-    wait_edges_sent(rows, True)
-    run_layer(0, True, rows, lambda t, u: build_pairs(t, 0, u, True), conv_pairs, rows, 1)
+    run_layer(0, True, rows, lambda t, u, k: build_pairs(t, 0, u, k, True), conv_pairs, rows, 1)
+    wait_edges_sent(0, rows, True)
 
     def gains(layer):
         g, s = bn_a[layer, 0:1, :], bn_a[layer, 1:2, :]
@@ -359,28 +367,28 @@
     def a_layer(layer, carry):
         par = lax.rem(layer, 2)
         weights_pairs(layer)
-        wait_edges_sent(rows)
+        wait_edges_sent(par, rows)
         wait_stats(par)
         g, s = gains(layer - 1)
         set_constants(par, g, s, count_a, True)
-        run_layer(par, False, rows, lambda t, u: build_pairs(t, par, u, False), conv_pairs, rows, 1 - par)
+        run_layer(par, False, rows, lambda t, u, k: build_pairs(t, par, u, k, False), conv_pairs, rows, 1 - par, BATCHES)
         return carry
 
     lax.fori_loop(1, n_layers, a_layer, 0)
 
     par = n_layers % 2
     weights_down()
-    wait_edges_sent(rows)
+    wait_edges_sent(par, rows)
     wait_stats(par)
     g, s = gains(n_layers - 1)
     set_constants(par, g, s, count_a, True)
-    run_layer(par, False, rows, lambda t, u: build_pairs(t, par, u, False, 1), conv_down, half, 1 - par)
+    run_layer(par, False, rows, lambda t, u, k: build_pairs(t, par, u, k, False, 1), conv_down, half, 1 - par)
 
     weights_wide()
-    wait_edges_sent(half)
+    wait_edges_sent(1 - par, half)
     wait_stats(1 - par)
     set_constants(1 - par, bn_down[0:1, :], bn_down[1:2, :], count_b, False)
-    run_layer(1 - par, False, half, lambda t, u: build_wide(t, 1 - par, u), conv_wide, 0, par)
+    run_layer(1 - par, False, half, lambda t, u, k: build_wide(t, 1 - par, u, k), conv_wide, 0, par)
     wait_stats(par)
     set_constants(par, bn_b[0, 0:1, :], bn_b[0, 1:2, :], count_b, False)
     cst_out[...] = cst[...]
@@ -417,29 +425,29 @@
             vmem((n_img, rows, ch, cols), BF16),
             vmem(w_a.shape, BF16), vmem(w_down.shape, BF16), vmem(w_b.shape, BF16),
             vmem((n_img, rows, pairs, 128), F32),
-            [vmem((4 * (half + 1), pairs, 128), BF16) for _ in range(UNROLL)],
-            [vmem(((rows + 2) * (pairs + 2 * EDGE), 128), F32) for _ in range(UNROLL)],
+            [vmem((4 * (half + 1), pairs, 128), BF16) for _ in range(BATCHES * UNROLL)],
+            [vmem(((rows + 2) * (pairs + 2 * EDGE), 128), F32) for _ in range(BATCHES * UNROLL)],
             vmem((2, 1536, 128), BF16),
             vmem((128, 128), BF16),
             vmem((n_img, pairs, 128), BF16), vmem((n_img, pairs, 128), BF16),
             vmem((n_img, pairs, 128), BF16), vmem((n_img, pairs, 128), BF16),
-            vmem((n_img, rows, 128), F32),
-            vmem((n_img, rows, 128), F32),
+            vmem((2, n_img, rows, 128), F32),
+            vmem((2, n_img, rows, 128), F32),
             vmem((2, n_img, pairs, 128), F32),
             vmem((2, n_img, pairs, 128), F32),
             vmem((2, n_img, rows, 128), F32),
             vmem((2, n_img, rows, 128), F32),
-            vmem((4, n_img // UNROLL, UNROLL, 128), F32),
             vmem((2, 4, n_img // UNROLL, UNROLL, 128), F32),
-            vmem((4, UNROLL, 128), F32),
+            vmem((2, 4, n_img // UNROLL, UNROLL, 128), F32),
+            vmem((2, 4, UNROLL, 128), F32),
             vmem((2, n_dev, 2, 128), F32),
             vmem((2, 8, 256), F32),
             vmem((8, 128), F32),
             dma((n_img // UNROLL,)),
             dma((3,)),
-            dma((2,)), dma((2, 2, n_img // UNROLL)),
-            dma((2,)), dma((2, 2, n_img // UNROLL)),
-            dma((4,)), dma((2, 4, n_img // UNROLL)),
+            dma((2, 2)), dma((2, 2, n_img // UNROLL)),
+            dma((2, 2)), dma((2, 2, n_img // UNROLL)),
+            dma((2, 4)), dma((2, 4, n_img // UNROLL)),
             dma((n_dev - 1,)), dma((2, n_dev)),
         ]
         in_vmem = pl.BlockSpec(memory_space=pltpu.VMEM)

time: 75.3 us -> 73.6 us (0.977)
  Pallas kernels: 75.1 us -> 73.4 us
    pallas_call x1, Pallas kernels: 73.6 us -> 71.9 us  [per_device(): pl.pallas_call(functools.partial(stack_kernel, dims), out_shape=(vmem((n_...]
where the time goes in v7:
time: 73.6 us; the launch traced here: 73.4 us
  Pallas kernels  73.4 us (100%)
    pallas_call x1, Pallas kernels, per_device(): pl.pallas_call(functools.partial(stack_kernel, dims), out_shape=(vmem((n_...  71.9 us
    pallas_call x1, Pallas kernels, per_device(): pl.pallas_call(finish_kernel, out_shape=jax.ShapeDtypeStruct((n_img, half...  1.5 us

profile of v7, /device:TPU:0, one launch (start us, length us, event | category | flops | bytes accessed | tf_op | source)
XLA Modules:
  0.0 73.4 jit_solution(8993158018945995935)
XLA Ops:
  0.0 71.9 %shard_map.73 = (f32[16,8,64,128]{3,2,1,0:T(8,128)S(1)}, f32[8,128]{1,0:T(8,128)S(1)}) custom-call(bf16[16,16,64,128]{3,2,1,0:T(8,128)(2,1)} %bitcast.1, bf16[4,3,3,64,64]{4,3,2,1,0:T(8,128)(2,1)} %w_a_ref.1, f32[4,2,64]{2,1,0:T(2,128)} %bn_a.1, bf16[3,3,64,128]{3,2,1,0:T(8,128)(2,1)} %w_down_ref.1, f32[2,128]{1,0:T(2,128)} %bn_down.1, ...), custom_call_target="tpu_custom_call" | custom-call | tf_op jit(solution)/shard_map/pallas_call | solution.py:456
  71.9 1.5 %shard_map.74 = bf16[16,8,64,128]{3,2,1,0:T(8,128)(2,1)} custom-call(f32[16,8,64,128]{3,2,1,0:T(8,128)S(1)} %get-tuple-element.7.z, f32[8,128]{1,0:T(8,128)S(1)} %get-tuple-element.8.cst_ref), custom_call_target="tpu_custom_call" | custom-call | tf_op jit(solution)/shard_map/pallas_call | solution.py:464

commit v8 on v7

--- a/solution.py
+++ b/solution.py
@@ -13,7 +13,7 @@
 EPS = 1e-5
 UNROLL = 4
 BATCHES = 2
-SPLIT = 1
+JOIN = 2
 VMEM_LIMIT = 51 * 1024 * 1024
 EDGE = 8
 
@@ -240,29 +240,32 @@
         rhs = jnp.concatenate([wmat[0, 0:lhs.shape[1]], wmat[1, 0:lhs.shape[1]]], axis=1)
         return jnp.dot(lhs, rhs, preferred_element_type=F32)
 
-    def conv_pairs(t, u, k, par_out):
-        n_q, n_i = half + 1, half // SPLIT
-        for i0 in range(0, half, n_i):
-            at = [c * n_q + i0 + lo for lo in (0, 1) for c in range(4)]
-            finish_conv(t * UNROLL + u, i0, dot([bufs[k][j:j + n_i].reshape(n_i * pairs, 128) for j in at]))
-        save_edges(t, u, rows, par_out)
-
-    def conv_down(t, u, k, par_out):
-        n_q = half + 1
-        at = [c * n_q + j for j, c in ((0, 2), (0, 3), (1, 0), (1, 1), (1, 2), (1, 3), (2, 0), (2, 1), (2, 2), (2, 3))]
-        finish_conv(t * UNROLL + u, 0, dot([jnp.concatenate([bufs[k][j + 2 * i] for i in range(quarter)], axis=0) for j in at]))
-        save_edges(t, u, half, par_out)
-
-    def conv_wide(t, u, k, par_out):
-        n_q = quarter + 1
-        at = [c * n_q + lo for lo in (0, 1) for c in range(6)]
-        finish_conv(t * UNROLL + u, 0, dot([bufs[k][j:j + quarter].reshape(quarter * pairs, 128) for j in at]), z_out)
+    def join(k, slots, size, n):
+        return [jnp.concatenate([block for a in range(n) for block in size(bufs[k + a], j)], axis=0) for j in slots]
+
+    def conv_pairs(t, u, k, par_out, n):
+        slots = [c * (half + 1) + lo for lo in (0, 1) for c in range(4)]
+        o = dot(join(k, slots, lambda buf, j: [buf[j:j + half].reshape(half * pairs, 128)], n))
+        for a in range(n):
+            finish_conv(t * UNROLL + u + a, 0, o[a * half * pairs:(a + 1) * half * pairs])
+            save_edges(t, u + a, rows, par_out)
+
+    def conv_down(t, u, k, par_out, n):
+        slots = [c * (half + 1) + j for j, c in ((0, 2), (0, 3), (1, 0), (1, 1), (1, 2), (1, 3), (2, 0), (2, 1), (2, 2), (2, 3))]
+        o = dot(join(k, slots, lambda buf, j: [buf[j + 2 * i] for i in range(quarter)], n))
+        for a in range(n):
+            finish_conv(t * UNROLL + u + a, 0, o[a * quarter * pairs:(a + 1) * quarter * pairs])
+            save_edges(t, u + a, half, par_out)
+
+    def conv_wide(t, u, k, par_out, n):
+        slots = [c * (quarter + 1) + lo for lo in (0, 1) for c in range(6)]
+        o = dot(join(k, slots, lambda buf, j: [buf[j:j + quarter].reshape(quarter * pairs, 128)], n))
+        for a in range(n):
+            finish_conv(t * UNROLL + u + a, 0, o[a * quarter * pairs:(a + 1) * quarter * pairs], z_out)
 
     n_steps = n_img // UNROLL
 
-    n_steps = n_img // UNROLL
-
-    def run_layer(par, raw, n_rows, build, conv, n_out, par_out, batches=1):
+    def run_layer(par, raw, n_rows, build, conv, n_out, par_out, n_join, batches=1):
         acc[...] = jnp.zeros_like(acc)
 
         def body(step, carry):
@@ -271,9 +274,10 @@
                 wait_edges(t, par, n_rows, raw)
                 prepare_corners(b, t, par, raw)
             for b, t in enumerate(steps):
-                for u in range(UNROLL):
-                    build(t, u, b * UNROLL + u)
-                    conv(t, u, b * UNROLL + u, par_out)
+                for u in range(0, UNROLL, n_join):
+                    for a in range(n_join):
+                        build(t, u + a, b * UNROLL + u + a)
+                    conv(t, u, b * UNROLL + u, par_out, n_join)
             if n_out:
                 @pl.when(step < n_steps // batches - 1)
                 def _():
@@ -355,7 +359,7 @@
     for copy in w_copies:
         copy.wait()
     weights_pairs(0)
-    run_layer(0, True, rows, lambda t, u, k: build_pairs(t, 0, u, k, True), conv_pairs, rows, 1)
+    run_layer(0, True, rows, lambda t, u, k: build_pairs(t, 0, u, k, True), conv_pairs, rows, 1, JOIN)
     wait_edges_sent(0, rows, True)
 
     def gains(layer):
@@ -371,7 +375,7 @@
         wait_stats(par)
         g, s = gains(layer - 1)
         set_constants(par, g, s, count_a, True)
-        run_layer(par, False, rows, lambda t, u, k: build_pairs(t, par, u, k, False), conv_pairs, rows, 1 - par, BATCHES)
+        run_layer(par, False, rows, lambda t, u, k: build_pairs(t, par, u, k, False), conv_pairs, rows, 1 - par, JOIN, BATCHES)
         return carry
 
     lax.fori_loop(1, n_layers, a_layer, 0)
@@ -382,13 +386,13 @@
     wait_stats(par)
     g, s = gains(n_layers - 1)
     set_constants(par, g, s, count_a, True)
-    run_layer(par, False, rows, lambda t, u, k: build_pairs(t, par, u, k, False, 1), conv_down, half, 1 - par)
+    run_layer(par, False, rows, lambda t, u, k: build_pairs(t, par, u, k, False, 1), conv_down, half, 1 - par, JOIN)
 
     weights_wide()
     wait_edges_sent(1 - par, half)
     wait_stats(1 - par)
     set_constants(1 - par, bn_down[0:1, :], bn_down[1:2, :], count_b, False)
-    run_layer(1 - par, False, half, lambda t, u, k: build_wide(t, 1 - par, u, k), conv_wide, 0, par)
+    run_layer(1 - par, False, half, lambda t, u, k: build_wide(t, 1 - par, u, k), conv_wide, 0, par, JOIN)
     wait_stats(par)
     set_constants(par, bn_b[0, 0:1, :], bn_b[0, 1:2, :], count_b, False)
     cst_out[...] = cst[...]

time: 73.6 us -> 72.6 us (0.986)
  Pallas kernels: 73.4 us -> 72.4 us
    pallas_call x1, Pallas kernels: 71.9 us -> 70.9 us  [per_device(): pl.pallas_call(functools.partial(stack_kernel, dims), out_shape=(vmem((n_...]
where the time goes in v8:
time: 72.6 us; the launch traced here: 72.4 us
  Pallas kernels  72.4 us (100%)
    pallas_call x1, Pallas kernels, per_device(): pl.pallas_call(functools.partial(stack_kernel, dims), out_shape=(vmem((n_...  70.9 us
    pallas_call x1, Pallas kernels, per_device(): pl.pallas_call(finish_kernel, out_shape=jax.ShapeDtypeStruct((n_img, half...  1.5 us

profile of v8, /device:TPU:0, one launch (start us, length us, event | category | flops | bytes accessed | tf_op | source)
XLA Modules:
  0.0 72.4 jit_solution(8390611388222902587)
XLA Ops:
  0.0 70.9 %shard_map.73 = (f32[16,8,64,128]{3,2,1,0:T(8,128)S(1)}, f32[8,128]{1,0:T(8,128)S(1)}) custom-call(bf16[16,16,64,128]{3,2,1,0:T(8,128)(2,1)} %bitcast.1, bf16[4,3,3,64,64]{4,3,2,1,0:T(8,128)(2,1)} %w_a_ref.1, f32[4,2,64]{2,1,0:T(2,128)} %bn_a.1, bf16[3,3,64,128]{3,2,1,0:T(8,128)(2,1)} %w_down_ref.1, f32[2,128]{1,0:T(2,128)} %bn_down.1, ...), custom_call_target="tpu_custom_call" | custom-call | tf_op jit(solution)/shard_map/pallas_call | solution.py:460
  70.9 1.5 %shard_map.74 = bf16[16,8,64,128]{3,2,1,0:T(8,128)(2,1)} custom-call(f32[16,8,64,128]{3,2,1,0:T(8,128)S(1)} %get-tuple-element.7.z, f32[8,128]{1,0:T(8,128)S(1)} %get-tuple-element.8.cst_ref), custom_call_target="tpu_custom_call" | custom-call | tf_op jit(solution)/shard_map/pallas_call | solution.py:468

commit v9 on v8

--- a/solution.py
+++ b/solution.py
@@ -13,7 +13,8 @@
 EPS = 1e-5
 UNROLL = 4
 BATCHES = 2
-JOIN = 2
+JOINS = (2, 2)
+LONG_JOINS = (1, 1, 2, 2, 2)
 VMEM_LIMIT = 51 * 1024 * 1024
 EDGE = 8
 
@@ -28,7 +29,8 @@
                  x_sem, w_sem, row_send, row_recv, col_send, col_recv, cor_send, cor_recv, st_send, st_recv):
     n_img, rows, pairs, ch, n_sp2, n_sp = dims
     half, quarter = rows // 2, rows // 4
-    wide = pairs + 2 * EDGE
+    wide = pairs + EDGE
+    data = pl.ds(0, pairs)
     n_dev = n_sp2 * n_sp
     sp = lax.axis_index("sp")
     sp2 = lax.axis_index("sp2")
@@ -76,12 +78,12 @@
 
         @pl.when(has_u)
         def _():
-            src, dst = (edge_u.at[some], first_d.at[some]) if first else (z.at[some, 0], halo_d.at[par, some])
+            src, dst = (edge_u.at[some], first_d.at[some]) if first else (z.at[some, 0, data], halo_d.at[par, some])
             rcopy(src, dst, row_send.at[par, 0], row_recv.at[par, 1, t], sp2, sp - 1).start()
 
         @pl.when(has_d)
         def _():
-            src, dst = (edge_d.at[some], first_u.at[some]) if first else (z.at[some, n_rows - 1], halo_u.at[par, some])
+            src, dst = (edge_d.at[some], first_u.at[some]) if first else (z.at[some, n_rows - 1, data], halo_u.at[par, some])
             rcopy(src, dst, row_send.at[par, 1], row_recv.at[par, 0, t], sp2, sp + 1).start()
 
     def wait_edges(t, par, n_rows, first=False):
@@ -89,12 +91,12 @@
 
         @pl.when(has_u)
         def _():
-            src, dst = (edge_u.at[some], first_u.at[some]) if first else (z.at[some, 0], halo_u.at[par, some])
+            src, dst = (edge_u.at[some], first_u.at[some]) if first else (z.at[some, 0, data], halo_u.at[par, some])
             rcopy(src, dst, row_send.at[par, 0], row_recv.at[par, 0, t], sp2, sp).wait_recv()
 
         @pl.when(has_d)
         def _():
-            src, dst = (edge_d.at[some], first_d.at[some]) if first else (z.at[some, n_rows - 1], halo_d.at[par, some])
+            src, dst = (edge_d.at[some], first_d.at[some]) if first else (z.at[some, n_rows - 1, data], halo_d.at[par, some])
             rcopy(src, dst, row_send.at[par, 1], row_recv.at[par, 1, t], sp2, sp).wait_recv()
 
         @pl.when(has_l)
@@ -116,12 +118,12 @@
 
         @pl.when(has_u)
         def _():
-            src, dst = (edge_u, first_u) if first else (z.at[every, 0], halo_u.at[0])
+            src, dst = (edge_u, first_u) if first else (z.at[every, 0, data], halo_u.at[0])
             rcopy(src, dst, row_send.at[par, 0], row_recv.at[0, 0, 0], sp2, sp).wait_send()
 
         @pl.when(has_d)
         def _():
-            src, dst = (edge_d, first_d) if first else (z.at[every, n_rows - 1], halo_d.at[0])
+            src, dst = (edge_d, first_d) if first else (z.at[every, n_rows - 1, data], halo_d.at[0])
             rcopy(src, dst, row_send.at[par, 1], row_recv.at[0, 1, 0], sp2, sp).wait_send()
 
         @pl.when(has_l)
@@ -150,13 +152,15 @@
     def wait_stats(par):
         for d in range(1, n_dev):
             stat_copy(d, par).wait_send()
+        for d in range(1, n_dev):
             src = lax.rem(me + d, n_dev)
             rcopy(stats.at[par, src], stats.at[par, src], st_send.at[d - 1], st_recv.at[par, src], sp2, sp).wait_recv()
 
     def set_constants(par, gain, shift, count, paired):
-        total = stats[par, 0]
-        for src in range(1, n_dev):
-            total = total + stats[par, src]
+        parts = [stats[par, src] for src in range(n_dev)]
+        while len(parts) > 1:
+            parts = [a + b for a, b in zip(parts[0::2], parts[1::2])]
+        total = parts[0]
         if paired:
             total = total + pltpu.roll(total, ch, 1)
         mean = total[0:1] * (1.0 / count)
@@ -169,9 +173,9 @@
 
     def save_edges(t, u, n_rows, par):
         img = t * UNROLL + u
-        flat = z.at[img].reshape(rows * pairs, 128)
-        first = flat[pl.ds(0, n_rows, stride=pairs), :]
-        final = flat[pl.ds(pairs - 1, n_rows, stride=pairs), :]
+        flat = z.at[img].reshape(rows * wide, 128)
+        first = flat[pl.ds(0, n_rows, stride=wide), :]
+        final = flat[pl.ds(pairs - 1, n_rows, stride=wide), :]
         edge_l[par, img, 0:n_rows, :] = first
         edge_r[par, img, 0:n_rows, :] = final
         corner_s[par, 0, t, u:u + 1, :] = first[0:1]
@@ -204,7 +208,7 @@
             elif p == n_rows + 1:
                 v = jnp.where(has_d, first_d[img].astype(F32) if raw else act(halo_d[par, img], raw), 0.0)
             else:
-                v = act(z[img, p - 1], raw)
+                v = act(z[img, p - 1, 0:pairs], raw)
             base = p * wide + EDGE
             buf[base:base + pairs, :] = v
             out.append((p, base, v))
@@ -232,8 +236,8 @@
         acc[0] += jnp.concatenate([s[:, :128], q[:, :128]], axis=1)
         acc[1] += jnp.concatenate([s[:, 128:], q[:, 128:]], axis=1)
         for i in range(o.shape[0] // pairs):
-            dst[img, 2 * (i0 + i)] = o[i * pairs:(i + 1) * pairs, :128]
-            dst[img, 2 * (i0 + i) + 1] = o[i * pairs:(i + 1) * pairs, 128:]
+            dst[img, 2 * (i0 + i), 0:pairs] = o[i * pairs:(i + 1) * pairs, :128]
+            dst[img, 2 * (i0 + i) + 1, 0:pairs] = o[i * pairs:(i + 1) * pairs, 128:]
 
     def dot(parts):
         lhs = jnp.concatenate(parts, axis=1)
@@ -265,19 +269,29 @@
 
     n_steps = n_img // UNROLL
 
-    def run_layer(par, raw, n_rows, build, conv, n_out, par_out, n_join, batches=1):
+    def run_layer(par, raw, n_rows, build, conv, n_out, par_out, constants, joins, batches=1):
         acc[...] = jnp.zeros_like(acc)
+        for t in range(batches):
+            wait_edges(t, par, n_rows, raw)
+        constants()
 
         def body(step, carry):
             steps = [step * batches + b for b in range(batches)]
+
+            @pl.when(step > 0)
+            def _():
+                for t in steps:
+                    wait_edges(t, par, n_rows, raw)
+
             for b, t in enumerate(steps):
-                wait_edges(t, par, n_rows, raw)
                 prepare_corners(b, t, par, raw)
-            for b, t in enumerate(steps):
-                for u in range(0, UNROLL, n_join):
-                    for a in range(n_join):
-                        build(t, u + a, b * UNROLL + u + a)
-                    conv(t, u, b * UNROLL + u, par_out, n_join)
+            k = 0
+            for n in joins:
+                t, u = steps[k // UNROLL], k % UNROLL
+                for a in range(n):
+                    build(t, u + a, k + a)
+                conv(t, u, k, par_out, n)
+                k += n
             if n_out:
                 @pl.when(step < n_steps // batches - 1)
                 def _():
@@ -336,8 +350,8 @@
                     r = 4 * g + 2 * b
                     upper = jnp.where(lane < ch, even, pltpu.roll(odd, ch, 1))
                     lower = jnp.where(lane < ch, pltpu.roll(even, ch, 1), odd)
-                    z[img, r] = upper
-                    z[img, r + 1] = lower
+                    z[img, r, 0:pairs] = upper
+                    z[img, r + 1, 0:pairs] = lower
                     if r == 0:
                         edge_u[img] = upper.astype(BF16)
                     if r + 2 == rows:
@@ -359,7 +373,7 @@
     for copy in w_copies:
         copy.wait()
     weights_pairs(0)
-    run_layer(0, True, rows, lambda t, u, k: build_pairs(t, 0, u, k, True), conv_pairs, rows, 1, JOIN)
+    run_layer(0, True, rows, lambda t, u, k: build_pairs(t, 0, u, k, True), conv_pairs, rows, 1, lambda: None, JOINS)
     wait_edges_sent(0, rows, True)
 
     def gains(layer):
@@ -372,10 +386,13 @@
         par = lax.rem(layer, 2)
         weights_pairs(layer)
         wait_edges_sent(par, rows)
-        wait_stats(par)
-        g, s = gains(layer - 1)
-        set_constants(par, g, s, count_a, True)
-        run_layer(par, False, rows, lambda t, u, k: build_pairs(t, par, u, k, False), conv_pairs, rows, 1 - par, JOIN, BATCHES)
+
+        def constants():
+            wait_stats(par)
+            g, s = gains(layer - 1)
+            set_constants(par, g, s, count_a, True)
+
+        run_layer(par, False, rows, lambda t, u, k: build_pairs(t, par, u, k, False), conv_pairs, rows, 1 - par, constants, LONG_JOINS, BATCHES)
         return carry
 
     lax.fori_loop(1, n_layers, a_layer, 0)
@@ -383,16 +400,22 @@
     par = n_layers % 2
     weights_down()
     wait_edges_sent(par, rows)
-    wait_stats(par)
-    g, s = gains(n_layers - 1)
-    set_constants(par, g, s, count_a, True)
-    run_layer(par, False, rows, lambda t, u, k: build_pairs(t, par, u, k, False, 1), conv_down, half, 1 - par, JOIN)
+
+    def constants():
+        wait_stats(par)
+        g, s = gains(n_layers - 1)
+        set_constants(par, g, s, count_a, True)
+
+    run_layer(par, False, rows, lambda t, u, k: build_pairs(t, par, u, k, False, 1), conv_down, half, 1 - par, constants, JOINS)
 
     weights_wide()
     wait_edges_sent(1 - par, half)
-    wait_stats(1 - par)
-    set_constants(1 - par, bn_down[0:1, :], bn_down[1:2, :], count_b, False)
-    run_layer(1 - par, False, half, lambda t, u, k: build_wide(t, 1 - par, u, k), conv_wide, 0, par, JOIN)
+
+    def constants():
+        wait_stats(1 - par)
+        set_constants(1 - par, bn_down[0:1, :], bn_down[1:2, :], count_b, False)
+
+    run_layer(1 - par, False, half, lambda t, u, k: build_wide(t, 1 - par, u, k), conv_wide, 0, par, constants, JOINS)
     wait_stats(par)
     set_constants(par, bn_b[0, 0:1, :], bn_b[0, 1:2, :], count_b, False)
     cst_out[...] = cst[...]
@@ -428,9 +451,9 @@
         scratch = [
             vmem((n_img, rows, ch, cols), BF16),
             vmem(w_a.shape, BF16), vmem(w_down.shape, BF16), vmem(w_b.shape, BF16),
-            vmem((n_img, rows, pairs, 128), F32),
+            vmem((n_img, rows, pairs + EDGE, 128), F32),
             [vmem((4 * (half + 1), pairs, 128), BF16) for _ in range(BATCHES * UNROLL)],
-            [vmem(((rows + 2) * (pairs + 2 * EDGE), 128), F32) for _ in range(BATCHES * UNROLL)],
+            [vmem(((rows + 2) * (pairs + EDGE) + EDGE, 128), F32) for _ in range(BATCHES * UNROLL)],
             vmem((2, 1536, 128), BF16),
             vmem((128, 128), BF16),
             vmem((n_img, pairs, 128), BF16), vmem((n_img, pairs, 128), BF16),

time: 72.6 us -> 71.9 us (level)
  no operation moved by 1% of the time
where the time goes in v9:
time: 71.9 us; the launch traced here: 71.8 us
  Pallas kernels  71.8 us (100%)
    pallas_call x1, Pallas kernels, per_device(): pl.pallas_call(functools.partial(stack_kernel, dims), out_shape=(vmem((n_...  70.3 us
    pallas_call x1, Pallas kernels, per_device(): pl.pallas_call(finish_kernel, out_shape=jax.ShapeDtypeStruct((n_img, half...  1.5 us

profile of v9, /device:TPU:0, one launch (start us, length us, event | category | flops | bytes accessed | tf_op | source)
XLA Modules:
  0.0 71.8 jit_solution(10993963050838263602)
XLA Ops:
  0.0 70.3 %shard_map.73 = (f32[16,8,64,128]{3,2,1,0:T(8,128)S(1)}, f32[8,128]{1,0:T(8,128)S(1)}) custom-call(bf16[16,16,64,128]{3,2,1,0:T(8,128)(2,1)} %bitcast.1, bf16[4,3,3,64,64]{4,3,2,1,0:T(8,128)(2,1)} %w_a_ref.1, f32[4,2,64]{2,1,0:T(2,128)} %bn_a.1, bf16[3,3,64,128]{3,2,1,0:T(8,128)(2,1)} %w_down_ref.1, f32[2,128]{1,0:T(2,128)} %bn_down.1, ...), custom_call_target="tpu_custom_call" | custom-call | tf_op jit(solution)/shard_map/pallas_call | solution.py:483
  70.3 1.5 %shard_map.74 = bf16[16,8,64,128]{3,2,1,0:T(8,128)(2,1)} custom-call(f32[16,8,64,128]{3,2,1,0:T(8,128)S(1)} %get-tuple-element.7.z, f32[8,128]{1,0:T(8,128)S(1)} %get-tuple-element.8.cst_ref), custom_call_target="tpu_custom_call" | custom-call | tf_op jit(solution)/shard_map/pallas_call | solution.py:491

commit v10 on v9

--- a/solution.py
+++ b/solution.py
@@ -406,7 +406,7 @@
         g, s = gains(n_layers - 1)
         set_constants(par, g, s, count_a, True)
 
-    run_layer(par, False, rows, lambda t, u, k: build_pairs(t, par, u, k, False, 1), conv_down, half, 1 - par, constants, JOINS)
+    run_layer(par, False, rows, lambda t, u, k: build_pairs(t, par, u, k, False, 1), conv_down, half, 1 - par, constants, JOINS * 2, BATCHES)
 
     weights_wide()
     wait_edges_sent(1 - par, half)
@@ -415,7 +415,7 @@
         wait_stats(1 - par)
         set_constants(1 - par, bn_down[0:1, :], bn_down[1:2, :], count_b, False)
 
-    run_layer(1 - par, False, half, lambda t, u, k: build_wide(t, 1 - par, u, k), conv_wide, 0, par, constants, JOINS)
+    run_layer(1 - par, False, half, lambda t, u, k: build_wide(t, 1 - par, u, k), conv_wide, 0, par, constants, JOINS * 2, BATCHES)
     wait_stats(par)
     set_constants(par, bn_b[0, 0:1, :], bn_b[0, 1:2, :], count_b, False)
     cst_out[...] = cst[...]

time: 71.9 us -> 72.3 us (level)
  no operation moved by 1% of the time
where the time goes in v10:
time: 72.3 us; the launch traced here: 72.1 us
  Pallas kernels  72.1 us (100%)
    pallas_call x1, Pallas kernels, per_device(): pl.pallas_call(functools.partial(stack_kernel, dims), out_shape=(vmem((n_...  70.6 us
    pallas_call x1, Pallas kernels, per_device(): pl.pallas_call(finish_kernel, out_shape=jax.ShapeDtypeStruct((n_img, half...  1.5 us

profile of v10, /device:TPU:0, one launch (start us, length us, event | category | flops | bytes accessed | tf_op | source)
XLA Modules:
  0.0 72.1 jit_solution(2077912754429228268)
XLA Ops:
  0.0 70.6 %shard_map.73 = (f32[16,8,64,128]{3,2,1,0:T(8,128)S(1)}, f32[8,128]{1,0:T(8,128)S(1)}) custom-call(bf16[16,16,64,128]{3,2,1,0:T(8,128)(2,1)} %bitcast.1, bf16[4,3,3,64,64]{4,3,2,1,0:T(8,128)(2,1)} %w_a_ref.1, f32[4,2,64]{2,1,0:T(2,128)} %bn_a.1, bf16[3,3,64,128]{3,2,1,0:T(8,128)(2,1)} %w_down_ref.1, f32[2,128]{1,0:T(2,128)} %bn_down.1, ...), custom_call_target="tpu_custom_call" | custom-call | tf_op jit(solution)/shard_map/pallas_call | solution.py:483
  70.6 1.5 %shard_map.74 = bf16[16,8,64,128]{3,2,1,0:T(8,128)(2,1)} custom-call(f32[16,8,64,128]{3,2,1,0:T(8,128)S(1)} %get-tuple-element.7.z, f32[8,128]{1,0:T(8,128)S(1)} %get-tuple-element.8.cst_ref), custom_call_target="tpu_custom_call" | custom-call | tf_op jit(solution)/shard_map/pallas_call | solution.py:491

commit v11 on v10

--- a/solution.py
+++ b/solution.py
@@ -373,7 +373,7 @@
     for copy in w_copies:
         copy.wait()
     weights_pairs(0)
-    run_layer(0, True, rows, lambda t, u, k: build_pairs(t, 0, u, k, True), conv_pairs, rows, 1, lambda: None, JOINS)
+    run_layer(0, True, rows, lambda t, u, k: build_pairs(t, 0, u, k, True), conv_pairs, rows, 1, lambda: None, LONG_JOINS, BATCHES)
     wait_edges_sent(0, rows, True)
 
     def gains(layer):
@@ -406,7 +406,7 @@
         g, s = gains(n_layers - 1)
         set_constants(par, g, s, count_a, True)
 
-    run_layer(par, False, rows, lambda t, u, k: build_pairs(t, par, u, k, False, 1), conv_down, half, 1 - par, constants, JOINS * 2, BATCHES)
+    run_layer(par, False, rows, lambda t, u, k: build_pairs(t, par, u, k, False, 1), conv_down, half, 1 - par, constants, JOINS)
 
     weights_wide()
     wait_edges_sent(1 - par, half)

time: 72.3 us -> 72.2 us (level)
  no operation moved by 1% of the time
where the time goes in v11:
time: 72.2 us; the launch traced here: 72 us
  Pallas kernels  72 us (100%)
    pallas_call x1, Pallas kernels, per_device(): pl.pallas_call(functools.partial(stack_kernel, dims), out_shape=(vmem((n_...  70.5 us
    pallas_call x1, Pallas kernels, per_device(): pl.pallas_call(finish_kernel, out_shape=jax.ShapeDtypeStruct((n_img, half...  1.5 us

profile of v11, /device:TPU:0, one launch (start us, length us, event | category | flops | bytes accessed | tf_op | source)
XLA Modules:
  0.0 72.0 jit_solution(3775364550033577637)
XLA Ops:
  0.0 70.5 %shard_map.73 = (f32[16,8,64,128]{3,2,1,0:T(8,128)S(1)}, f32[8,128]{1,0:T(8,128)S(1)}) custom-call(bf16[16,16,64,128]{3,2,1,0:T(8,128)(2,1)} %bitcast.1, bf16[4,3,3,64,64]{4,3,2,1,0:T(8,128)(2,1)} %w_a_ref.1, f32[4,2,64]{2,1,0:T(2,128)} %bn_a.1, bf16[3,3,64,128]{3,2,1,0:T(8,128)(2,1)} %w_down_ref.1, f32[2,128]{1,0:T(2,128)} %bn_down.1, ...), custom_call_target="tpu_custom_call" | custom-call | tf_op jit(solution)/shard_map/pallas_call | solution.py:483
  70.5 1.5 %shard_map.74 = bf16[16,8,64,128]{3,2,1,0:T(8,128)(2,1)} custom-call(f32[16,8,64,128]{3,2,1,0:T(8,128)S(1)} %get-tuple-element.7.z, f32[8,128]{1,0:T(8,128)S(1)} %get-tuple-element.8.cst_ref), custom_call_target="tpu_custom_call" | custom-call | tf_op jit(solution)/shard_map/pallas_call | solution.py:491
